TPU v7x, 128 devices: a whole 4x4x4 slice. The times are simulated.
128 devices in a mesh: graph: 32 (over z, x, core), batch: 4 (over y).
Axes of the slice: x: 4, y: 4, z: 4, core: 2. Of those that a mesh axis runs over, the one named last changes fastest.
Arguments:
- node_latent: bfloat16 [4, 4096, 512], P('batch', 'graph'), may hold values from -6 to 6
- edge_latent: bfloat16 [4, 32768, 512], P('batch', 'graph'), may hold values from -6 to 6
- node_cotangent: bfloat16 [4, 4096, 512], P('batch', 'graph'), may hold values from -6 to 6
- edge_w_in: bfloat16 [2, 1536, 512], replicated, may hold values from -0.15625 to 0.15625
- edge_w_out: bfloat16 [2, 512, 512], replicated, may hold values from -0.25 to 0.25
- node_w_in: bfloat16 [2, 1024, 512], replicated, may hold values from -0.1875 to 0.1875
- node_w_out: bfloat16 [2, 512, 512], replicated, may hold values from -0.25 to 0.25
- edge_gain: float32 [2, 512], replicated, may hold values from 0.25 to 1.75
- node_gain: float32 [2, 512], replicated, may hold values from 0.25 to 1.75
- edge_slot: int32 [32768], P('graph'), may hold values from 0 to 1151, as said below
- edge_receiver: int32 [32768], P('graph'), may hold values from 0 to 127
- send_list: int32 [1024, 32], P('graph'), may hold values from 0 to 127, as said below
- edge_count: int32 [32], P('graph'), may hold values from 256 to 1024, as said below
Outputs:
- node_out: float32 [4, 4096, 512], P('batch', 'graph')
- node_grad: float32 [4, 4096, 512], P('batch', 'graph')
- grad_edge_in: float32 [2, 1536, 512], P(None, ('graph', 'batch'))
- grad_edge_out: float32 [2, 512, 512], P(None, ('graph', 'batch'))
- grad_node_in: float32 [2, 1024, 512], P(None, ('graph', 'batch'))
- grad_node_out: float32 [2, 512, 512], P(None, ('graph', 'batch'))
- grad_edge_gain: float32 [2, 512], P(None, ('graph', 'batch'))
- grad_node_gain: float32 [2, 512], P(None, ('graph', 'batch'))
Inputs may be any that keep to these rules, and one draw needn't show every extreme that they name: `edge_slot`: for edge j of partition p = j // 1024: a slot below 128 names a node of partition p; a slot s of 128 or more names row (s - 128) % 32 of the list that partition q = (s - 128) // 32 keeps for partition p, and q differs from p cyclically by 1 to 2 steps or by exactly 32 // 2 steps. `edge_receiver`: the receiving node is a node of the edge's own partition. `send_list`: row q * 32 + p holds 32 distinct node numbers within partition q, the nodes whose latents partition p may read. `edge_count`: edge slots at or above a partition's count carry no edge.
All inputs are finite; a program needn't handle non-finite values.
Results may differ from a plain program's by a relative error of at most 0.035.
Values may be sent and summed in bfloat16 or wider, within the bound.
No kernel may reach another device: no remote copies, remote signals or barrier semaphores. Data moves between devices by JAX's collectives and lax.ppermute only.
A program may use at most 128 MiB of HBM per device.

v0:
```python
import functools

import jax
import jax.numpy as jnp
from jax import lax
from jax.experimental import pallas as pl
from jax.experimental.pallas import tpu as pltpu
from jax.sharding import PartitionSpec as P

HOPS = 2
EPSILON = 1e-05
CHUNK = 256
OFFSETS = (-2, -1, 1, 2, 16)
F32 = jnp.float32
BF16 = jnp.bfloat16


def nn(a, b):
    return lax.dot_general(a, b, (((1,), (0,)), ((), ())), preferred_element_type=F32)


def nt(a, b):
    return lax.dot_general(a, b, (((1,), (1,)), ((), ())), preferred_element_type=F32)


def tn(a, b):
    return lax.dot_general(a, b, (((0,), (0,)), ((), ())), preferred_element_type=F32)


def sigmoid(x):
    return 0.5 * jnp.tanh(0.5 * x) + 0.5


def layer_norm(z):
    centre = z - jnp.mean(z, axis=-1, keepdims=True)
    inv = lax.rsqrt(jnp.mean(centre * centre, axis=-1, keepdims=True) + EPSILON)
    return centre * inv, inv


def layer_norm_back(grad, gain, normed, inv):
    gn = grad * gain
    m1 = jnp.mean(gn, axis=-1, keepdims=True)
    m2 = jnp.mean(gn * normed, axis=-1, keepdims=True)
    return inv * (gn - m1 - normed * m2)


def swish_back(pre):
    s = sigmoid(pre)
    return s * (1.0 + pre * (1.0 - s))


def list_onehot(lists_ref, own, offset, nodes):
    row = lists_ref[pl.ds((own - offset) & 31, 1), :]
    ids = lax.broadcasted_iota(jnp.int32, (nodes, row.shape[1]), 0)
    return jnp.where(ids == row, 1.0, 0.0).astype(BF16)


def send_blocks(lists_ref, own, vb, outs):
    for offset, out in zip(OFFSETS, outs):
        onehot = list_onehot(lists_ref, own, offset, vb.shape[0])
        out[...] = tn(onehot, vb).astype(BF16)


def returned(lists_ref, own, blocks):
    total = None
    for offset, block in zip(OFFSETS, blocks):
        term = nn(list_onehot(lists_ref, own, offset, 128), block[...])
        total = term if total is None else total + term
    return total


def build_onehot(onehot_ref, slot_ref, receiver_ref, own):
    edges = slot_ref.shape[1]
    slot = slot_ref[...]
    row = slot - 128
    distance = ((row >> 5) - own) & 31
    block = jnp.where(distance == 30, 0, jnp.where(distance == 31, 1, jnp.where(distance == 1, 2, jnp.where(distance == 2, 3, 4))))
    position = jnp.where(slot < 128, slot, 128 + block * 32 + (row & 31))
    ids = lax.broadcasted_iota(jnp.int32, (128, edges), 0)
    onehot_ref[0:128, :] = jnp.where(ids == receiver_ref[...], 1.0, 0.0).astype(BF16)
    ids = lax.broadcasted_iota(jnp.int32, (384, edges), 0)
    onehot_ref[128:512, :] = jnp.where(ids == position, 1.0, 0.0).astype(BF16)


def fill_senders(sender_ref, vb, blocks):
    sender_ref[0:128, :] = vb
    for n, block in enumerate(blocks):
        sender_ref[128 + 32 * n : 160 + 32 * n, :] = block[...]


def fill_projected(layer, proj_ref, vb, sender_ref, w_in_ref):
    proj_ref[0:128, :] = nn(vb, w_in_ref[layer, 1024:1536, :]).astype(BF16)
    proj_ref[128:416, :] = nn(sender_ref[...], w_in_ref[layer, 512:1024, :]).astype(BF16)
    proj_ref[416:512, :] = jnp.zeros((96, 512), BF16)


def live_rows(base, count):
    rows = base + lax.broadcasted_iota(jnp.int32, (CHUNK, 1), 0)
    return jnp.where(rows < count, 1.0, 0.0).astype(F32)


def node_forward(layer, vb, agg, w_in_ref, w_out_ref):
    pre = nn(vb, w_in_ref[layer, 0:512, :]) + nn(agg, w_in_ref[layer, 512:1024, :])
    hidden = (pre * sigmoid(pre)).astype(BF16)
    normed, inv = layer_norm(nn(hidden, w_out_ref[layer]))
    return pre, hidden, normed, inv


def split_store(k, scratch_ref, keep_ref, send_ref, at, rows):
    for c in range(16):
        mine = pl.multiple_of(2 * c * rows + k * rows, 16)
        other = pl.multiple_of(2 * c * rows + (1 - k) * rows, 16)
        keep_ref[c, at : at + rows, :] = scratch_ref[pl.ds(mine, rows), :]
        send_ref[c, at : at + rows, :] = scratch_ref[pl.ds(other, rows), :]


def store_gains(edge_gain, node_gain, keep_ref, send_ref):
    pad = jnp.concatenate([edge_gain, node_gain, jnp.zeros((14, 512), F32)], axis=0).astype(BF16)
    keep_ref[16, 0:16, :] = pad
    send_ref[16, 0:16, :] = pad


def node_backward(layer, grad, vb, agg, pre, hidden, normed, inv, w_in_ref, w_out_ref, gain, g_in_ref, g_out_ref):
    grad_gain = jnp.sum(grad * normed, axis=0, keepdims=True)
    dz = layer_norm_back(grad, gain, normed, inv).astype(BF16)
    g_out_ref[...] = tn(hidden, dz).astype(BF16)
    da = (nt(dz, w_out_ref[layer]) * swish_back(pre)).astype(BF16)
    g_in_ref[0:512, :] = tn(vb, da).astype(BF16)
    g_in_ref[512:1024, :] = tn(agg, da).astype(BF16)
    return grad_gain, nt(da, w_in_ref[layer, 0:512, :]), nt(da, w_in_ref[layer, 512:1024, :])


def gather_kernel(own_ref, lists_ref, vb_ref, *outs):
    send_blocks(lists_ref, own_ref[0], vb_ref[0], outs)


def forward_kernel(
    own_ref, count_ref, lists_ref, slot_ref, receiver_ref, vb_ref, eb_ref, b0, b1, b2, b3, b4,
    we_in, we_out, wn_in, wn_out, e_gain_ref, n_gain_ref,
    v_out, vb_out, eb_out, pre_out, normed_out, inv_out, n_pre_out, n_normed_out, n_inv_out, agg_out,
    o0, o1, o2, o3, o4,
    onehot, senders, proj, message,
):
    own, count = own_ref[0], count_ref[0]
    build_onehot(onehot, slot_ref, receiver_ref, own)
    vb = vb_ref[0]
    fill_senders(senders, vb, (b0, b1, b2, b3, b4))
    fill_projected(0, proj, vb, senders, we_in)
    gain = e_gain_ref[0:1, :]
    for n in range(eb_ref.shape[1] // CHUNK):
        rows = slice(n * CHUNK, (n + 1) * CHUNK)
        eb = eb_ref[0, rows, :]
        pre = nn(eb, we_in[0, 0:512, :]) + tn(onehot[:, rows], proj[...])
        hidden = (pre * sigmoid(pre)).astype(BF16)
        normed, inv = layer_norm(nn(hidden, we_out[0]))
        m = normed * gain * live_rows(n * CHUNK, count)
        pre_out[rows, :] = pre.astype(BF16)
        normed_out[rows, :] = normed.astype(BF16)
        inv_out[rows, :] = jnp.broadcast_to(inv, (CHUNK, 128))
        message[rows, :] = m.astype(BF16)
        eb_out[rows, :] = (eb.astype(F32) + m).astype(BF16)
    agg = nn(onehot[0:128, :], message[...]).astype(BF16)
    pre, _, normed, inv = node_forward(0, vb, agg, wn_in, wn_out)
    v = vb.astype(F32) + normed * n_gain_ref[0:1, :]
    v_out[...] = v
    vb1 = v.astype(BF16)
    vb_out[...] = vb1
    n_pre_out[...] = pre
    n_normed_out[...] = normed
    n_inv_out[...] = jnp.broadcast_to(inv, (128, 128))
    agg_out[...] = agg
    send_blocks(lists_ref, own, vb1, (o0, o1, o2, o3, o4))


def edge_tail(layer, onehot, senders, vb, eb, h_ref, dz_ref, da_ref, we_in, g_in, g_out, outs):
    g_out[...] = tn(h_ref[...], dz_ref[...]).astype(BF16)
    g_in[0:512, :] = tn(eb, da_ref[...]).astype(BF16)
    gathered = nn(onehot[0:416, :], da_ref[...]).astype(BF16)
    at_receiver = gathered[0:128, :]
    at_sender = gathered[128:416, :]
    g_in[512:1024, :] = tn(senders[...], at_sender).astype(BF16)
    g_in[1024:1536, :] = tn(vb, at_receiver).astype(BF16)
    back = nt(at_sender, we_in[layer, 512:1024, :])
    for n, out in enumerate(outs):
        out[...] = back[128 + 32 * n : 160 + 32 * n, :].astype(BF16)
    return nt(at_receiver, we_in[layer, 1024:1536, :]) + back[0:128, :]


def write_grads(k, g_in, g_out, gn_in, gn_out, edge_gain, node_gain, keep, send):
    split_store(k, g_in, keep, send, 0, 48)
    split_store(k, g_out, keep, send, 48, 16)
    split_store(k, gn_in, keep, send, 64, 32)
    split_store(k, gn_out, keep, send, 96, 16)
    store_gains(edge_gain, node_gain, keep, send)


def middle_kernel(
    own_ref, count_ref, slot_ref, receiver_ref, v_ref, vb_ref, eb_ref, cot_ref, b0, b1, b2, b3, b4,
    we_in, we_out, wn_in, wn_out, e_gain_ref, n_gain_ref,
    node_out, grad_out, edge_grad_out, keep, send, o0, o1, o2, o3, o4,
    onehot, senders, proj, message, pre_s, normed_s, inv_s, hidden_s, dz_s, da_s, g_in, g_out, gn_in, gn_out,
):
    own, count = own_ref[0], count_ref[0]
    build_onehot(onehot, slot_ref, receiver_ref, own)
    vb = vb_ref[...]
    fill_senders(senders, vb, (b0, b1, b2, b3, b4))
    fill_projected(1, proj, vb, senders, we_in)
    gain = e_gain_ref[1:2, :]
    chunks = eb_ref.shape[0] // CHUNK
    for n in range(chunks):
        rows = slice(n * CHUNK, (n + 1) * CHUNK)
        pre = nn(eb_ref[rows, :], we_in[1, 0:512, :]) + tn(onehot[:, rows], proj[...])
        hidden = (pre * sigmoid(pre)).astype(BF16)
        normed, inv = layer_norm(nn(hidden, we_out[1]))
        m = normed * gain * live_rows(n * CHUNK, count)
        pre_s[rows, :] = pre
        normed_s[rows, :] = normed
        inv_s[rows, :] = jnp.broadcast_to(inv, (CHUNK, 128))
        hidden_s[rows, :] = hidden
        message[rows, :] = m.astype(BF16)
    agg = nn(onehot[0:128, :], message[...]).astype(BF16)
    n_pre, n_hidden, n_normed, n_inv = node_forward(1, vb, agg, wn_in, wn_out)
    n_gain = n_gain_ref[1:2, :]
    node_out[0] = v_ref[...] + n_normed * n_gain
    grad = cot_ref[0].astype(F32)
    grad_n_gain, grad_v, grad_agg = node_backward(
        1, grad, vb, agg, n_pre, n_hidden, n_normed, n_inv, wn_in, wn_out, n_gain, gn_in, gn_out
    )
    grad_agg = grad_agg.astype(BF16)
    grad_e_gain = jnp.zeros((1, 512), F32)
    for n in range(chunks):
        rows = slice(n * CHUNK, (n + 1) * CHUNK)
        gm = tn(onehot[0:128, rows], grad_agg) * live_rows(n * CHUNK, count)
        normed = normed_s[rows, :]
        grad_e_gain += jnp.sum(gm * normed, axis=0, keepdims=True)
        dz = layer_norm_back(gm, gain, normed, inv_s[rows, 0:1]).astype(BF16)
        dz_s[rows, :] = dz
        da = (nt(dz, we_out[1]) * swish_back(pre_s[rows, :])).astype(BF16)
        da_s[rows, :] = da
        edge_grad_out[rows, :] = nt(da, we_in[1, 0:512, :]).astype(BF16)
    grad_ends = edge_tail(1, onehot, senders, vb, eb_ref[...], hidden_s, dz_s, da_s, we_in, g_in, g_out, (o0, o1, o2, o3, o4))
    grad_out[...] = grad + grad_v + grad_ends
    write_grads(own & 1, g_in, g_out, gn_in, gn_out, grad_e_gain, grad_n_gain, keep, send)


def backward_kernel(
    own_ref, count_ref, lists_ref, slot_ref, receiver_ref, vb_ref, eb_ref, s0, s1, s2, s3, s4,
    grad_ref, r0, r1, r2, r3, r4, edge_grad_ref, pre_ref, normed_ref, inv_ref, n_pre_ref, n_normed_ref, n_inv_ref, agg_ref,
    we_in, we_out, wn_in, wn_out, e_gain_ref, n_gain_ref,
    grad_out, keep, send, o0, o1, o2, o3, o4,
    onehot, senders, hidden_s, dz_s, da_s, g_in, g_out, gn_in, gn_out,
):
    own, count = own_ref[0], count_ref[0]
    build_onehot(onehot, slot_ref, receiver_ref, own)
    vb = vb_ref[0]
    fill_senders(senders, vb, (s0, s1, s2, s3, s4))
    grad = grad_ref[...] + returned(lists_ref, own, (r0, r1, r2, r3, r4))
    n_pre = n_pre_ref[...]
    n_hidden = (n_pre * sigmoid(n_pre)).astype(BF16)
    grad_n_gain, grad_v, grad_agg = node_backward(
        0, grad, vb, agg_ref[...], n_pre, n_hidden, n_normed_ref[...], n_inv_ref[:, 0:1], wn_in, wn_out, n_gain_ref[0:1, :], gn_in, gn_out
    )
    grad_agg = grad_agg.astype(BF16)
    gain = e_gain_ref[0:1, :]
    grad_e_gain = jnp.zeros((1, 512), F32)
    for n in range(eb_ref.shape[1] // CHUNK):
        rows = slice(n * CHUNK, (n + 1) * CHUNK)
        gm = tn(onehot[0:128, rows], grad_agg) + edge_grad_ref[rows, :].astype(F32)
        gm = gm * live_rows(n * CHUNK, count)
        normed = normed_ref[rows, :].astype(F32)
        grad_e_gain += jnp.sum(gm * normed, axis=0, keepdims=True)
        dz = layer_norm_back(gm, gain, normed, inv_ref[rows, 0:1]).astype(BF16)
        dz_s[rows, :] = dz
        pre = pre_ref[rows, :].astype(F32)
        s = sigmoid(pre)
        hidden_s[rows, :] = (pre * s).astype(BF16)
        da_s[rows, :] = (nt(dz, we_out[0]) * (s * (1.0 + pre * (1.0 - s)))).astype(BF16)
    grad_ends = edge_tail(0, onehot, senders, vb, eb_ref[0], hidden_s, dz_s, da_s, we_in, g_in, g_out, (o0, o1, o2, o3, o4))
    grad_out[...] = grad + grad_v + grad_ends
    write_grads(own & 1, g_in, g_out, gn_in, gn_out, grad_e_gain, grad_n_gain, keep, send)


def pack_kernel(keep_ref, recv_ref, out_ref, stage):
    gains = (keep_ref[16, 0:16, :].astype(F32) + recv_ref[16, 0:16, :].astype(F32))[0:8, :]

    def step(c, carry):
        rows = keep_ref[c].astype(F32) + recv_ref[c].astype(F32)
        for b in range(4):
            stage[b, 0:12, :] = rows[12 * b : 12 * b + 12, :]
            stage[b, 12:16, :] = rows[48 + 4 * b : 52 + 4 * b, :]
            stage[b, 16:24, :] = rows[64 + 8 * b : 72 + 8 * b, :]
            stage[b, 24:28, :] = rows[96 + 4 * b : 100 + 4 * b, :]
            stage[b, 28:32, :] = gains[0:4, :]
            out_ref[4 * c + b] = stage[b].astype(BF16)
        return carry

    lax.fori_loop(0, 16, step, 0)


def finish_kernel(
    device_ref, own_ref, lists_ref, grad_ref, r0, r1, r2, r3, r4, x0_ref, x1_ref,
    node_grad, g_e_in, g_e_out, g_n_in, g_n_out, g_e_gain, g_n_gain,
    stage,
):
    node_grad[0] = grad_ref[...] + returned(lists_ref, own_ref[0], (r0, r1, r2, r3, r4))
    picks = lax.broadcasted_iota(jnp.int32, (512, 128), 0) - 4 * device_ref[0]
    select = jnp.where(picks == lax.broadcasted_iota(jnp.int32, (512, 128), 1), 1.0, 0.0).astype(F32)
    for layer, x_ref in enumerate((x0_ref, x1_ref)):

        def step(n, total, x_ref=x_ref):
            return total + x_ref[n].astype(F32)

        stage[...] = lax.fori_loop(0, 64, step, jnp.zeros((32, 512), F32), unroll=8)
        g_e_in[layer] = stage[0:12, :]
        g_e_out[layer] = stage[12:16, :]
        g_n_in[layer] = stage[16:24, :]
        g_n_out[layer] = stage[24:28, :]
        gains = lax.dot_general(
            stage[24:32, :], select, (((1,), (0,)), ((), ())), precision=lax.Precision.HIGHEST, preferred_element_type=F32
        )
        g_e_gain[layer : layer + 1, :] = gains[4:5, 0:4]
        g_n_gain[layer : layer + 1, :] = gains[5:6, 0:4]


def body(
    node_latent,
    edge_latent,
    node_cotangent,
    edge_w_in,
    edge_w_out,
    node_w_in,
    node_w_out,
    edge_gain,
    node_gain,
    edge_slot,
    edge_receiver,
    send_list,
    edge_count,
):
    width = node_latent.shape[2]
    nodes = node_latent.shape[1]
    edges = edge_slot.shape[0]
    graph = lax.axis_size("graph")
    own = lax.axis_index("graph").astype(jnp.int32)
    own_arr = own.reshape(1)
    device = (own * lax.axis_size("batch") + lax.axis_index("batch").astype(jnp.int32)).reshape(1)
    slot = edge_slot.reshape(1, edges)
    receiver = edge_receiver.reshape(1, edges)
    sds = jax.ShapeDtypeStruct
    vmem = pl.BlockSpec(memory_space=pltpu.VMEM)
    smem = pl.BlockSpec(memory_space=pltpu.SMEM)
    block = sds((32, width), BF16)
    params = pltpu.CompilerParams(vmem_limit_bytes=40 * 1024 * 1024)

    weight_args = (edge_w_in, edge_w_out, node_w_in, node_w_out, edge_gain, node_gain)

    def shift(blocks, sign):
        outs = []
        for offset, value in zip(OFFSETS, blocks):
            outs.append(lax.ppermute(value, "graph", [((i + sign * offset) % graph, i) for i in range(graph)]))
        return outs

    def call(kernel, outs, scratch, specs, *args):
        return pl.pallas_call(
            kernel,
            out_shape=outs,
            in_specs=specs,
            out_specs=jax.tree.map(lambda _: vmem, outs),
            scratch_shapes=scratch,
            compiler_params=params,
        )(*args)

    onehot_s = pltpu.VMEM((512, edges), BF16)
    sender_s = pltpu.VMEM((288, width), BF16)
    proj_s = pltpu.VMEM((512, width), BF16)
    edge_b = pltpu.VMEM((edges, width), BF16)
    edge_f = pltpu.VMEM((edges, width), F32)
    grads_s = [pltpu.VMEM((r, width), BF16) for r in (1536, 512, 1024, 512)]
    half = sds((17, 112, width), BF16)
    nodes_f = sds((nodes, width), F32)
    nodes_b = sds((nodes, width), BF16)
    edges_b = sds((edges, width), BF16)
    col = sds((edges, 128), F32)

    first = call(gather_kernel, [block] * 5, [], [smem, vmem, vmem], own_arr, send_list, node_latent)
    senders0 = shift(first, 1)
    v1, vb1, eb1, pre0, normed0, inv0, n_pre0, n_normed0, n_inv0, agg0, *second = call(
        forward_kernel,
        [nodes_f, nodes_b, edges_b, edges_b, edges_b, col, nodes_f, nodes_f, sds((nodes, 128), F32), nodes_b] + [block] * 5,
        [onehot_s, sender_s, proj_s, edge_b],
        [smem, smem] + [vmem] * 10 + [vmem] * 6,
        own_arr, edge_count, send_list, slot, receiver, node_latent, edge_latent, *senders0, *weight_args,
    )
    senders1 = shift(second, 1)
    node_out, grad1, edge_grad, keep1, send1, *back1 = call(
        middle_kernel,
        [sds((1, nodes, width), F32), nodes_f, edges_b, half, half] + [block] * 5,
        [onehot_s, sender_s, proj_s, edge_b, edge_f, edge_f, pltpu.VMEM((edges, 128), F32), edge_b, edge_b, edge_b] + grads_s,
        [smem, smem] + [vmem] * 11 + [vmem] * 6,
        own_arr, edge_count, slot, receiver, v1, vb1, eb1, node_cotangent, *senders1, *weight_args,
    )

    def scatter(keep, send):
        recv = lax.ppermute(send, "graph", [(i, i ^ 1) for i in range(graph)])
        packed = call(pack_kernel, sds((64, 32, width), BF16), [pltpu.VMEM((4, 32, width), F32)], [vmem, vmem], keep, recv)
        groups = [[(2 * c + k) * 4 + b for c in range(16) for b in range(4)] for k in range(2)]
        return lax.all_to_all(packed, ("graph", "batch"), 0, 0, tiled=True, axis_index_groups=groups)

    returned1 = shift(back1, -1)
    x1 = scatter(keep1, send1)
    grad0, keep0, send0, *back0 = call(
        backward_kernel,
        [nodes_f, half, half] + [block] * 5,
        [onehot_s, sender_s, edge_b, edge_b, edge_b] + grads_s,
        [smem, smem] + [vmem] * 24 + [vmem] * 6,
        own_arr, edge_count, send_list, slot, receiver, node_latent, edge_latent, *senders0,
        grad1, *returned1, edge_grad, pre0, normed0, inv0, n_pre0, n_normed0, n_inv0, agg0, *weight_args,
    )
    returned0 = shift(back0, -1)
    x0 = scatter(keep0, send0)
    grads = call(
        finish_kernel,
        [sds((1, nodes, width), F32)] + [sds((2, r, width), F32) for r in (12, 4, 8, 4)] + [sds((2, 4), F32)] * 2,
        [pltpu.VMEM((32, width), F32)],
        [smem, smem] + [vmem] * 9,
        device, own_arr, send_list, grad0, *returned0, x0, x1,
    )
    return (node_out, *grads)


def solution(mesh):
    in_specs = (
        P("batch", "graph", None),
        P("batch", "graph", None),
        P("batch", "graph", None),
        P(),
        P(),
        P(),
        P(),
        P(),
        P(),
        P("graph"),
        P("graph"),
        P("graph", None),
        P("graph"),
    )
    out_specs = (
        P("batch", "graph", None),
        P("batch", "graph", None),
        P(None, ("graph", "batch"), None),
        P(None, ("graph", "batch"), None),
        P(None, ("graph", "batch"), None),
        P(None, ("graph", "batch"), None),
        P(None, ("graph", "batch")),
        P(None, ("graph", "batch")),
    )
    return jax.shard_map(body, mesh=mesh, in_specs=in_specs, out_specs=out_specs, check_vma=False)
```

profile of v0, /device:TPU:0, one launch (start us, length us, event | category | flops | bytes accessed | tf_op | source)
XLA Modules:
  0.0 179.2 jit_solution(16199003448585221992)
XLA Ops:
  2.5 1.7 collective-permute-start
  4.2 5.1 %collective-permute-start.2 = (bf16[32,512]{1,0:T(8,128)(2,1)S(1)}, bf16[32,512]{1,0:T(8,128)(2,1)S(1)}, u32[]{:S(2)}, u32[]{:S(2)}) collective-permute-start(bf16[32,512]{1,0:T(8,128)(2,1)S(1)} %get-tuple-element.55), channel_id=1, source_target_pairs={{4,0},{8,4},{12,8},{16,12},{20,16},{24,20},{28,24},{32,28},{36,32}... | collective-permute-start | bytes 98312 | tf_op jit(solution)/shard_map/ppermute | solution.py:360
  9.3 1.5 collective-permute-start.3
  10.8 1.7 collective-permute-start.4
  13.2 3.0 %collective-permute-done.4.b4.s4 = bf16[32,512]{1,0:T(8,128)(2,1)S(1)} collective-permute-done((bf16[32,512]{1,0:T(8,128)(2,1)S(1)}, bf16[32,512]{1,0:T(8,128)(2,1)S(1)}, u32[]{:S(2)}, u32[]{:S(2)}) %collective-permute-start.4) | collective-permute-done | bytes 32800 | tf_op jit(solution)/shard_map/ppermute | solution.py:360
  16.2 1.9 %copy-done = bf16[2,1536,512]{2,1,0:T(8,128)(2,1)S(1)} copy-done((bf16[2,1536,512]{2,1,0:T(8,128)(2,1)S(1)}, bf16[2,1536,512]{2,1,0:T(8,128)(2,1)}, u32[]{:S(2)}) %copy-start) | copy-done | bytes 3145752
  18.1 1.6 copy-done.2
  19.7 1.2 copy-done.4
  20.9 1.2 copy-done.6
  22.1 1.2 copy-done.10
  27.7 4.0 %shard_map.189 = (f32[128,512]{1,0:T(8,128)S(1)}, bf16[128,512]{1,0:T(8,128)(2,1)S(1)}, bf16[1024,512]{1,0:T(8,128)(2,1)S(1)}, bf16[1024,512]{1,0:T(8,128)(2,1)S...) custom-call(s32[1]{0:T(128)} %bitcast.own_ref, ...), custom_call_target="tpu_custom_call" | custom-call | tf_op jit(solution)/shard_map/pallas_call | solution.py:364
  33.4 5.1 %collective-permute-start.7 = (bf16[32,512]{1,0:T(8,128)(2,1)S(1)}, bf16[32,512]{1,0:T(8,128)(2,1)S(1)}, u32[]{:S(2)}, u32[]{:S(2)}) collective-permute-start(bf16[32,512]{1,0:T(8,128)(2,1)S(1)} %get-tuple-element.63), channel_id=1, source_target_pairs={{4,0},{8,4},{12,8},{16,12},{20,16},{24,20},{28,24},{32,28},{36,32}... | collective-permute-start | bytes 98312 | tf_op jit(solution)/shard_map/ppermute | solution.py:360
  38.5 1.5 collective-permute-start.8
  40.5 1.9 %collective-permute-done.8.b3 = bf16[32,512]{1,0:T(8,128)(2,1)S(1)} collective-permute-done((bf16[32,512]{1,0:T(8,128)(2,1)S(1)}, bf16[32,512]{1,0:T(8,128)(2,1)S(1)}, u32[]{:S(2)}, u32[]{:S(2)}) %collective-permute-start.8) | collective-permute-done | bytes 32800 | tf_op jit(solution)/shard_map/ppermute | solution.py:360
  42.4 3.0 %collective-permute-done.9.b4 = bf16[32,512]{1,0:T(8,128)(2,1)S(1)} collective-permute-done((bf16[32,512]{1,0:T(8,128)(2,1)S(1)}, bf16[32,512]{1,0:T(8,128)(2,1)S(1)}, u32[]{:S(2)}, u32[]{:S(2)}) %collective-permute-start.9) | collective-permute-done | bytes 32800 | tf_op jit(solution)/shard_map/ppermute | solution.py:360
  45.4 11.4 %shard_map.190 = (f32[1,128,512]{2,1,0:T(8,128)}, f32[128,512]{1,0:T(8,128)S(1)}, bf16[1024,512]{1,0:T(8,128)(2,1)S(1)}, bf16[17,112,512]{2,1,0:T(8,128)(2,1)S(1...) custom-call(s32[1]{0:T(128)} %bitcast.own_ref, ...), custom_call_target="tpu_custom_call" | custom-call | tf_op jit(solution)/shard_map/pallas_call | solution.py:364
  61.7 3.9 %collective-permute-done.21.recv_ref = bf16[17,112,512]{2,1,0:T(8,128)(2,1)S(1)} collective-permute-done((bf16[17,112,512]{2,1,0:T(8,128)(2,1)S(1)}, bf16[17,112,512]{2,1,0:T(8,128)(2,1)S(1)}, u32[]{:S(2)}, u32[]{:S(2)}) %collective-permute-start.21) | collective-permute-done | bytes 1949728 | tf_op jit(solution)/shard_map/ppermute | solution.py:404
  66.5 1.3 copy-done.9
  67.9 7.3 %all-to-all-start.1 = ((bf16[64,32,512]{2,1,0:T(8,128)(2,1)}), bf16[64,32,512]{2,1,0:T(8,128)(2,1)}, u32[]{:S(2)}, u32[]{:S(2)}) async-start(bf16[64,32,512]{2,1,0:T(8,128)(2,1)} %copy-done.9), calls=%async_computation.1 | async-start | bytes 4194304 | tf_op jit(solution)/shard_map/all_to_all | solution.py:407
  75.2 5.2 %collective-permute-start.10 = (bf16[32,512]{1,0:T(8,128)(2,1)}, bf16[32,512]{1,0:T(8,128)(2,1)S(1)}, u32[]{:S(2)}, u32[]{:S(2)}) collective-permute-start(bf16[32,512]{1,0:T(8,128)(2,1)} %copy-done.69), channel_id=1, source_target_pairs={{8,0},{12,4},{16,8},{20,12},{24,16},{28,20},{32,24},{36,28},{40,32... | collective-permute-start | bytes 98312 | tf_op jit(solution)/shard_map/ppermute | solution.py:360
  81.9 18.0 %collective-permute-done.10.r0 = bf16[32,512]{1,0:T(8,128)(2,1)S(1)} collective-permute-done((bf16[32,512]{1,0:T(8,128)(2,1)}, bf16[32,512]{1,0:T(8,128)(2,1)S(1)}, u32[]{:S(2)}, u32[]{:S(2)}) %collective-permute-start.10) | collective-permute-done | bytes 32800 | tf_op jit(solution)/shard_map/ppermute | solution.py:360
  101.1 3.1 %collective-permute-done.13.r3 = bf16[32,512]{1,0:T(8,128)(2,1)S(1)} collective-permute-done((bf16[32,512]{1,0:T(8,128)(2,1)}, bf16[32,512]{1,0:T(8,128)(2,1)S(1)}, u32[]{:S(2)}, u32[]{:S(2)}) %collective-permute-start.13) | collective-permute-done | bytes 32800 | tf_op jit(solution)/shard_map/ppermute | solution.py:360
  105.4 1.2 copy-done.18
  106.6 1.2 copy-done.20
  119.1 9.1 %shard_map.191 = (f32[128,512]{1,0:T(8,128)S(1)}, bf16[17,112,512]{2,1,0:T(8,128)(2,1)S(1)}, bf16[17,112,512]{2,1,0:T(8,128)(2,1)S(1)}, bf16[32,512]{1,0:T(8,128...) custom-call(s32[1]{0:T(128)} %bitcast.own_ref, ...), custom_call_target="tpu_custom_call" | custom-call | tf_op jit(solution)/shard_map/pallas_call | solution.py:364
  132.0 3.9 %collective-permute-done.20.recv_ref = bf16[17,112,512]{2,1,0:T(8,128)(2,1)S(1)} collective-permute-done((bf16[17,112,512]{2,1,0:T(8,128)(2,1)S(1)}, bf16[17,112,512]{2,1,0:T(8,128)(2,1)S(1)}, u32[]{:S(2)}, u32[]{:S(2)}) %collective-permute-start.20) | collective-permute-done | bytes 1949728 | tf_op jit(solution)/shard_map/ppermute | solution.py:404
  135.9 2.2 %shard_map.192 = bf16[64,32,512]{2,1,0:T(8,128)(2,1)} custom-call(bf16[17,112,512]{2,1,0:T(8,128)(2,1)S(1)} %get-tuple-element.87.keep_ref, bf16[17,112,512]{2,1,0:T(8,128)(2,1)S(1)} %collective-permute-done.20.recv_ref), custom_call_target="tpu_custom_call" | custom-call | tf_op jit(solution)/shard_map/pallas_call | solution.py:364
  138.2 6.4 %all-to-all-start = ((bf16[64,32,512]{2,1,0:T(8,128)(2,1)}), bf16[64,32,512]{2,1,0:T(8,128)(2,1)S(1)}, u32[]{:S(2)}, u32[]{:S(2)}) async-start(bf16[64,32,512]{2,1,0:T(8,128)(2,1)} %shard_map.192), calls=%async_computation | async-start | bytes 4194304 | tf_op jit(solution)/shard_map/all_to_all | solution.py:407
  144.7 5.3 %collective-permute-start.15 = (bf16[32,512]{1,0:T(8,128)(2,1)S(1)}, bf16[32,512]{1,0:T(8,128)(2,1)S(1)}, u32[]{:S(2)}, u32[]{:S(2)}) collective-permute-start(bf16[32,512]{1,0:T(8,128)(2,1)S(1)} %copy-done.64), channel_id=1, source_target_pairs={{8,0},{12,4},{16,8},{20,12},{24,16},{28,20},{32,24},{36,28},{40,32... | collective-permute-start | bytes 98312 | tf_op jit(solution)/shard_map/ppermute | solution.py:360
  151.6 18.1 %collective-permute-done.15.r0 = bf16[32,512]{1,0:T(8,128)(2,1)S(1)} collective-permute-done((bf16[32,512]{1,0:T(8,128)(2,1)S(1)}, bf16[32,512]{1,0:T(8,128)(2,1)S(1)}, u32[]{:S(2)}, u32[]{:S(2)}) %collective-permute-start.15) | collective-permute-done | bytes 32800 | tf_op jit(solution)/shard_map/ppermute | solution.py:360
  170.8 3.1 %collective-permute-done.18.r3 = bf16[32,512]{1,0:T(8,128)(2,1)S(1)} collective-permute-done((bf16[32,512]{1,0:T(8,128)(2,1)S(1)}, bf16[32,512]{1,0:T(8,128)(2,1)S(1)}, u32[]{:S(2)}, u32[]{:S(2)}) %collective-permute-start.18) | collective-permute-done | bytes 32800 | tf_op jit(solution)/shard_map/ppermute | solution.py:360
  175.0 3.5 %shard_map.194 = (f32[1,128,512]{2,1,0:T(8,128)}, f32[2,12,512]{2,1,0:T(8,128)S(1)}, f32[2,4,512]{2,1,0:T(4,128)}, f32[2,8,512]{2,1,0:T(8,128)}, f32[2,4,512]{2,...) custom-call(s32[1]{0:T(128)} %bitcast.3.device_ref, s32[1]{0:T(128)} %bitcast.own_ref, s32[32,32]{1,0:T(8,128)S(1)} %copy-done.25, ...), custom_call_target="tpu_custom_call" | custom-call | tf_op jit(solution)/shard_map/pallas_call | solution.py:364
  (164 shorter events, 37.6 us)
Async XLA Ops:
  2.5 10.6 %collective-permute-start = (bf16[32,512]{1,0:T(8,128)(2,1)S(1)}, bf16[32,512]{1,0:T(8,128)(2,1)S(1)}, u32[]{:S(2)}, u32[]{:S(2)}) collective-permute-start(bf16[32,512]{1,0:T(8,128)(2,1)S(1)} %get-tuple-element.53), channel_id=1, source_target_pairs={{120,0},{124,4},{0,8},{4,12},{8,16},{12,20},{16,24},{20,28},{24,32... | collective-permute-start | bytes 98312 | tf_op jit(solution)/shard_map/ppermute | solution.py:360
  4.2 8.9 %collective-permute-start.1 = (bf16[32,512]{1,0:T(8,128)(2,1)S(1)}, bf16[32,512]{1,0:T(8,128)(2,1)S(1)}, u32[]{:S(2)}, u32[]{:S(2)}) collective-permute-start(bf16[32,512]{1,0:T(8,128)(2,1)S(1)} %get-tuple-element.54), channel_id=1, source_target_pairs={{124,0},{0,4},{4,8},{8,12},{12,16},{16,20},{20,24},{24,28},{28,32}... | collective-permute-start | bytes 98312 | tf_op jit(solution)/shard_map/ppermute | solution.py:360
  4.2 9.0 %collective-permute-start.2 = (bf16[32,512]{1,0:T(8,128)(2,1)S(1)}, bf16[32,512]{1,0:T(8,128)(2,1)S(1)}, u32[]{:S(2)}, u32[]{:S(2)}) collective-permute-start(bf16[32,512]{1,0:T(8,128)(2,1)S(1)} %get-tuple-element.55), channel_id=1, source_target_pairs={{4,0},{8,4},{12,8},{16,12},{20,16},{24,20},{28,24},{32,28},{36,32}... | collective-permute-start | bytes 98312 | tf_op jit(solution)/shard_map/ppermute | solution.py:360
  9.3 3.9 %collective-permute-start.3 = (bf16[32,512]{1,0:T(8,128)(2,1)S(1)}, bf16[32,512]{1,0:T(8,128)(2,1)S(1)}, u32[]{:S(2)}, u32[]{:S(2)}) collective-permute-start(bf16[32,512]{1,0:T(8,128)(2,1)S(1)} %get-tuple-element.56), channel_id=1, source_target_pairs={{8,0},{12,4},{16,8},{20,12},{24,16},{28,20},{32,24},{36,28},{40,32... | collective-permute-start | bytes 98312 | tf_op jit(solution)/shard_map/ppermute | solution.py:360
  10.8 5.4 %collective-permute-start.4 = (bf16[32,512]{1,0:T(8,128)(2,1)S(1)}, bf16[32,512]{1,0:T(8,128)(2,1)S(1)}, u32[]{:S(2)}, u32[]{:S(2)}) collective-permute-start(bf16[32,512]{1,0:T(8,128)(2,1)S(1)} %get-tuple-element.57), channel_id=1, source_target_pairs={{64,0},{68,4},{72,8},{76,12},{80,16},{84,20},{88,24},{92,28},{96,3... | collective-permute-start | bytes 98312 | tf_op jit(solution)/shard_map/ppermute | solution.py:360
  32.8 24.0 %copy-start.33 = (bf16[128,512]{1,0:T(8,128)(2,1)}, bf16[128,512]{1,0:T(8,128)(2,1)S(1)}, u32[]{:S(2)}) copy-start(bf16[128,512]{1,0:T(8,128)(2,1)S(1)} %get-tuple-element.80.agg_ref) | copy-start | bytes 393220
  32.8 24.0 %copy-start.45 = (f32[128,128]{1,0:T(8,128)}, f32[128,128]{1,0:T(8,128)S(1)}, u32[]{:S(2)}) copy-start(f32[128,128]{1,0:T(8,128)S(1)} %get-tuple-element.79.n_inv_ref) | copy-start | bytes 196612
  32.8 7.7 %collective-permute-start.5 = (bf16[32,512]{1,0:T(8,128)(2,1)S(1)}, bf16[32,512]{1,0:T(8,128)(2,1)S(1)}, u32[]{:S(2)}, u32[]{:S(2)}) collective-permute-start(bf16[32,512]{1,0:T(8,128)(2,1)S(1)} %get-tuple-element.61), channel_id=1, source_target_pairs={{120,0},{124,4},{0,8},{4,12},{8,16},{12,20},{16,24},{20,28},{24,32... | collective-permute-start | bytes 98312 | tf_op jit(solution)/shard_map/ppermute | solution.py:360
  33.4 7.1 %collective-permute-start.6 = (bf16[32,512]{1,0:T(8,128)(2,1)S(1)}, bf16[32,512]{1,0:T(8,128)(2,1)S(1)}, u32[]{:S(2)}, u32[]{:S(2)}) collective-permute-start(bf16[32,512]{1,0:T(8,128)(2,1)S(1)} %get-tuple-element.62), channel_id=1, source_target_pairs={{124,0},{0,4},{4,8},{8,12},{12,16},{16,20},{20,24},{24,28},{28,32}... | collective-permute-start | bytes 98312 | tf_op jit(solution)/shard_map/ppermute | solution.py:360
  33.4 7.1 %collective-permute-start.7 = (bf16[32,512]{1,0:T(8,128)(2,1)S(1)}, bf16[32,512]{1,0:T(8,128)(2,1)S(1)}, u32[]{:S(2)}, u32[]{:S(2)}) collective-permute-start(bf16[32,512]{1,0:T(8,128)(2,1)S(1)} %get-tuple-element.63), channel_id=1, source_target_pairs={{4,0},{8,4},{12,8},{16,12},{20,16},{24,20},{28,24},{32,28},{36,32}... | collective-permute-start | bytes 98312 | tf_op jit(solution)/shard_map/ppermute | solution.py:360
  38.5 3.9 %collective-permute-start.8 = (bf16[32,512]{1,0:T(8,128)(2,1)S(1)}, bf16[32,512]{1,0:T(8,128)(2,1)S(1)}, u32[]{:S(2)}, u32[]{:S(2)}) collective-permute-start(bf16[32,512]{1,0:T(8,128)(2,1)S(1)} %get-tuple-element.64), channel_id=1, source_target_pairs={{8,0},{12,4},{16,8},{20,12},{24,16},{28,20},{32,24},{36,28},{40,32... | collective-permute-start | bytes 98312 | tf_op jit(solution)/shard_map/ppermute | solution.py:360
  40.0 5.4 %collective-permute-start.9 = (bf16[32,512]{1,0:T(8,128)(2,1)S(1)}, bf16[32,512]{1,0:T(8,128)(2,1)S(1)}, u32[]{:S(2)}, u32[]{:S(2)}) collective-permute-start(bf16[32,512]{1,0:T(8,128)(2,1)S(1)} %get-tuple-element.65), channel_id=1, source_target_pairs={{64,0},{68,4},{72,8},{76,12},{80,16},{84,20},{88,24},{92,28},{96,3... | collective-permute-start | bytes 98312 | tf_op jit(solution)/shard_map/ppermute | solution.py:360
  61.7 3.9 %collective-permute-start.21 = (bf16[17,112,512]{2,1,0:T(8,128)(2,1)S(1)}, bf16[17,112,512]{2,1,0:T(8,128)(2,1)S(1)}, u32[]{:S(2)}, u32[]{:S(2)}) collective-permute-start(bf16[17,112,512]{2,1,0:T(8,128)(2,1)S(1)} %get-tuple-element.90), channel_id=1, source_target_pairs={{0,4},{4,0},{8,12},{12,8},{16,20},{20,16},{24,28},{28,24},{32,36},... | collective-permute-start | bytes 5849096 | tf_op jit(solution)/shard_map/ppermute | solution.py:404
  67.9 36.3 %copy-start.5 = (bf16[2,512,512]{2,1,0:T(8,128)(2,1)S(1)}, bf16[2,512,512]{2,1,0:T(8,128)(2,1)}, u32[]{:S(2)}) copy-start(bf16[2,512,512]{2,1,0:T(8,128)(2,1)} %we_out.5) | copy-start | bytes 3145732
  67.9 36.3 %copy-start.8 = (bf16[2,512,512]{2,1,0:T(8,128)(2,1)S(1)}, bf16[2,512,512]{2,1,0:T(8,128)(2,1)}, u32[]{:S(2)}) copy-start(bf16[2,512,512]{2,1,0:T(8,128)(2,1)} %wn_out.5) | copy-start | bytes 3145732
  67.9 36.3 %copy-start.11 = (bf16[1,1024,512]{2,1,0:T(8,128)(2,1)S(1)}, bf16[1,1024,512]{2,1,0:T(8,128)(2,1)}, u32[]{:S(2)}) copy-start(bf16[1,1024,512]{2,1,0:T(8,128)(2,1)} %eb_ref.3) | copy-start | bytes 3145732
  67.9 36.3 %copy-start.14 = (bf16[1,128,512]{2,1,0:T(8,128)(2,1)S(1)}, bf16[1,128,512]{2,1,0:T(8,128)(2,1)}, u32[]{:S(2)}) copy-start(bf16[1,128,512]{2,1,0:T(8,128)(2,1)} %vb_ref.5) | copy-start | bytes 393220
  67.9 36.3 %copy-start.25 = (s32[32,32]{1,0:T(8,128)S(1)}, s32[32,32]{1,0:T(8,128)}, u32[]{:S(2)}) copy-start(s32[32,32]{1,0:T(8,128)} %lists_ref.7) | copy-start | bytes 12292
  67.9 70.3 %all-to-all-start.1 = ((bf16[64,32,512]{2,1,0:T(8,128)(2,1)}), bf16[64,32,512]{2,1,0:T(8,128)(2,1)}, u32[]{:S(2)}, u32[]{:S(2)}) async-start(bf16[64,32,512]{2,1,0:T(8,128)(2,1)} %copy-done.9), calls=%async_computation.1 | async-start | bytes 4194304 | tf_op jit(solution)/shard_map/all_to_all | solution.py:407
  75.2 24.7 %collective-permute-start.10 = (bf16[32,512]{1,0:T(8,128)(2,1)}, bf16[32,512]{1,0:T(8,128)(2,1)S(1)}, u32[]{:S(2)}, u32[]{:S(2)}) collective-permute-start(bf16[32,512]{1,0:T(8,128)(2,1)} %copy-done.69), channel_id=1, source_target_pairs={{8,0},{12,4},{16,8},{20,12},{24,16},{28,20},{32,24},{36,28},{40,32... | collective-permute-start | bytes 98312 | tf_op jit(solution)/shard_map/ppermute | solution.py:360
  80.4 19.6 %collective-permute-start.11 = (bf16[32,512]{1,0:T(8,128)(2,1)}, bf16[32,512]{1,0:T(8,128)(2,1)S(1)}, u32[]{:S(2)}, u32[]{:S(2)}) collective-permute-start(bf16[32,512]{1,0:T(8,128)(2,1)} %copy-done.68), channel_id=1, source_target_pairs={{4,0},{8,4},{12,8},{16,12},{20,16},{24,20},{28,24},{32,28},{36,32}... | collective-permute-start | bytes 98312 | tf_op jit(solution)/shard_map/ppermute | solution.py:360
  80.4 20.7 %collective-permute-start.12 = (bf16[32,512]{1,0:T(8,128)(2,1)}, bf16[32,512]{1,0:T(8,128)(2,1)S(1)}, u32[]{:S(2)}, u32[]{:S(2)}) collective-permute-start(bf16[32,512]{1,0:T(8,128)(2,1)} %copy-done.67), channel_id=1, source_target_pairs={{124,0},{0,4},{4,8},{8,12},{12,16},{16,20},{20,24},{24,28},{28,32}... | collective-permute-start | bytes 98312 | tf_op jit(solution)/shard_map/ppermute | solution.py:360
  80.9 23.3 %collective-permute-start.13 = (bf16[32,512]{1,0:T(8,128)(2,1)}, bf16[32,512]{1,0:T(8,128)(2,1)S(1)}, u32[]{:S(2)}, u32[]{:S(2)}) collective-permute-start(bf16[32,512]{1,0:T(8,128)(2,1)} %copy-done.66), channel_id=1, source_target_pairs={{120,0},{124,4},{0,8},{4,12},{8,16},{12,20},{16,24},{20,28},{24,32... | collective-permute-start | bytes 98312 | tf_op jit(solution)/shard_map/ppermute | solution.py:360
  81.3 22.9 %collective-permute-start.14 = (bf16[32,512]{1,0:T(8,128)(2,1)}, bf16[32,512]{1,0:T(8,128)(2,1)S(1)}, u32[]{:S(2)}, u32[]{:S(2)}) collective-permute-start(bf16[32,512]{1,0:T(8,128)(2,1)} %copy-done.65), channel_id=1, source_target_pairs={{64,0},{68,4},{72,8},{76,12},{80,16},{84,20},{88,24},{92,28},{96,3... | collective-permute-start | bytes 98312 | tf_op jit(solution)/shard_map/ppermute | solution.py:360
  132.0 3.9 %collective-permute-start.20 = (bf16[17,112,512]{2,1,0:T(8,128)(2,1)S(1)}, bf16[17,112,512]{2,1,0:T(8,128)(2,1)S(1)}, u32[]{:S(2)}, u32[]{:S(2)}) collective-permute-start(bf16[17,112,512]{2,1,0:T(8,128)(2,1)S(1)} %get-tuple-element.88), channel_id=1, source_target_pairs={{0,4},{4,0},{8,12},{12,8},{16,20},{20,16},{24,28},{28,24},{32,36},... | collective-permute-start | bytes 5849096 | tf_op jit(solution)/shard_map/ppermute | solution.py:404
  138.2 36.8 %copy-start.29 = (f32[128,512]{1,0:T(8,128)S(1)}, f32[128,512]{1,0:T(8,128)}, u32[]{:S(2)}) copy-start(f32[128,512]{1,0:T(8,128)} %copy-done.28) | copy-start | bytes 786436
  138.2 36.8 %all-to-all-start = ((bf16[64,32,512]{2,1,0:T(8,128)(2,1)}), bf16[64,32,512]{2,1,0:T(8,128)(2,1)S(1)}, u32[]{:S(2)}, u32[]{:S(2)}) async-start(bf16[64,32,512]{2,1,0:T(8,128)(2,1)} %shard_map.192), calls=%async_computation | async-start | bytes 4194304 | tf_op jit(solution)/shard_map/all_to_all | solution.py:407
  144.7 25.0 %collective-permute-start.15 = (bf16[32,512]{1,0:T(8,128)(2,1)S(1)}, bf16[32,512]{1,0:T(8,128)(2,1)S(1)}, u32[]{:S(2)}, u32[]{:S(2)}) collective-permute-start(bf16[32,512]{1,0:T(8,128)(2,1)S(1)} %copy-done.64), channel_id=1, source_target_pairs={{8,0},{12,4},{16,8},{20,12},{24,16},{28,20},{32,24},{36,28},{40,32... | collective-permute-start | bytes 98312 | tf_op jit(solution)/shard_map/ppermute | solution.py:360
  149.9 19.8 %collective-permute-start.16 = (bf16[32,512]{1,0:T(8,128)(2,1)S(1)}, bf16[32,512]{1,0:T(8,128)(2,1)S(1)}, u32[]{:S(2)}, u32[]{:S(2)}) collective-permute-start(bf16[32,512]{1,0:T(8,128)(2,1)S(1)} %copy-done.62), channel_id=1, source_target_pairs={{4,0},{8,4},{12,8},{16,12},{20,16},{24,20},{28,24},{32,28},{36,32}... | collective-permute-start | bytes 98312 | tf_op jit(solution)/shard_map/ppermute | solution.py:360
  149.9 20.9 %collective-permute-start.17 = (bf16[32,512]{1,0:T(8,128)(2,1)S(1)}, bf16[32,512]{1,0:T(8,128)(2,1)S(1)}, u32[]{:S(2)}, u32[]{:S(2)}) collective-permute-start(bf16[32,512]{1,0:T(8,128)(2,1)S(1)} %copy-done.60), channel_id=1, source_target_pairs={{124,0},{0,4},{4,8},{8,12},{12,16},{16,20},{20,24},{24,28},{28,32}... | collective-permute-start | bytes 98312 | tf_op jit(solution)/shard_map/ppermute | solution.py:360
  150.4 23.5 %collective-permute-start.18 = (bf16[32,512]{1,0:T(8,128)(2,1)S(1)}, bf16[32,512]{1,0:T(8,128)(2,1)S(1)}, u32[]{:S(2)}, u32[]{:S(2)}) collective-permute-start(bf16[32,512]{1,0:T(8,128)(2,1)S(1)} %copy-done.58), channel_id=1, source_target_pairs={{120,0},{124,4},{0,8},{4,12},{8,16},{12,20},{16,24},{20,28},{24,32... | collective-permute-start | bytes 98312 | tf_op jit(solution)/shard_map/ppermute | solution.py:360
  150.9 23.0 %collective-permute-start.19 = (bf16[32,512]{1,0:T(8,128)(2,1)S(1)}, bf16[32,512]{1,0:T(8,128)(2,1)S(1)}, u32[]{:S(2)}, u32[]{:S(2)}) collective-permute-start(bf16[32,512]{1,0:T(8,128)(2,1)S(1)} %copy-done.56), channel_id=1, source_target_pairs={{64,0},{68,4},{72,8},{76,12},{80,16},{84,20},{88,24},{92,28},{96,3... | collective-permute-start | bytes 98312 | tf_op jit(solution)/shard_map/ppermute | solution.py:360
  (62 other events, 326.6 us)
where the time goes:
time: 181 us; the launch traced here: 179 us
  waiting for transfers between devices  61.4 us (34%)
  starting transfers between devices  44.9 us (25%)
  local copies, waits for them, and re-layouts  39.7 us (22%)
  Pallas kernels  31.4 us (17%)
    ppermute x20, waiting for transfers between devices, shift(): lax.ppermute(value, 'graph', [((i + sign * offset) % graph, i) for i in r...  52.5 us
    unnamed x141, local copies, waits for them, and re-layouts  39.7 us
    pallas_call x7, Pallas kernels, call(): pl.pallas_call(kernel, out_shape=outs, in_specs=specs, out_specs=jax.tree...  31.4 us
    ppermute x20, starting transfers between devices, shift(): lax.ppermute(value, 'graph', [((i + sign * offset) % graph, i) for i in r...  31.2 us
    all_to_all x2, starting transfers between devices, scatter(): lax.all_to_all(packed, ('graph', 'batch'), 0, 0, tiled=True, axis_index_g...  13.7 us
    ppermute x2, waiting for transfers between devices, scatter(): recv = lax.ppermute(send, 'graph', [(i, i ^ 1) for i in range(graph)])  7.89 us
  transfers between devices with their start and end apart: 24, of which 12 were waited for; matrix products, arithmetic and copies ran while one was open for 0% of the time, Pallas kernels for 6%

commit v1 on v0

v1 whole, which is shorter than its diff:
```python
import functools

import jax
import jax.numpy as jnp
from jax import lax
from jax.experimental import pallas as pl
from jax.experimental.pallas import tpu as pltpu
from jax.sharding import PartitionSpec as P

HOPS = 2
EPSILON = 1e-05
CHUNK = 256
ORDER = (4, 2, 3, 1, 0)
F32 = jnp.float32
BF16 = jnp.bfloat16


def nn(a, b):
    return lax.dot_general(a, b, (((1,), (0,)), ((), ())), preferred_element_type=F32)


def nt(a, b):
    return lax.dot_general(a, b, (((1,), (1,)), ((), ())), preferred_element_type=F32)


def tn(a, b):
    return lax.dot_general(a, b, (((0,), (0,)), ((), ())), preferred_element_type=F32)


def sigmoid(x):
    return 0.5 * jnp.tanh(0.5 * x) + 0.5


def layer_norm(z):
    centre = z - jnp.mean(z, axis=-1, keepdims=True)
    inv = lax.rsqrt(jnp.mean(centre * centre, axis=-1, keepdims=True) + EPSILON)
    return centre * inv, inv


def layer_norm_back(grad, gain, normed, inv):
    gn = grad * gain
    m1 = jnp.mean(gn, axis=-1, keepdims=True)
    m2 = jnp.mean(gn * normed, axis=-1, keepdims=True)
    return inv * (gn - m1 - normed * m2)


def swish_back(pre):
    s = sigmoid(pre)
    return s * (1.0 + pre * (1.0 - s))


def neighbours(own):
    return own ^ 1, ((((own - 1) & 31) ^ 1) + 1) & 31, (own - 2) & 31, (own + 2) & 31, own ^ 16


def readers(own):
    swap, near, below, above, far = neighbours(own)
    return swap, near, above, below, far


def list_onehot(lists_ref, reader, nodes):
    row = lists_ref[pl.ds(reader, 1), :]
    ids = lax.broadcasted_iota(jnp.int32, (nodes, row.shape[1]), 0)
    return jnp.where(ids == row, 1.0, 0.0).astype(BF16)


def send_blocks(lists_ref, own, vb, outs):
    for reader, out in zip(readers(own), outs):
        onehot = list_onehot(lists_ref, reader, vb.shape[0])
        out[...] = tn(onehot, vb).astype(BF16)


def returned(lists_ref, own, blocks):
    total = None
    for reader, block in zip(readers(own), blocks):
        term = nn(list_onehot(lists_ref, reader, 128), block[...])
        total = term if total is None else total + term
    return total


class Copies:
    def __init__(self, sems):
        self.sems, self.count = sems, 0

    def start(self, *pairs):
        handles = []
        for source, target in pairs:
            handles.append(pltpu.make_async_copy(source, target, self.sems.at[self.count]))
            self.count += 1
        for handle in handles:
            handle.start()
        return handles


def wait(handles):
    for handle in handles:
        handle.wait()


def load_weights(copies, layer, sources, targets):
    we_in, we_out, wn_in, wn_out = sources
    te_in, te_out, tn_in, tn_out = targets
    ends = copies.start((we_in.at[layer, pl.ds(512, 1024)], te_in.at[pl.ds(512, 1024)]))
    edge = copies.start((we_in.at[layer, pl.ds(0, 512)], te_in.at[pl.ds(0, 512)]), (we_out.at[layer], te_out))
    node = copies.start((wn_in.at[layer], tn_in), (wn_out.at[layer], tn_out))
    return ends, edge, node


def build_onehot(onehot_ref, slot_ref, receiver_ref, own):
    edges = slot_ref.shape[1]
    slot = slot_ref[...]
    row = slot - 128
    source = row >> 5
    block = jnp.full(source.shape, 4, jnp.int32)
    for n, other in enumerate(neighbours(own)[:4]):
        block = jnp.where(source == other, n, block)
    position = jnp.where(slot < 128, slot, 128 + block * 32 + (row & 31))
    ids = lax.broadcasted_iota(jnp.int32, (128, edges), 0)
    onehot_ref[0:128, :] = jnp.where(ids == receiver_ref[...], 1.0, 0.0).astype(BF16)
    ids = lax.broadcasted_iota(jnp.int32, (384, edges), 0)
    onehot_ref[128:512, :] = jnp.where(ids == position, 1.0, 0.0).astype(BF16)


def fill_projected(proj_ref, vb, sender_ref, w_in_ref):
    proj_ref[0:128, :] = nn(vb, w_in_ref[1024:1536, :]).astype(BF16)
    proj_ref[128:416, :] = nn(sender_ref[...], w_in_ref[512:1024, :]).astype(BF16)
    proj_ref[416:512, :] = jnp.zeros((96, 512), BF16)


def live_rows(base, count):
    rows = base + lax.broadcasted_iota(jnp.int32, (CHUNK, 1), 0)
    return jnp.where(rows < count, 1.0, 0.0).astype(F32)


def node_forward(vb, agg, w_in_ref, w_out_ref):
    pre = nn(vb, w_in_ref[0:512, :]) + nn(agg, w_in_ref[512:1024, :])
    hidden = (pre * sigmoid(pre)).astype(BF16)
    normed, inv = layer_norm(nn(hidden, w_out_ref[...]))
    return pre, hidden, normed, inv


def split_store(k, scratch_ref, keep_ref, send_ref, at, rows):
    for c in range(16):
        mine = pl.multiple_of(2 * c * rows + k * rows, 16)
        other = pl.multiple_of(2 * c * rows + (1 - k) * rows, 16)
        keep_ref[c, at : at + rows, :] = scratch_ref[pl.ds(mine, rows), :]
        send_ref[c, at : at + rows, :] = scratch_ref[pl.ds(other, rows), :]


def store_gains(edge_gain, node_gain, keep_ref, send_ref):
    pad = jnp.concatenate([edge_gain, node_gain, jnp.zeros((14, 512), F32)], axis=0).astype(BF16)
    keep_ref[16, 0:16, :] = pad
    send_ref[16, 0:16, :] = pad


def node_backward(grad, vb, agg, pre, hidden, normed, inv, w_in_ref, w_out_ref, gain, g_in_ref, g_out_ref):
    grad_gain = jnp.sum(grad * normed, axis=0, keepdims=True)
    dz = layer_norm_back(grad, gain, normed, inv).astype(BF16)
    g_out_ref[...] = tn(hidden, dz).astype(BF16)
    da = (nt(dz, w_out_ref[...]) * swish_back(pre)).astype(BF16)
    g_in_ref[0:512, :] = tn(vb, da).astype(BF16)
    g_in_ref[512:1024, :] = tn(agg, da).astype(BF16)
    return grad_gain, nt(da, w_in_ref[0:512, :]), nt(da, w_in_ref[512:1024, :])


def gather_kernel(own_ref, lists_ref, vb_ref, o0, o1, o2, o3, o4, lists, vb, sems):
    wait(Copies(sems).start((lists_ref, lists), (vb_ref.at[0], vb)))
    send_blocks(lists, own_ref[0], vb[...], (o0, o1, o2, o3, o4))


def forward_kernel(
    own_ref, count_ref, lists_ref, slot_ref, receiver_ref, vb_ref, eb_ref, b0, b1, b2, b3, b4,
    we_in_ref, we_out_ref, wn_in_ref, wn_out_ref, e_gain_ref, n_gain_ref,
    state_out, sides_out, eb_out, saved_out, inv_out, o0, o1, o2, o3, o4,
    lists, slot, receiver, eb, we_in, we_out, wn_in, wn_out, e_gain, n_gain,
    onehot, proj, message, state, sides, eb_next, saved, inv_s, sems,
):
    own, count = own_ref[0], count_ref[0]
    copies = Copies(sems)
    index = copies.start((slot_ref, slot), (receiver_ref, receiver))
    ends = copies.start((vb_ref.at[0], sides.at[pl.ds(0, 128)]))
    ends += copies.start(*[(block, sides.at[pl.ds(128 + 32 * n, 32)]) for n, block in enumerate((b0, b1, b2, b3, b4))])
    more, edge, node = load_weights(copies, 0, (we_in_ref, we_out_ref, wn_in_ref, wn_out_ref), (we_in, we_out, wn_in, wn_out))
    edge += copies.start((eb_ref.at[0], eb), (e_gain_ref, e_gain))
    node += copies.start((n_gain_ref, n_gain), (lists_ref, lists))
    wait(index)
    build_onehot(onehot, slot, receiver, own)
    wait(ends + more)
    vb = sides[0:128, :]
    fill_projected(proj, vb, sides.at[0:288], we_in)
    wait(edge)
    gain = e_gain[0:1, :]
    saves = []
    for n in range(eb.shape[0] // CHUNK):
        rows = slice(n * CHUNK, (n + 1) * CHUNK)
        part = pl.ds(n * CHUNK, CHUNK)
        latent = eb[rows, :]
        pre = nn(latent, we_in[0:512, :]) + tn(onehot[:, rows], proj[...])
        hidden = (pre * sigmoid(pre)).astype(BF16)
        normed, inv = layer_norm(nn(hidden, we_out[...]))
        m = normed * gain * live_rows(n * CHUNK, count)
        saved[0, rows, :] = pre.astype(BF16)
        saved[1, rows, :] = normed.astype(BF16)
        inv_s[rows, :] = jnp.broadcast_to(inv, (CHUNK, 128))
        message[rows, :] = m.astype(BF16)
        eb_next[rows, :] = (latent.astype(F32) + m).astype(BF16)
        saves += copies.start(
            (eb_next.at[part], eb_out.at[part]), (saved.at[0, part], saved_out.at[0, part]),
            (saved.at[1, part], saved_out.at[1, part]), (inv_s.at[part], inv_out.at[part]),
        )
    agg = nn(onehot[0:128, :], message[...]).astype(BF16)
    wait(node)
    pre, _, normed, inv = node_forward(vb, agg, wn_in, wn_out)
    v = vb.astype(F32) + normed * n_gain[0:1, :]
    state[0] = v
    state[1] = pre
    state[2] = normed
    state[3] = jnp.broadcast_to(inv, (128, 512))
    sides[288:416, :] = agg
    saves += copies.start((state, state_out), (sides, sides_out))
    send_blocks(lists, own, v.astype(BF16), (o0, o1, o2, o3, o4))
    wait(saves)


def edge_tail(onehot, senders, vb, eb, h_ref, dz_ref, da_ref, we_in, g_in, g_out, outs):
    g_out[...] = tn(h_ref[...], dz_ref[...]).astype(BF16)
    g_in[0:512, :] = tn(eb[...], da_ref[...]).astype(BF16)
    gathered = nn(onehot[0:416, :], da_ref[...]).astype(BF16)
    at_receiver = gathered[0:128, :]
    at_sender = gathered[128:416, :]
    g_in[512:1024, :] = tn(senders[...], at_sender).astype(BF16)
    g_in[1024:1536, :] = tn(vb, at_receiver).astype(BF16)
    back = nt(at_sender, we_in[512:1024, :])
    for n, out in enumerate(outs):
        out[...] = back[128 + 32 * n : 160 + 32 * n, :].astype(BF16)
    return nt(at_receiver, we_in[1024:1536, :]) + back[0:128, :]


def write_grads(k, g_in, g_out, gn_in, gn_out, edge_gain, node_gain, keep, send):
    split_store(k, g_in, keep, send, 0, 48)
    split_store(k, g_out, keep, send, 48, 16)
    split_store(k, gn_in, keep, send, 64, 32)
    split_store(k, gn_out, keep, send, 96, 16)
    store_gains(edge_gain, node_gain, keep, send)


def middle_kernel(
    own_ref, count_ref, slot_ref, receiver_ref, state_ref, eb_ref, cot_ref, b0, b1, b2, b3, b4,
    we_in_ref, we_out_ref, wn_in_ref, wn_out_ref, e_gain_ref, n_gain_ref,
    node_out, edge_grad_out, grad_out, keep, send, o0, o1, o2, o3, o4,
    slot, receiver, v, cot, eb, we_in, we_out, wn_in, wn_out, e_gain, n_gain,
    onehot, senders, proj, message, pre_s, normed_s, inv_s, hidden_s, dz_s, da_s, edge_grad, g_in, g_out, gn_in, gn_out, sems,
):
    own, count = own_ref[0], count_ref[0]
    copies = Copies(sems)
    index = copies.start((slot_ref, slot), (receiver_ref, receiver), (state_ref.at[0], v))
    ends = copies.start(*[(block, senders.at[pl.ds(128 + 32 * n, 32)]) for n, block in enumerate((b0, b1, b2, b3, b4))])
    more, edge, node = load_weights(copies, 1, (we_in_ref, we_out_ref, wn_in_ref, wn_out_ref), (we_in, we_out, wn_in, wn_out))
    edge += copies.start((eb_ref, eb), (e_gain_ref, e_gain))
    node += copies.start((n_gain_ref, n_gain), (cot_ref.at[0], cot))
    wait(index)
    build_onehot(onehot, slot, receiver, own)
    vb = v[...].astype(BF16)
    senders[0:128, :] = vb
    wait(ends + more)
    fill_projected(proj, vb, senders, we_in)
    wait(edge)
    gain = e_gain[1:2, :]
    chunks = eb.shape[0] // CHUNK
    for n in range(chunks):
        rows = slice(n * CHUNK, (n + 1) * CHUNK)
        pre = nn(eb[rows, :], we_in[0:512, :]) + tn(onehot[:, rows], proj[...])
        hidden = (pre * sigmoid(pre)).astype(BF16)
        normed, inv = layer_norm(nn(hidden, we_out[...]))
        m = normed * gain * live_rows(n * CHUNK, count)
        pre_s[rows, :] = pre
        normed_s[rows, :] = normed
        inv_s[rows, :] = jnp.broadcast_to(inv, (CHUNK, 128))
        hidden_s[rows, :] = hidden
        message[rows, :] = m.astype(BF16)
    agg = nn(onehot[0:128, :], message[...]).astype(BF16)
    wait(node)
    n_pre, n_hidden, n_normed, n_inv = node_forward(vb, agg, wn_in, wn_out)
    n_gain_row = n_gain[1:2, :]
    v[...] = v[...] + n_normed * n_gain_row
    saves = copies.start((v, node_out.at[0]))
    grad = cot[...].astype(F32)
    grad_n_gain, grad_v, grad_agg = node_backward(
        grad, vb, agg, n_pre, n_hidden, n_normed, n_inv, wn_in, wn_out, n_gain_row, gn_in, gn_out
    )
    grad_agg = grad_agg.astype(BF16)
    grad_e_gain = jnp.zeros((1, 512), F32)
    for n in range(chunks):
        rows = slice(n * CHUNK, (n + 1) * CHUNK)
        gm = tn(onehot[0:128, rows], grad_agg) * live_rows(n * CHUNK, count)
        normed = normed_s[rows, :]
        grad_e_gain += jnp.sum(gm * normed, axis=0, keepdims=True)
        dz = layer_norm_back(gm, gain, normed, inv_s[rows, 0:1]).astype(BF16)
        dz_s[rows, :] = dz
        da = (nt(dz, we_out[...]) * swish_back(pre_s[rows, :])).astype(BF16)
        da_s[rows, :] = da
        edge_grad[rows, :] = nt(da, we_in[0:512, :]).astype(BF16)
    saves += copies.start((edge_grad, edge_grad_out))
    grad_ends = edge_tail(onehot, senders, vb, eb, hidden_s, dz_s, da_s, we_in, g_in, g_out, (o0, o1, o2, o3, o4))
    grad_out[...] = grad + grad_v + grad_ends
    write_grads(own & 1, g_in, g_out, gn_in, gn_out, grad_e_gain, grad_n_gain, keep, send)
    wait(saves)


def backward_kernel(
    own_ref, count_ref, slot_ref, receiver_ref, eb_ref, grad_ref, state_ref, sides_ref, edge_grad_ref, saved_ref, inv_ref,
    we_in_ref, we_out_ref, wn_in_ref, wn_out_ref, e_gain_ref, n_gain_ref,
    grad_out, keep, send, o0, o1, o2, o3, o4,
    slot, receiver, eb, grad_s, state, sides, edge_grad, saved, inv_s, we_in, we_out, wn_in, wn_out, e_gain, n_gain,
    onehot, hidden_s, dz_s, da_s, g_in, g_out, gn_in, gn_out, sems,
):
    own, count = own_ref[0], count_ref[0]
    copies = Copies(sems)
    first = copies.start((slot_ref, slot), (receiver_ref, receiver), (grad_ref, grad_s), (state_ref.at[pl.ds(1, 3)], state))
    first += copies.start((sides_ref, sides), (n_gain_ref, n_gain), (wn_out_ref.at[0], wn_out), (wn_in_ref.at[0], wn_in))
    edge = copies.start((edge_grad_ref, edge_grad), (saved_ref, saved), (inv_ref, inv_s), (e_gain_ref, e_gain), (we_out_ref.at[0], we_out))
    last = copies.start((eb_ref.at[0], eb), (we_in_ref.at[0], we_in))
    wait(first)
    build_onehot(onehot, slot, receiver, own)
    vb = sides[0:128, :]
    grad = grad_s[...]
    n_pre = state[0]
    n_hidden = (n_pre * sigmoid(n_pre)).astype(BF16)
    grad_n_gain, grad_v, grad_agg = node_backward(
        grad, vb, sides[288:416, :], n_pre, n_hidden, state[1], state[2], wn_in, wn_out, n_gain[0:1, :], gn_in, gn_out
    )
    grad_agg = grad_agg.astype(BF16)
    wait(edge)
    gain = e_gain[0:1, :]
    grad_e_gain = jnp.zeros((1, 512), F32)
    for n in range(eb.shape[0] // CHUNK):
        rows = slice(n * CHUNK, (n + 1) * CHUNK)
        gm = tn(onehot[0:128, rows], grad_agg) + edge_grad[rows, :].astype(F32)
        gm = gm * live_rows(n * CHUNK, count)
        normed = saved[1, rows, :].astype(F32)
        grad_e_gain += jnp.sum(gm * normed, axis=0, keepdims=True)
        dz = layer_norm_back(gm, gain, normed, inv_s[rows, 0:1]).astype(BF16)
        dz_s[rows, :] = dz
        pre = saved[0, rows, :].astype(F32)
        s = sigmoid(pre)
        hidden_s[rows, :] = (pre * s).astype(BF16)
        da_s[rows, :] = (nt(dz, we_out[...]) * (s * (1.0 + pre * (1.0 - s)))).astype(BF16)
    wait(last)
    grad_ends = edge_tail(onehot, sides.at[0:288], vb, eb, hidden_s, dz_s, da_s, we_in, g_in, g_out, (o0, o1, o2, o3, o4))
    grad_out[...] = grad + grad_v + grad_ends
    write_grads(own & 1, g_in, g_out, gn_in, gn_out, grad_e_gain, grad_n_gain, keep, send)


def pack_blocks(keep_ref, recv_ref, out_ref, stage, packed, sems):
    gains = (keep_ref[16, 0:16, :].astype(F32) + recv_ref[16, 0:16, :].astype(F32))[0:8, :]
    copies = Copies(sems)
    saves = []
    for c in range(16):
        rows = keep_ref[c].astype(F32) + recv_ref[c].astype(F32)
        for b in range(4):
            stage[b, 0:12, :] = rows[12 * b : 12 * b + 12, :]
            stage[b, 12:16, :] = rows[48 + 4 * b : 52 + 4 * b, :]
            stage[b, 16:24, :] = rows[64 + 8 * b : 72 + 8 * b, :]
            stage[b, 24:28, :] = rows[96 + 4 * b : 100 + 4 * b, :]
            stage[b, 28:32, :] = gains[0:4, :]
            packed[4 * c + b] = stage[b].astype(BF16)
        saves += copies.start((packed.at[pl.ds(4 * c, 4)], out_ref.at[pl.ds(4 * c, 4)]))
    return saves


def pack_kernel(keep_ref, recv_ref, out_ref, stage, packed, sems):
    wait(pack_blocks(keep_ref, recv_ref, out_ref, stage, packed, sems))


def pack_return_kernel(own_ref, keep_ref, recv_ref, grad_ref, lists_ref, r0, r1, r2, r3, r4, out_ref, grad_out, stage, packed, lists, grad_s, sems, grad_sems):
    loads = Copies(grad_sems)
    load = loads.start((lists_ref, lists))
    saves = pack_blocks(keep_ref, recv_ref, out_ref, stage, packed, sems)
    wait(load)
    grad_s[...] = grad_ref[...] + returned(lists, own_ref[0], (r0, r1, r2, r3, r4))
    wait(saves + loads.start((grad_s, grad_out)))


def sum_blocks(x):
    def step(n, total):
        return total + x[n].astype(F32)

    return lax.fori_loop(0, 64, step, jnp.zeros((32, 512), F32), unroll=8)


def sum_kernel(x_ref, out_ref, x, sems):
    wait(Copies(sems).start((x_ref, x)))
    out_ref[...] = sum_blocks(x)


def finish_kernel(
    device_ref, own_ref, lists_ref, grad_ref, r0, r1, r2, r3, r4, x0_ref, total1_ref,
    node_grad, g_e_in, g_e_out, g_n_in, g_n_out, g_e_gain, g_n_gain,
    lists, stage, sems,
):
    wait(Copies(sems).start((lists_ref, lists)))
    node_grad[0] = grad_ref[...] + returned(lists, own_ref[0], (r0, r1, r2, r3, r4))
    picks = lax.broadcasted_iota(jnp.int32, (512, 128), 0) - 4 * device_ref[0]
    select = jnp.where(picks == lax.broadcasted_iota(jnp.int32, (512, 128), 1), 1.0, 0.0).astype(F32)
    for layer in (1, 0):
        if layer == 0:
            stage[...] = sum_blocks(x0_ref)
        else:
            stage[...] = total1_ref[...]
        g_e_in[layer] = stage[0:12, :]
        g_e_out[layer] = stage[12:16, :]
        g_n_in[layer] = stage[16:24, :]
        g_n_out[layer] = stage[24:28, :]
        gains = lax.dot_general(
            stage[24:32, :], select, (((1,), (0,)), ((), ())), precision=lax.Precision.HIGHEST, preferred_element_type=F32
        )
        g_e_gain[layer : layer + 1, :] = gains[4:5, 0:4]
        g_n_gain[layer : layer + 1, :] = gains[5:6, 0:4]


def body(
    node_latent,
    edge_latent,
    node_cotangent,
    edge_w_in,
    edge_w_out,
    node_w_in,
    node_w_out,
    edge_gain,
    node_gain,
    edge_slot,
    edge_receiver,
    send_list,
    edge_count,
):
    width = node_latent.shape[2]
    nodes = node_latent.shape[1]
    edges = edge_slot.shape[0]
    graph = lax.axis_size("graph")
    own = lax.axis_index("graph").astype(jnp.int32)
    own_arr = own.reshape(1)
    device = (own * lax.axis_size("batch") + lax.axis_index("batch").astype(jnp.int32)).reshape(1)
    slot = edge_slot.reshape(1, edges)
    receiver = edge_receiver.reshape(1, edges)
    sds = jax.ShapeDtypeStruct
    vmem = pl.BlockSpec(memory_space=pltpu.VMEM)
    smem = pl.BlockSpec(memory_space=pltpu.SMEM)
    free = pl.BlockSpec(memory_space=pl.ANY)
    hbm = pl.BlockSpec(memory_space=pltpu.HBM)

    def exchange(blocks, back):
        sources = [(readers if back else neighbours)(i) for i in range(graph)]
        outs = {}
        for n in ORDER:
            outs[n] = lax.ppermute(blocks[n], "graph", [(sources[i][n], i) for i in range(graph)])
        return [outs[n] for n in range(5)]

    def call(kernel, mib, outs, scratch, specs, args):
        shapes = [pltpu.HBM(o.shape, o.dtype) if place is hbm else o for o, place in outs]
        args = [pltpu.with_memory_space_constraint(a, pltpu.HBM) if place is hbm else a for a, place in zip(args, specs)]
        return pl.pallas_call(
            kernel,
            out_shape=shapes,
            in_specs=[free if place is hbm else place for place in specs],
            out_specs=[free if place is hbm else place for _, place in outs],
            scratch_shapes=scratch,
            compiler_params=pltpu.CompilerParams(vmem_limit_bytes=mib * 1024 * 1024),
        )(*args)

    def vb16(*shape):
        return pltpu.VMEM(shape, BF16)

    def vf32(*shape):
        return pltpu.VMEM(shape, F32)

    def sems(n):
        return pltpu.SemaphoreType.DMA((n,))

    index_s = [pltpu.VMEM((1, edges), jnp.int32)] * 2
    lists_s = pltpu.VMEM(send_list.shape, jnp.int32)
    weights_s = [vb16(*w.shape[1:]) for w in (edge_w_in, edge_w_out, node_w_in, node_w_out)] + [vf32(*edge_gain.shape), vf32(*node_gain.shape)]
    weight_args = (edge_w_in, edge_w_out, node_w_in, node_w_out, edge_gain, node_gain)
    edge_b, edge_f = vb16(edges, width), vf32(edges, width)
    grads_s = [vb16(r, width) for r in (1536, 512, 1024, 512)]
    blocks_out = [(sds((32, width), BF16), vmem)] * 5
    half = (sds((17, 112, width), BF16), vmem)
    node_b, node_f, inv_s = vb16(nodes, width), vf32(nodes, width), vf32(edges, 128)

    first = call(gather_kernel, 2, blocks_out, [lists_s, node_b, sems(2)], [smem, hbm, hbm], (own_arr, send_list, node_latent))
    senders0 = exchange(first, False)
    state0, sides0, eb1, saved0, inv0, *second = call(
        forward_kernel,
        24,
        [(sds((4, nodes, width), F32), hbm), (sds((416, width), BF16), hbm), (sds((edges, width), BF16), hbm), (sds((2, edges, width), BF16), hbm), (sds((edges, 128), F32), hbm)] + blocks_out,
        [lists_s] + index_s + [edge_b] + weights_s + [vb16(512, edges), vb16(512, width), edge_b, vf32(4, nodes, width), vb16(416, width), edge_b, vb16(2, edges, width), inv_s, sems(48)],
        [smem, smem] + [hbm] * 5 + [free] * 5 + [hbm] * 6,
        (own_arr, edge_count, send_list, slot, receiver, node_latent, edge_latent, *senders0, *weight_args),
    )
    senders1 = exchange(second, False)
    node_out, edge_grad, grad1, keep1, send1, *back1 = call(
        middle_kernel,
        32,
        [(sds((1, nodes, width), F32), hbm), (sds((edges, width), BF16), hbm), (sds((nodes, width), F32), vmem), half, half] + blocks_out,
        index_s + [node_f, node_b, edge_b] + weights_s + [vb16(512, edges), vb16(288, width), vb16(512, width), edge_b, edge_f, edge_f, inv_s, edge_b, edge_b, edge_b, edge_b] + grads_s + [sems(24)],
        [smem, smem] + [hbm] * 5 + [free] * 5 + [hbm] * 6,
        (own_arr, edge_count, slot, receiver, state0, eb1, node_cotangent, *senders1, *weight_args),
    )

    def swap(send):
        return lax.ppermute(send, "graph", [(i, i ^ 1) for i in range(graph)])

    def spread(packed):
        groups = [[(2 * c + k) * 4 + b for c in range(16) for b in range(4)] for k in range(2)]
        return lax.all_to_all(packed, ("graph", "batch"), 0, 0, tiled=True, axis_index_groups=groups)

    packed_out = (sds((64, 32, width), BF16), hbm)
    pack_s = [vf32(4, 32, width), vb16(64, 32, width)]
    returned1 = exchange(back1, True)
    packed1, grad1 = call(
        pack_return_kernel,
        6,
        [packed_out, (sds((nodes, width), F32), hbm)],
        pack_s + [lists_s, node_f, sems(16), sems(2)],
        [smem, vmem, vmem, vmem, hbm] + [vmem] * 5,
        (own_arr, keep1, swap(send1), grad1, send_list, *returned1),
    )
    x1 = spread(packed1)
    grad0, keep0, send0, *back0 = call(
        backward_kernel,
        24,
        [(sds((nodes, width), F32), vmem), half, half] + blocks_out,
        index_s + [edge_b, node_f, vf32(3, nodes, width), vb16(416, width), edge_b, vb16(2, edges, width), inv_s] + weights_s + [vb16(512, edges), edge_b, edge_b, edge_b] + grads_s + [sems(24)],
        [smem, smem] + [hbm] * 15,
        (own_arr, edge_count, slot, receiver, edge_latent, grad1, state0, sides0, edge_grad, saved0, inv0, *weight_args),
    )
    returned0 = exchange(back0, True)
    (packed0,) = call(pack_kernel, 6, [packed_out], pack_s + [sems(16)], [vmem, vmem], (keep0, swap(send0)))
    x0 = spread(packed0)
    (total1,) = call(sum_kernel, 4, [(sds((32, width), F32), vmem)], [vb16(64, 32, width), sems(1)], [free], (x1,))
    grads = call(
        finish_kernel,
        6,
        [(sds((1, nodes, width), F32), vmem)] + [(sds((2, r, width), F32), vmem) for r in (12, 4, 8, 4)] + [(sds((2, 4), F32), vmem)] * 2,
        [lists_s, vf32(32, width), sems(1)],
        [smem, smem, hbm] + [vmem] * 8,
        (device, own_arr, send_list, grad0, *returned0, x0, total1),
    )
    return (node_out, *grads)


def solution(mesh):
    in_specs = (
        P("batch", "graph", None),
        P("batch", "graph", None),
        P("batch", "graph", None),
        P(),
        P(),
        P(),
        P(),
        P(),
        P(),
        P("graph"),
        P("graph"),
        P("graph", None),
        P("graph"),
    )
    out_specs = (
        P("batch", "graph", None),
        P("batch", "graph", None),
        P(None, ("graph", "batch"), None),
        P(None, ("graph", "batch"), None),
        P(None, ("graph", "batch"), None),
        P(None, ("graph", "batch"), None),
        P(None, ("graph", "batch")),
        P(None, ("graph", "batch")),
    )
    return jax.shard_map(body, mesh=mesh, in_specs=in_specs, out_specs=out_specs, check_vma=False)
```

time: 181 us -> 146 us (0.81)
  local copies, waits for them, and re-layouts: 39.7 us -> 0.66 us
  Pallas kernels: 31.4 us -> 39.5 us
  waiting for transfers between devices: 61.4 us -> 55.4 us
  starting transfers between devices: 44.9 us -> 48 us
    unnamed x141 -> x1, local copies, waits for them, and re-layouts: 39.7 us -> 0.66 us
    ppermute x22, waiting for transfers between devices: 60.3 us -> 40.8 us  [the longest x20 37.2 us: exchange(): lax.ppermute(blocks[n], 'graph', [(sources[i][n], i) for i in range(graph)])]
    all_to_all x2, waiting for transfers between devices: 1.08 us -> 14.6 us  [spread(): lax.all_to_all(packed, ('graph', 'batch'), 0, 0, tiled=True, axis_index_g...]
    pallas_call x7 -> x8, Pallas kernels: 31.4 us -> 39.5 us  [call(): pl.pallas_call(kernel, out_shape=shapes, in_specs=[free if place is hbm e...]
    ppermute x22, starting transfers between devices: 31.2 us -> 33.1 us  [the longest x20 31.3 us: exchange(): lax.ppermute(blocks[n], 'graph', [(sources[i][n], i) for i in range(graph)])]
  transfers between devices with their start and end apart: 24 -> 24, of which waited for: 12 -> 11; matrix products, arithmetic and copies ran while one was open for 0% -> 0% of each run, Pallas kernels for 6% -> 8%
where the time goes in v1:
time: 146 us; the launch traced here: 145 us
  waiting for transfers between devices  55.4 us (38%)
  starting transfers between devices  48 us (33%)
  Pallas kernels  39.5 us (27%)
    pallas_call x8, Pallas kernels, call(): pl.pallas_call(kernel, out_shape=shapes, in_specs=[free if place is hbm e...  39.5 us
    ppermute x20, waiting for transfers between devices, exchange(): lax.ppermute(blocks[n], 'graph', [(sources[i][n], i) for i in range(graph)])  37.2 us
    ppermute x20, starting transfers between devices, exchange(): lax.ppermute(blocks[n], 'graph', [(sources[i][n], i) for i in range(graph)])  31.3 us
    all_to_all x2, starting transfers between devices, spread(): lax.all_to_all(packed, ('graph', 'batch'), 0, 0, tiled=True, axis_index_g...  15 us
    all_to_all x2, waiting for transfers between devices, spread(): lax.all_to_all(packed, ('graph', 'batch'), 0, 0, tiled=True, axis_index_g...  14.6 us
    ppermute x2, waiting for transfers between devices, swap(): return lax.ppermute(send, 'graph', [(i, i ^ 1) for i in range(graph)])  3.58 us
  transfers between devices with their start and end apart: 24, of which 11 were waited for; matrix products, arithmetic and copies ran while one was open for 0% of the time, Pallas kernels for 8%

profile of v1, /device:TPU:0, one launch (start us, length us, event | category | flops | bytes accessed | tf_op | source)
XLA Modules:
  0.0 145.0 jit_solution(12284765741337334324)
XLA Ops:
  0.6 1.2 shard_map.188
  1.9 6.4 %collective-permute-start.1 = (bf16[32,512]{1,0:T(8,128)(2,1)S(1)}, bf16[32,512]{1,0:T(8,128)(2,1)S(1)}, u32[]{:S(2)}, u32[]{:S(2)}) collective-permute-start(bf16[32,512]{1,0:T(8,128)(2,1)S(1)} %get-tuple-element.51), channel_id=1, source_target_pairs={{124,0},{8,4},{4,8},{16,12},{12,16},{24,20},{20,24},{32,28},{28,32... | collective-permute-start | bytes 98312 | tf_op jit(solution)/shard_map/ppermute | solution.py:455
  8.4 5.3 %collective-permute-start.3 = (bf16[32,512]{1,0:T(8,128)(2,1)S(1)}, bf16[32,512]{1,0:T(8,128)(2,1)S(1)}, u32[]{:S(2)}, u32[]{:S(2)}) collective-permute-start(bf16[32,512]{1,0:T(8,128)(2,1)S(1)} %get-tuple-element.53), channel_id=1, source_target_pairs={{8,0},{12,4},{16,8},{20,12},{24,16},{28,20},{32,24},{36,28},{40,32... | collective-permute-start | bytes 98312 | tf_op jit(solution)/shard_map/ppermute | solution.py:455
  14.4 1.2 collective-permute-done.2.b2
  15.6 3.5 %collective-permute-done.4.b4 = bf16[32,512]{1,0:T(8,128)(2,1)S(1)} collective-permute-done((bf16[32,512]{1,0:T(8,128)(2,1)S(1)}, bf16[32,512]{1,0:T(8,128)(2,1)S(1)}, u32[]{:S(2)}, u32[]{:S(2)}) %collective-permute-start.4) | collective-permute-done | bytes 32800 | tf_op jit(solution)/shard_map/ppermute | solution.py:455
  19.2 7.8 %shard_map.189 = (f32[4,128,512]{2,1,0:T(8,128)}, bf16[416,512]{1,0:T(8,128)(2,1)}, bf16[1024,512]{1,0:T(8,128)(2,1)}, bf16[2,1024,512]{2,1,0:T(8,128)(2,1)}, f3...) custom-call(s32[1]{0:T(128)} %bitcast.own_ref, ...), custom_call_target="tpu_custom_call" | custom-call | tf_op jit(solution)/shard_map/pallas_call | solution.py:461
  27.0 1.9 %collective-permute-start.6 = (bf16[32,512]{1,0:T(8,128)(2,1)S(1)}, bf16[32,512]{1,0:T(8,128)(2,1)S(1)}, u32[]{:S(2)}, u32[]{:S(2)}) collective-permute-start(bf16[32,512]{1,0:T(8,128)(2,1)S(1)} %get-tuple-element.58), channel_id=1, source_target_pairs={{124,0},{8,4},{4,8},{16,12},{12,16},{24,20},{20,24},{32,28},{28,32... | collective-permute-start | bytes 98312 | tf_op jit(solution)/shard_map/ppermute | solution.py:455
  29.2 5.2 %collective-permute-start.8 = (bf16[32,512]{1,0:T(8,128)(2,1)S(1)}, bf16[32,512]{1,0:T(8,128)(2,1)S(1)}, u32[]{:S(2)}, u32[]{:S(2)}) collective-permute-start(bf16[32,512]{1,0:T(8,128)(2,1)S(1)} %get-tuple-element.60), channel_id=1, source_target_pairs={{8,0},{12,4},{16,8},{20,12},{24,16},{28,20},{32,24},{36,28},{40,32... | collective-permute-start | bytes 98312 | tf_op jit(solution)/shard_map/ppermute | solution.py:455
  34.3 1.9 %collective-permute-done.7.b2 = bf16[32,512]{1,0:T(8,128)(2,1)S(1)} collective-permute-done((bf16[32,512]{1,0:T(8,128)(2,1)S(1)}, bf16[32,512]{1,0:T(8,128)(2,1)S(1)}, u32[]{:S(2)}, u32[]{:S(2)}) %collective-permute-start.7) | collective-permute-done | bytes 32800 | tf_op jit(solution)/shard_map/ppermute | solution.py:455
  36.2 3.5 %collective-permute-done.9.b4 = bf16[32,512]{1,0:T(8,128)(2,1)S(1)} collective-permute-done((bf16[32,512]{1,0:T(8,128)(2,1)S(1)}, bf16[32,512]{1,0:T(8,128)(2,1)S(1)}, u32[]{:S(2)}, u32[]{:S(2)}) %collective-permute-start.9) | collective-permute-done | bytes 32800 | tf_op jit(solution)/shard_map/ppermute | solution.py:455
  39.7 13.4 %shard_map.190 = (f32[1,128,512]{2,1,0:T(8,128)}, bf16[1024,512]{1,0:T(8,128)(2,1)}, f32[128,512]{1,0:T(8,128)S(1)}, bf16[17,112,512]{2,1,0:T(8,128)(2,1)S(1)}, ...) custom-call(s32[1]{0:T(128)} %bitcast.own_ref, ...), custom_call_target="tpu_custom_call" | custom-call | tf_op jit(solution)/shard_map/pallas_call | solution.py:461
  53.7 1.5 %collective-permute-start.12 = (bf16[32,512]{1,0:T(8,128)(2,1)S(1)}, bf16[32,512]{1,0:T(8,128)(2,1)S(1)}, u32[]{:S(2)}, u32[]{:S(2)}) collective-permute-start(bf16[32,512]{1,0:T(8,128)(2,1)S(1)} %get-tuple-element.67), channel_id=1, source_target_pairs={{124,0},{8,4},{4,8},{16,12},{12,16},{24,20},{20,24},{32,28},{28,32... | collective-permute-start | bytes 98312 | tf_op jit(solution)/shard_map/ppermute | solution.py:455
  55.6 1.7 %collective-permute-start.14 = (bf16[32,512]{1,0:T(8,128)(2,1)S(1)}, bf16[32,512]{1,0:T(8,128)(2,1)S(1)}, u32[]{:S(2)}, u32[]{:S(2)}) collective-permute-start(bf16[32,512]{1,0:T(8,128)(2,1)S(1)} %get-tuple-element.69), channel_id=1, source_target_pairs={{120,0},{124,4},{0,8},{4,12},{8,16},{12,20},{16,24},{20,28},{24,32... | collective-permute-start | bytes 98312 | tf_op jit(solution)/shard_map/ppermute | solution.py:455
  57.3 3.1 %collective-permute-done.12.r1 = bf16[32,512]{1,0:T(8,128)(2,1)S(1)} collective-permute-done((bf16[32,512]{1,0:T(8,128)(2,1)S(1)}, bf16[32,512]{1,0:T(8,128)(2,1)S(1)}, u32[]{:S(2)}, u32[]{:S(2)}) %collective-permute-start.12) | collective-permute-done | bytes 32800 | tf_op jit(solution)/shard_map/ppermute | solution.py:455
  60.4 2.7 %collective-permute-done.14.r3 = bf16[32,512]{1,0:T(8,128)(2,1)S(1)} collective-permute-done((bf16[32,512]{1,0:T(8,128)(2,1)S(1)}, bf16[32,512]{1,0:T(8,128)(2,1)S(1)}, u32[]{:S(2)}, u32[]{:S(2)}) %collective-permute-start.14) | collective-permute-done | bytes 32800 | tf_op jit(solution)/shard_map/ppermute | solution.py:455
  63.1 2.2 %shard_map.191 = (bf16[64,32,512]{2,1,0:T(8,128)(2,1)}, f32[128,512]{1,0:T(8,128)}) custom-call(s32[1]{0:T(128)} %bitcast.own_ref, bf16[17,112,512]{2,1,0:T(8,128)(2,1)S(1)} %get-tuple-element.63.keep_ref, bf16[17,112,512]{2,1,0:T(8,128)(2,1)S(1)} %collective-permute-done.10.recv_ref, f32[128,512]{1,0:T(8,128)S(1)} %get-tuple-element.65.grad_ref, ...), custom_call_target="tpu_custom_call" | custom-call | tf_op jit(solution)/shard_map/pallas_call | solution.py:461
  65.3 8.4 %all-to-all-start.1 = ((bf16[64,32,512]{2,1,0:T(8,128)(2,1)}), bf16[64,32,512]{2,1,0:T(8,128)(2,1)S(1)}, u32[]{:S(2)}, u32[]{:S(2)}) async-start(bf16[64,32,512]{2,1,0:T(8,128)(2,1)} %get-tuple-element.84), calls=%async_computation.1 | async-start | bytes 4194304 | tf_op jit(solution)/shard_map/all_to_all | solution.py:514
  73.7 9.0 %shard_map.192 = (f32[128,512]{1,0:T(8,128)S(1)}, bf16[17,112,512]{2,1,0:T(8,128)(2,1)S(1)}, bf16[17,112,512]{2,1,0:T(8,128)(2,1)S(1)}, bf16[32,512]{1,0:T(8,128...) custom-call(s32[1]{0:T(128)} %bitcast.own_ref, ...), custom_call_target="tpu_custom_call" | custom-call | tf_op jit(solution)/shard_map/pallas_call | solution.py:461
  82.7 1.7 %collective-permute-start.21 = (bf16[17,112,512]{2,1,0:T(8,128)(2,1)S(1)}, bf16[17,112,512]{2,1,0:T(8,128)(2,1)S(1)}, u32[]{:S(2)}, u32[]{:S(2)}) collective-permute-start(bf16[17,112,512]{2,1,0:T(8,128)(2,1)S(1)} %get-tuple-element.83), channel_id=1, source_target_pairs={{0,4},{4,0},{8,12},{12,8},{16,20},{20,16},{24,28},{28,24},{32,36},... | collective-permute-start | bytes 5849096 | tf_op jit(solution)/shard_map/ppermute | solution.py:510
  84.4 3.6 %collective-permute-done.21.recv_ref = bf16[17,112,512]{2,1,0:T(8,128)(2,1)S(1)} collective-permute-done((bf16[17,112,512]{2,1,0:T(8,128)(2,1)S(1)}, bf16[17,112,512]{2,1,0:T(8,128)(2,1)S(1)}, u32[]{:S(2)}, u32[]{:S(2)}) %collective-permute-start.21) | collective-permute-done | bytes 1949728 | tf_op jit(solution)/shard_map/ppermute | solution.py:510
  88.0 1.6 %shard_map.193 = bf16[64,32,512]{2,1,0:T(8,128)(2,1)} custom-call(bf16[17,112,512]{2,1,0:T(8,128)(2,1)S(1)} %get-tuple-element.82.keep_ref, bf16[17,112,512]{2,1,0:T(8,128)(2,1)S(1)} %collective-permute-done.21.recv_ref), custom_call_target="tpu_custom_call" | custom-call | tf_op jit(solution)/shard_map/pallas_call | solution.py:461
  89.6 13.9 %all-to-all-done.1.x_ref = bf16[64,32,512]{2,1,0:T(8,128)(2,1)S(1)} async-done(((bf16[64,32,512]{2,1,0:T(8,128)(2,1)}), bf16[64,32,512]{2,1,0:T(8,128)(2,1)S(1)}, u32[]{:S(2)}, u32[]{:S(2)}) %all-to-all-start.1) | async-done | bytes 2097184 | tf_op jit(solution)/shard_map/all_to_all | solution.py:514
  103.5 6.5 %all-to-all-start = ((bf16[64,32,512]{2,1,0:T(8,128)(2,1)}), bf16[64,32,512]{2,1,0:T(8,128)(2,1)}, u32[]{:S(2)}, u32[]{:S(2)}) async-start(bf16[64,32,512]{2,1,0:T(8,128)(2,1)} %shard_map.193), calls=%async_computation | async-start | bytes 4194304 | tf_op jit(solution)/shard_map/all_to_all | solution.py:514
  110.4 5.0 %collective-permute-start.17 = (bf16[32,512]{1,0:T(8,128)(2,1)S(1)}, bf16[32,512]{1,0:T(8,128)(2,1)S(1)}, u32[]{:S(2)}, u32[]{:S(2)}) collective-permute-start(bf16[32,512]{1,0:T(8,128)(2,1)S(1)} %get-tuple-element.78), channel_id=1, source_target_pairs={{124,0},{8,4},{4,8},{16,12},{12,16},{24,20},{20,24},{32,28},{28,32... | collective-permute-start | bytes 98312 | tf_op jit(solution)/shard_map/ppermute | solution.py:455
  115.4 0.8 collective-permute-start.18
  116.2 1.2 collective-permute-start.19
  117.4 0.6 collective-permute-start.20
  118.5 19.3 %collective-permute-done.17.r1 = bf16[32,512]{1,0:T(8,128)(2,1)S(1)} collective-permute-done((bf16[32,512]{1,0:T(8,128)(2,1)S(1)}, bf16[32,512]{1,0:T(8,128)(2,1)S(1)}, u32[]{:S(2)}, u32[]{:S(2)}) %collective-permute-start.17) | collective-permute-done | bytes 32800 | tf_op jit(solution)/shard_map/ppermute | solution.py:455
  137.8 1.9 %collective-permute-done.19.r3 = bf16[32,512]{1,0:T(8,128)(2,1)S(1)} collective-permute-done((bf16[32,512]{1,0:T(8,128)(2,1)S(1)}, bf16[32,512]{1,0:T(8,128)(2,1)S(1)}, u32[]{:S(2)}, u32[]{:S(2)}) %collective-permute-start.19) | collective-permute-done | bytes 32800 | tf_op jit(solution)/shard_map/ppermute | solution.py:455
  139.8 0.7 all-to-all-done.x0_ref
  140.5 3.8 %shard_map.195 = (f32[1,128,512]{2,1,0:T(8,128)}, f32[2,12,512]{2,1,0:T(8,128)S(1)}, f32[2,4,512]{2,1,0:T(4,128)}, f32[2,8,512]{2,1,0:T(8,128)}, f32[2,4,512]{2,...) custom-call(s32[1]{0:T(128)} %bitcast.3.device_ref, s32[1]{0:T(128)} %bitcast.own_ref, s32[32,32]{1,0:T(8,128)} %lists_ref.7, ...), custom_call_target="tpu_custom_call" | custom-call | tf_op jit(solution)/shard_map/pallas_call | solution.py:461
  144.3 0.7 copy.21
  (25 shorter events, 2.1 us)
Async XLA Ops:
  1.9 12.5 %collective-permute-start = (bf16[32,512]{1,0:T(8,128)(2,1)S(1)}, bf16[32,512]{1,0:T(8,128)(2,1)S(1)}, u32[]{:S(2)}, u32[]{:S(2)}) collective-permute-start(bf16[32,512]{1,0:T(8,128)(2,1)S(1)} %get-tuple-element.50), channel_id=1, source_target_pairs={{4,0},{0,4},{12,8},{8,12},{20,16},{16,20},{28,24},{24,28},{36,32},... | collective-permute-start | bytes 98312 | tf_op jit(solution)/shard_map/ppermute | solution.py:455
  1.9 12.5 %collective-permute-start.1 = (bf16[32,512]{1,0:T(8,128)(2,1)S(1)}, bf16[32,512]{1,0:T(8,128)(2,1)S(1)}, u32[]{:S(2)}, u32[]{:S(2)}) collective-permute-start(bf16[32,512]{1,0:T(8,128)(2,1)S(1)} %get-tuple-element.51), channel_id=1, source_target_pairs={{124,0},{8,4},{4,8},{16,12},{12,16},{24,20},{20,24},{32,28},{28,32... | collective-permute-start | bytes 98312 | tf_op jit(solution)/shard_map/ppermute | solution.py:455
  8.4 7.2 %collective-permute-start.2 = (bf16[32,512]{1,0:T(8,128)(2,1)S(1)}, bf16[32,512]{1,0:T(8,128)(2,1)S(1)}, u32[]{:S(2)}, u32[]{:S(2)}) collective-permute-start(bf16[32,512]{1,0:T(8,128)(2,1)S(1)} %get-tuple-element.52), channel_id=1, source_target_pairs={{120,0},{124,4},{0,8},{4,12},{8,16},{12,20},{16,24},{20,28},{24,32... | collective-permute-start | bytes 98312 | tf_op jit(solution)/shard_map/ppermute | solution.py:455
  8.4 7.2 %collective-permute-start.3 = (bf16[32,512]{1,0:T(8,128)(2,1)S(1)}, bf16[32,512]{1,0:T(8,128)(2,1)S(1)}, u32[]{:S(2)}, u32[]{:S(2)}) collective-permute-start(bf16[32,512]{1,0:T(8,128)(2,1)S(1)} %get-tuple-element.53), channel_id=1, source_target_pairs={{8,0},{12,4},{16,8},{20,12},{24,16},{28,20},{32,24},{36,28},{40,32... | collective-permute-start | bytes 98312 | tf_op jit(solution)/shard_map/ppermute | solution.py:455
  13.7 5.4 %collective-permute-start.4 = (bf16[32,512]{1,0:T(8,128)(2,1)S(1)}, bf16[32,512]{1,0:T(8,128)(2,1)S(1)}, u32[]{:S(2)}, u32[]{:S(2)}) collective-permute-start(bf16[32,512]{1,0:T(8,128)(2,1)S(1)} %get-tuple-element.54), channel_id=1, source_target_pairs={{64,0},{68,4},{72,8},{76,12},{80,16},{84,20},{88,24},{92,28},{96,3... | collective-permute-start | bytes 98312 | tf_op jit(solution)/shard_map/ppermute | solution.py:455
  26.9 7.4 %collective-permute-start.5 = (bf16[32,512]{1,0:T(8,128)(2,1)S(1)}, bf16[32,512]{1,0:T(8,128)(2,1)S(1)}, u32[]{:S(2)}, u32[]{:S(2)}) collective-permute-start(bf16[32,512]{1,0:T(8,128)(2,1)S(1)} %get-tuple-element.57), channel_id=1, source_target_pairs={{4,0},{0,4},{12,8},{8,12},{20,16},{16,20},{28,24},{24,28},{36,32},... | collective-permute-start | bytes 98312 | tf_op jit(solution)/shard_map/ppermute | solution.py:455
  27.0 7.3 %collective-permute-start.6 = (bf16[32,512]{1,0:T(8,128)(2,1)S(1)}, bf16[32,512]{1,0:T(8,128)(2,1)S(1)}, u32[]{:S(2)}, u32[]{:S(2)}) collective-permute-start(bf16[32,512]{1,0:T(8,128)(2,1)S(1)} %get-tuple-element.58), channel_id=1, source_target_pairs={{124,0},{8,4},{4,8},{16,12},{12,16},{24,20},{20,24},{32,28},{28,32... | collective-permute-start | bytes 98312 | tf_op jit(solution)/shard_map/ppermute | solution.py:455
  29.0 7.2 %collective-permute-start.7 = (bf16[32,512]{1,0:T(8,128)(2,1)S(1)}, bf16[32,512]{1,0:T(8,128)(2,1)S(1)}, u32[]{:S(2)}, u32[]{:S(2)}) collective-permute-start(bf16[32,512]{1,0:T(8,128)(2,1)S(1)} %get-tuple-element.59), channel_id=1, source_target_pairs={{120,0},{124,4},{0,8},{4,12},{8,16},{12,20},{16,24},{20,28},{24,32... | collective-permute-start | bytes 98312 | tf_op jit(solution)/shard_map/ppermute | solution.py:455
  29.2 7.0 %collective-permute-start.8 = (bf16[32,512]{1,0:T(8,128)(2,1)S(1)}, bf16[32,512]{1,0:T(8,128)(2,1)S(1)}, u32[]{:S(2)}, u32[]{:S(2)}) collective-permute-start(bf16[32,512]{1,0:T(8,128)(2,1)S(1)} %get-tuple-element.60), channel_id=1, source_target_pairs={{8,0},{12,4},{16,8},{20,12},{24,16},{28,20},{32,24},{36,28},{40,32... | collective-permute-start | bytes 98312 | tf_op jit(solution)/shard_map/ppermute | solution.py:455
  34.3 5.4 %collective-permute-start.9 = (bf16[32,512]{1,0:T(8,128)(2,1)S(1)}, bf16[32,512]{1,0:T(8,128)(2,1)S(1)}, u32[]{:S(2)}, u32[]{:S(2)}) collective-permute-start(bf16[32,512]{1,0:T(8,128)(2,1)S(1)} %get-tuple-element.61), channel_id=1, source_target_pairs={{64,0},{68,4},{72,8},{76,12},{80,16},{84,20},{88,24},{92,28},{96,3... | collective-permute-start | bytes 98312 | tf_op jit(solution)/shard_map/ppermute | solution.py:455
  53.1 9.9 %collective-permute-start.10 = (bf16[17,112,512]{2,1,0:T(8,128)(2,1)S(1)}, bf16[17,112,512]{2,1,0:T(8,128)(2,1)S(1)}, u32[]{:S(2)}, u32[]{:S(2)}) collective-permute-start(bf16[17,112,512]{2,1,0:T(8,128)(2,1)S(1)} %get-tuple-element.64), channel_id=1, source_target_pairs={{0,4},{4,0},{8,12},{12,8},{16,20},{20,16},{24,28},{28,24},{32,36},... | collective-permute-start | bytes 5849096 | tf_op jit(solution)/shard_map/ppermute | solution.py:510
  53.2 4.1 %collective-permute-start.11 = (bf16[32,512]{1,0:T(8,128)(2,1)S(1)}, bf16[32,512]{1,0:T(8,128)(2,1)S(1)}, u32[]{:S(2)}, u32[]{:S(2)}) collective-permute-start(bf16[32,512]{1,0:T(8,128)(2,1)S(1)} %get-tuple-element.66), channel_id=1, source_target_pairs={{4,0},{0,4},{12,8},{8,12},{20,16},{16,20},{28,24},{24,28},{36,32},... | collective-permute-start | bytes 98312 | tf_op jit(solution)/shard_map/ppermute | solution.py:455
  53.7 6.7 %collective-permute-start.12 = (bf16[32,512]{1,0:T(8,128)(2,1)S(1)}, bf16[32,512]{1,0:T(8,128)(2,1)S(1)}, u32[]{:S(2)}, u32[]{:S(2)}) collective-permute-start(bf16[32,512]{1,0:T(8,128)(2,1)S(1)} %get-tuple-element.67), channel_id=1, source_target_pairs={{124,0},{8,4},{4,8},{16,12},{12,16},{24,20},{20,24},{32,28},{28,32... | collective-permute-start | bytes 98312 | tf_op jit(solution)/shard_map/ppermute | solution.py:455
  55.3 5.1 %collective-permute-start.13 = (bf16[32,512]{1,0:T(8,128)(2,1)S(1)}, bf16[32,512]{1,0:T(8,128)(2,1)S(1)}, u32[]{:S(2)}, u32[]{:S(2)}) collective-permute-start(bf16[32,512]{1,0:T(8,128)(2,1)S(1)} %get-tuple-element.68), channel_id=1, source_target_pairs={{8,0},{12,4},{16,8},{20,12},{24,16},{28,20},{32,24},{36,28},{40,32... | collective-permute-start | bytes 98312 | tf_op jit(solution)/shard_map/ppermute | solution.py:455
  55.6 7.5 %collective-permute-start.14 = (bf16[32,512]{1,0:T(8,128)(2,1)S(1)}, bf16[32,512]{1,0:T(8,128)(2,1)S(1)}, u32[]{:S(2)}, u32[]{:S(2)}) collective-permute-start(bf16[32,512]{1,0:T(8,128)(2,1)S(1)} %get-tuple-element.69), channel_id=1, source_target_pairs={{120,0},{124,4},{0,8},{4,12},{8,16},{12,20},{16,24},{20,28},{24,32... | collective-permute-start | bytes 98312 | tf_op jit(solution)/shard_map/ppermute | solution.py:455
  57.3 5.8 %collective-permute-start.15 = (bf16[32,512]{1,0:T(8,128)(2,1)S(1)}, bf16[32,512]{1,0:T(8,128)(2,1)S(1)}, u32[]{:S(2)}, u32[]{:S(2)}) collective-permute-start(bf16[32,512]{1,0:T(8,128)(2,1)S(1)} %get-tuple-element.70), channel_id=1, source_target_pairs={{64,0},{68,4},{72,8},{76,12},{80,16},{84,20},{88,24},{92,28},{96,3... | collective-permute-start | bytes 98312 | tf_op jit(solution)/shard_map/ppermute | solution.py:455
  65.3 38.2 %all-to-all-start.1 = ((bf16[64,32,512]{2,1,0:T(8,128)(2,1)}), bf16[64,32,512]{2,1,0:T(8,128)(2,1)S(1)}, u32[]{:S(2)}, u32[]{:S(2)}) async-start(bf16[64,32,512]{2,1,0:T(8,128)(2,1)} %get-tuple-element.84), calls=%async_computation.1 | async-start | bytes 4194304 | tf_op jit(solution)/shard_map/all_to_all | solution.py:514
  82.7 5.3 %collective-permute-start.21 = (bf16[17,112,512]{2,1,0:T(8,128)(2,1)S(1)}, bf16[17,112,512]{2,1,0:T(8,128)(2,1)S(1)}, u32[]{:S(2)}, u32[]{:S(2)}) collective-permute-start(bf16[17,112,512]{2,1,0:T(8,128)(2,1)S(1)} %get-tuple-element.83), channel_id=1, source_target_pairs={{0,4},{4,0},{8,12},{12,8},{16,20},{20,16},{24,28},{28,24},{32,36},... | collective-permute-start | bytes 5849096 | tf_op jit(solution)/shard_map/ppermute | solution.py:510
  103.5 37.0 %all-to-all-start = ((bf16[64,32,512]{2,1,0:T(8,128)(2,1)}), bf16[64,32,512]{2,1,0:T(8,128)(2,1)}, u32[]{:S(2)}, u32[]{:S(2)}) async-start(bf16[64,32,512]{2,1,0:T(8,128)(2,1)} %shard_map.193), calls=%async_computation | async-start | bytes 4194304 | tf_op jit(solution)/shard_map/all_to_all | solution.py:514
  110.1 8.4 %collective-permute-start.16 = (bf16[32,512]{1,0:T(8,128)(2,1)S(1)}, bf16[32,512]{1,0:T(8,128)(2,1)S(1)}, u32[]{:S(2)}, u32[]{:S(2)}) collective-permute-start(bf16[32,512]{1,0:T(8,128)(2,1)S(1)} %get-tuple-element.77), channel_id=1, source_target_pairs={{4,0},{0,4},{12,8},{8,12},{20,16},{16,20},{28,24},{24,28},{36,32},... | collective-permute-start | bytes 98312 | tf_op jit(solution)/shard_map/ppermute | solution.py:455
  110.4 27.4 %collective-permute-start.17 = (bf16[32,512]{1,0:T(8,128)(2,1)S(1)}, bf16[32,512]{1,0:T(8,128)(2,1)S(1)}, u32[]{:S(2)}, u32[]{:S(2)}) collective-permute-start(bf16[32,512]{1,0:T(8,128)(2,1)S(1)} %get-tuple-element.78), channel_id=1, source_target_pairs={{124,0},{8,4},{4,8},{16,12},{12,16},{24,20},{20,24},{32,28},{28,32... | collective-permute-start | bytes 98312 | tf_op jit(solution)/shard_map/ppermute | solution.py:455
  115.4 22.5 %collective-permute-start.18 = (bf16[32,512]{1,0:T(8,128)(2,1)S(1)}, bf16[32,512]{1,0:T(8,128)(2,1)S(1)}, u32[]{:S(2)}, u32[]{:S(2)}) collective-permute-start(bf16[32,512]{1,0:T(8,128)(2,1)S(1)} %get-tuple-element.79), channel_id=1, source_target_pairs={{8,0},{12,4},{16,8},{20,12},{24,16},{28,20},{32,24},{36,28},{40,32... | collective-permute-start | bytes 98312 | tf_op jit(solution)/shard_map/ppermute | solution.py:455
  116.2 23.6 %collective-permute-start.19 = (bf16[32,512]{1,0:T(8,128)(2,1)S(1)}, bf16[32,512]{1,0:T(8,128)(2,1)S(1)}, u32[]{:S(2)}, u32[]{:S(2)}) collective-permute-start(bf16[32,512]{1,0:T(8,128)(2,1)S(1)} %get-tuple-element.80), channel_id=1, source_target_pairs={{120,0},{124,4},{0,8},{4,12},{8,16},{12,20},{16,24},{20,28},{24,32... | collective-permute-start | bytes 98312 | tf_op jit(solution)/shard_map/ppermute | solution.py:455
  117.4 22.4 %collective-permute-start.20 = (bf16[32,512]{1,0:T(8,128)(2,1)S(1)}, bf16[32,512]{1,0:T(8,128)(2,1)S(1)}, u32[]{:S(2)}, u32[]{:S(2)}) collective-permute-start(bf16[32,512]{1,0:T(8,128)(2,1)S(1)} %get-tuple-element.81), channel_id=1, source_target_pairs={{64,0},{68,4},{72,8},{76,12},{80,16},{84,20},{88,24},{92,28},{96,3... | collective-permute-start | bytes 98312 | tf_op jit(solution)/shard_map/ppermute | solution.py:455

commit v2 on v1

v2 whole, which is shorter than its diff:
```python
import jax
import jax.numpy as jnp
from jax import lax
from jax.experimental import pallas as pl
from jax.experimental.pallas import tpu as pltpu
from jax.sharding import PartitionSpec as P


EPSILON = 1e-05
CHUNK = 256
ORDER = (4, 2, 3, 1, 0)
F32 = jnp.float32
BF16 = jnp.bfloat16


def nn(a, b):
    return lax.dot_general(a, b, (((1,), (0,)), ((), ())), preferred_element_type=F32)


def nt(a, b):
    return lax.dot_general(a, b, (((1,), (1,)), ((), ())), preferred_element_type=F32)


def tn(a, b):
    return lax.dot_general(a, b, (((0,), (0,)), ((), ())), preferred_element_type=F32)


def sigmoid(x):
    return 0.5 * jnp.tanh(0.5 * x) + 0.5


def layer_norm(z):
    centre = z - jnp.mean(z, axis=-1, keepdims=True)
    inv = lax.rsqrt(jnp.mean(centre * centre, axis=-1, keepdims=True) + EPSILON)
    return centre * inv, inv


def layer_norm_back(grad, gain, normed, inv):
    gn = grad * gain
    m1 = jnp.mean(gn, axis=-1, keepdims=True)
    m2 = jnp.mean(gn * normed, axis=-1, keepdims=True)
    return inv * (gn - m1 - normed * m2)


def swish_back(pre):
    s = sigmoid(pre)
    return s * (1.0 + pre * (1.0 - s))


def neighbours(own):
    return own ^ 1, ((((own - 1) & 31) ^ 1) + 1) & 31, (own - 2) & 31, (own + 2) & 31, own ^ 16


def readers(own):
    swap, near, below, above, far = neighbours(own)
    return swap, near, above, below, far


def list_onehot(lists_ref, reader, nodes):
    row = lists_ref[pl.ds(reader, 1), :]
    ids = lax.broadcasted_iota(jnp.int32, (nodes, row.shape[1]), 0)
    return jnp.where(ids == row, 1.0, 0.0).astype(BF16)


def send_blocks(lists_ref, own, vb, outs):
    for reader, out in zip(readers(own), outs):
        onehot = list_onehot(lists_ref, reader, vb.shape[0])
        out[...] = tn(onehot, vb).astype(BF16)


def returned(lists_ref, own, blocks):
    total = None
    for reader, block in zip(readers(own), blocks):
        term = nn(list_onehot(lists_ref, reader, 128), block[...])
        total = term if total is None else total + term
    return total


class Copies:
    def __init__(self, sems):
        self.sems, self.count = sems, 0

    def start(self, *pairs):
        handles = []
        for source, target in pairs:
            handles.append(pltpu.make_async_copy(source, target, self.sems.at[self.count]))
            self.count += 1
        for handle in handles:
            handle.start()
        return handles


def wait(handles):
    for handle in handles:
        handle.wait()


def build_onehot(onehot_ref, slot_ref, receiver_ref, own):
    edges = slot_ref.shape[1]
    slot = slot_ref[...]
    row = slot - 128
    source = row >> 5
    block = jnp.full(source.shape, 4, jnp.int32)
    for n, other in enumerate(neighbours(own)[:4]):
        block = jnp.where(source == other, n, block)
    position = jnp.where(slot < 128, slot, 128 + block * 32 + (row & 31))
    ids = lax.broadcasted_iota(jnp.int32, (128, edges), 0)
    onehot_ref[0:128, :] = jnp.where(ids == receiver_ref[...], 1.0, 0.0).astype(BF16)
    ids = lax.broadcasted_iota(jnp.int32, (384, edges), 0)
    onehot_ref[128:512, :] = jnp.where(ids == position, 1.0, 0.0).astype(BF16)


def live_rows(base, count):
    rows = base + lax.broadcasted_iota(jnp.int32, (CHUNK, 1), 0)
    return jnp.where(rows < count, 1.0, 0.0).astype(F32)


def node_forward(vb, agg, w_in_ref, w_out_ref):
    pre = nn(vb, w_in_ref[0:512, :]) + nn(agg, w_in_ref[512:1024, :])
    hidden = (pre * sigmoid(pre)).astype(BF16)
    normed, inv = layer_norm(nn(hidden, w_out_ref[...]))
    return pre, hidden, normed, inv


def split_store(k, scratch_ref, keep_ref, send_ref, at, rows):
    for c in range(16):
        mine = pl.multiple_of(2 * c * rows + k * rows, 16)
        other = pl.multiple_of(2 * c * rows + (1 - k) * rows, 16)
        keep_ref[c, at : at + rows, :] = scratch_ref[pl.ds(mine, rows), :]
        send_ref[c, at : at + rows, :] = scratch_ref[pl.ds(other, rows), :]


def store_gains(edge_gain, node_gain, keep_ref, send_ref):
    pad = jnp.concatenate([edge_gain, node_gain, jnp.zeros((14, 512), F32)], axis=0).astype(BF16)
    keep_ref[16, 0:16, :] = pad
    send_ref[16, 0:16, :] = pad


def node_backward(grad, vb, agg, pre, hidden, normed, inv, w_in_ref, w_out_ref, gain, g_in_ref, g_out_ref):
    grad_gain = jnp.sum(grad * normed, axis=0, keepdims=True)
    dz = layer_norm_back(grad, gain, normed, inv).astype(BF16)
    g_out_ref[...] = tn(hidden, dz).astype(BF16)
    da = (nt(dz, w_out_ref[...]) * swish_back(pre)).astype(BF16)
    g_in_ref[0:512, :] = tn(vb, da).astype(BF16)
    g_in_ref[512:1024, :] = tn(agg, da).astype(BF16)
    return grad_gain, nt(da, w_in_ref[0:512, :]), nt(da, w_in_ref[512:1024, :])


def gather_kernel(own_ref, lists_ref, vb_ref, lists, vb, o0, o1, o2, o3, o4, sems):
    wait(Copies(sems).start((lists_ref, lists), (vb_ref.at[0], vb)))
    send_blocks(lists, own_ref[0], vb[...], (o0, o1, o2, o3, o4))


def start_weights(copies, layer, sources, targets):
    return [copies.start((source.at[layer], target)) for source, target in zip(sources, targets)]


def first_kernel(
    own_ref, slot_ref, receiver_ref, eb_ref, vb, we_in_ref, we_out_ref, wn_in_ref, wn_out_ref, e_gain_ref, n_gain_ref,
    onehot, eb, we_in, we_out, wn_in, wn_out, e_gain, n_gain, part, proj,
    slot, receiver, sems,
):
    copies = Copies(sems)
    index = copies.start((slot_ref, slot), (receiver_ref, receiver))
    loads = start_weights(copies, 0, (we_in_ref, we_out_ref, wn_in_ref, wn_out_ref), (we_in, we_out, wn_in, wn_out))
    latent = copies.start((eb_ref.at[0], eb))
    gains = copies.start((e_gain_ref, e_gain), (n_gain_ref, n_gain))
    wait(index)
    build_onehot(onehot, slot, receiver, own_ref[0])
    wait(loads[0])
    proj[0:128, :] = nn(vb[...], we_in[1024:1536, :]).astype(BF16)
    proj[128:256, :] = nn(vb[...], we_in[512:1024, :]).astype(BF16)
    wait(latent)
    part[...] = nn(eb[...], we_in[0:512, :])
    for load in loads[1:]:
        wait(load)
    wait(gains)


def second_kernel(
    state, eb, cot_ref, we_in_ref, we_out_ref, wn_in_ref, wn_out_ref,
    cot, we_in, we_out, wn_in, wn_out, part, proj, sems,
):
    copies = Copies(sems)
    loads = start_weights(copies, 1, (we_in_ref, we_out_ref, wn_in_ref, wn_out_ref), (we_in, we_out, wn_in, wn_out))
    load = copies.start((cot_ref.at[0], cot))
    vb = state[0].astype(BF16)
    wait(loads[0])
    proj[0:128, :] = nn(vb, we_in[1024:1536, :]).astype(BF16)
    proj[128:256, :] = nn(vb, we_in[512:1024, :]).astype(BF16)
    part[...] = nn(eb[...], we_in[0:512, :])
    for handles in loads[1:]:
        wait(handles)
    wait(load)


def fill_remote(proj, near, senders, vb, blocks, w_in_ref):
    senders[0:128, :] = vb
    for n, block in enumerate(blocks):
        senders[128 + 32 * n : 160 + 32 * n, :] = block[...]
    proj[0:256, :] = near[...]
    proj[256:416, :] = nn(senders[128:288, :], w_in_ref[512:1024, :]).astype(BF16)
    proj[416:512, :] = jnp.zeros((96, 512), BF16)


def forward_kernel(
    own_ref, count_ref, lists, vb_ref, onehot, eb, we_in, we_out, wn_in, wn_out, e_gain, n_gain, part, near, b0, b1, b2, b3, b4,
    state, sides, eb_next, saved_out, inv_out, o0, o1, o2, o3, o4,
    proj, message, saved, inv_s, sems,
):
    own, count = own_ref[0], count_ref[0]
    vb = vb_ref[...]
    fill_remote(proj, near, sides, vb, (b0, b1, b2, b3, b4), we_in)
    gain = e_gain[0:1, :]
    copies, saves = Copies(sems), []
    for n in range(eb.shape[0] // CHUNK):
        rows = slice(n * CHUNK, (n + 1) * CHUNK)
        pre = part[rows, :] + tn(onehot[:, rows], proj[...])
        hidden = (pre * sigmoid(pre)).astype(BF16)
        normed, inv = layer_norm(nn(hidden, we_out[...]))
        m = normed * gain * live_rows(n * CHUNK, count)
        saved[0, rows, :] = pre.astype(BF16)
        saved[1, rows, :] = normed.astype(BF16)
        inv_s[rows, :] = jnp.broadcast_to(inv, (CHUNK, 128))
        message[rows, :] = m.astype(BF16)
        eb_next[rows, :] = (eb[rows, :].astype(F32) + m).astype(BF16)
        at = pl.ds(n * CHUNK, CHUNK)
        saves += copies.start(
            (saved.at[0, at], saved_out.at[0, at]), (saved.at[1, at], saved_out.at[1, at]), (inv_s.at[at], inv_out.at[at])
        )
    agg = nn(onehot[0:128, :], message[...]).astype(BF16)
    pre, _, normed, inv = node_forward(vb, agg, wn_in, wn_out)
    v = vb.astype(F32) + normed * n_gain[0:1, :]
    state[0] = v
    state[1] = pre
    state[2] = normed
    state[3] = jnp.broadcast_to(inv, (128, 512))
    sides[288:416, :] = agg
    send_blocks(lists, own, v.astype(BF16), (o0, o1, o2, o3, o4))
    wait(saves)


def edge_tail(onehot, senders, vb, eb, h_ref, dz_ref, da_ref, we_in, g_in, g_out, outs):
    g_out[...] = tn(h_ref[...], dz_ref[...]).astype(BF16)
    g_in[0:512, :] = tn(eb[...], da_ref[...]).astype(BF16)
    gathered = nn(onehot[0:416, :], da_ref[...]).astype(BF16)
    at_receiver = gathered[0:128, :]
    at_sender = gathered[128:416, :]
    g_in[512:1024, :] = tn(senders[...], at_sender).astype(BF16)
    g_in[1024:1536, :] = tn(vb, at_receiver).astype(BF16)
    back = nt(at_sender, we_in[512:1024, :])
    for n, out in enumerate(outs):
        out[...] = back[128 + 32 * n : 160 + 32 * n, :].astype(BF16)
    return nt(at_receiver, we_in[1024:1536, :]) + back[0:128, :]


def write_grads(k, g_in, g_out, gn_in, gn_out, edge_gain, node_gain, keep, send):
    split_store(k, g_in, keep, send, 0, 48)
    split_store(k, g_out, keep, send, 48, 16)
    split_store(k, gn_in, keep, send, 64, 32)
    split_store(k, gn_out, keep, send, 96, 16)
    store_gains(edge_gain, node_gain, keep, send)


def middle_kernel(
    own_ref, count_ref, state, onehot, eb, cot, we_in, we_out, wn_in, wn_out, e_gain, n_gain, part, near, b0, b1, b2, b3, b4,
    node_out, edge_grad_out, grad_out, keep, send, o0, o1, o2, o3, o4,
    v, edge_grad, senders, proj, message, pre_s, normed_s, inv_s, hidden_s, dz_s, da_s, g_in, g_out, gn_in, gn_out, sems,
):
    own, count = own_ref[0], count_ref[0]
    vb = state[0].astype(BF16)
    fill_remote(proj, near, senders, vb, (b0, b1, b2, b3, b4), we_in)
    gain = e_gain[1:2, :]
    chunks = eb.shape[0] // CHUNK
    for n in range(chunks):
        rows = slice(n * CHUNK, (n + 1) * CHUNK)
        pre = part[rows, :] + tn(onehot[:, rows], proj[...])
        hidden = (pre * sigmoid(pre)).astype(BF16)
        normed, inv = layer_norm(nn(hidden, we_out[...]))
        m = normed * gain * live_rows(n * CHUNK, count)
        pre_s[rows, :] = pre
        normed_s[rows, :] = normed
        inv_s[rows, :] = jnp.broadcast_to(inv, (CHUNK, 128))
        hidden_s[rows, :] = hidden
        message[rows, :] = m.astype(BF16)
    agg = nn(onehot[0:128, :], message[...]).astype(BF16)
    n_pre, n_hidden, n_normed, n_inv = node_forward(vb, agg, wn_in, wn_out)
    n_gain_row = n_gain[1:2, :]
    v[...] = state[0] + n_normed * n_gain_row
    copies = Copies(sems)
    saves = copies.start((v, node_out.at[0]))
    grad = cot[...].astype(F32)
    grad_n_gain, grad_v, grad_agg = node_backward(
        grad, vb, agg, n_pre, n_hidden, n_normed, n_inv, wn_in, wn_out, n_gain_row, gn_in, gn_out
    )
    grad_agg = grad_agg.astype(BF16)
    grad_e_gain = jnp.zeros((1, 512), F32)
    for n in range(chunks):
        rows = slice(n * CHUNK, (n + 1) * CHUNK)
        gm = tn(onehot[0:128, rows], grad_agg) * live_rows(n * CHUNK, count)
        normed = normed_s[rows, :]
        grad_e_gain += jnp.sum(gm * normed, axis=0, keepdims=True)
        dz = layer_norm_back(gm, gain, normed, inv_s[rows, 0:1]).astype(BF16)
        dz_s[rows, :] = dz
        da = (nt(dz, we_out[...]) * swish_back(pre_s[rows, :])).astype(BF16)
        da_s[rows, :] = da
        edge_grad[rows, :] = nt(da, we_in[0:512, :]).astype(BF16)
        at = pl.ds(n * CHUNK, CHUNK)
        saves += copies.start((edge_grad.at[at], edge_grad_out.at[at]))
    grad_ends = edge_tail(onehot, senders, vb, eb, hidden_s, dz_s, da_s, we_in, g_in, g_out, (o0, o1, o2, o3, o4))
    grad_out[...] = grad + grad_v + grad_ends
    write_grads(own & 1, g_in, g_out, gn_in, gn_out, grad_e_gain, grad_n_gain, keep, send)
    wait(saves)


def backward_kernel(
    own_ref, count_ref, lists, onehot, grad_ref, r0, r1, r2, r3, r4, eb_ref, state_ref, sides_ref, edge_grad_ref, saved_ref, inv_ref,
    we_in_ref, we_out_ref, wn_in_ref, wn_out_ref, e_gain_ref, n_gain_ref,
    grad_out, keep, send, o0, o1, o2, o3, o4,
    eb, state, sides, edge_grad, saved, inv_s, we_in, we_out, wn_in, wn_out, e_gain, n_gain,
    hidden_s, dz_s, da_s, g_in, g_out, gn_in, gn_out, sems,
):
    own, count = own_ref[0], count_ref[0]
    copies = Copies(sems)
    node = copies.start((state_ref.at[pl.ds(1, 3)], state), (sides_ref, sides), (n_gain_ref, n_gain))
    node += copies.start((wn_out_ref.at[0], wn_out), (wn_in_ref.at[0], wn_in))
    edge = copies.start((edge_grad_ref, edge_grad), (saved_ref, saved), (inv_ref, inv_s), (e_gain_ref, e_gain), (we_out_ref.at[0], we_out))
    last = copies.start((eb_ref.at[0], eb), (we_in_ref.at[0], we_in))
    wait(node)
    vb = sides[0:128, :]
    grad = grad_ref[...] + returned(lists, own, (r0, r1, r2, r3, r4))
    n_pre = state[0]
    n_hidden = (n_pre * sigmoid(n_pre)).astype(BF16)
    grad_n_gain, grad_v, grad_agg = node_backward(
        grad, vb, sides[288:416, :], n_pre, n_hidden, state[1], state[2], wn_in, wn_out, n_gain[0:1, :], gn_in, gn_out
    )
    grad_agg = grad_agg.astype(BF16)
    wait(edge)
    gain = e_gain[0:1, :]
    grad_e_gain = jnp.zeros((1, 512), F32)
    for n in range(eb.shape[0] // CHUNK):
        rows = slice(n * CHUNK, (n + 1) * CHUNK)
        gm = tn(onehot[0:128, rows], grad_agg) + edge_grad[rows, :].astype(F32)
        gm = gm * live_rows(n * CHUNK, count)
        normed = saved[1, rows, :].astype(F32)
        grad_e_gain += jnp.sum(gm * normed, axis=0, keepdims=True)
        dz = layer_norm_back(gm, gain, normed, inv_s[rows, 0:1]).astype(BF16)
        dz_s[rows, :] = dz
        pre = saved[0, rows, :].astype(F32)
        s = sigmoid(pre)
        hidden_s[rows, :] = (pre * s).astype(BF16)
        da_s[rows, :] = (nt(dz, we_out[...]) * (s * (1.0 + pre * (1.0 - s)))).astype(BF16)
    wait(last)
    grad_ends = edge_tail(onehot, sides.at[0:288], vb, eb, hidden_s, dz_s, da_s, we_in, g_in, g_out, (o0, o1, o2, o3, o4))
    grad_out[...] = grad + grad_v + grad_ends
    write_grads(own & 1, g_in, g_out, gn_in, gn_out, grad_e_gain, grad_n_gain, keep, send)


def pack_blocks(keep_ref, recv_ref, out_ref, stage, packed, sems):
    gains = (keep_ref[16, 0:16, :].astype(F32) + recv_ref[16, 0:16, :].astype(F32))[0:8, :]
    copies = Copies(sems)
    saves = []
    for c in range(16):
        rows = keep_ref[c].astype(F32) + recv_ref[c].astype(F32)
        for b in range(4):
            stage[b, 0:12, :] = rows[12 * b : 12 * b + 12, :]
            stage[b, 12:16, :] = rows[48 + 4 * b : 52 + 4 * b, :]
            stage[b, 16:24, :] = rows[64 + 8 * b : 72 + 8 * b, :]
            stage[b, 24:28, :] = rows[96 + 4 * b : 100 + 4 * b, :]
            stage[b, 28:32, :] = gains[0:4, :]
            packed[4 * c + b] = stage[b].astype(BF16)
        saves += copies.start((packed.at[pl.ds(4 * c, 4)], out_ref.at[pl.ds(4 * c, 4)]))
    return saves


def pack_kernel(keep_ref, recv_ref, out_ref, stage, packed, sems):
    wait(pack_blocks(keep_ref, recv_ref, out_ref, stage, packed, sems))


def sum_blocks(x):
    def step(n, total):
        return total + x[n].astype(F32)

    return lax.fori_loop(0, 64, step, jnp.zeros((32, 512), F32), unroll=8)


def pick_gains(rows, device):
    picks = lax.broadcasted_iota(jnp.int32, (512, 128), 0) - 4 * device
    select = jnp.where(picks == lax.broadcasted_iota(jnp.int32, (512, 128), 1), 1.0, 0.0).astype(F32)
    return lax.dot_general(rows, select, (((1,), (0,)), ((), ())), precision=lax.Precision.HIGHEST, preferred_element_type=F32)


def sum_kernel(device_ref, x_ref, out_ref, gains_ref, x, sems):
    wait(Copies(sems).start((x_ref, x)))
    out_ref[...] = sum_blocks(x)
    gains_ref[...] = pick_gains(out_ref[24:32, :], device_ref[0])


def node_grad_kernel(own_ref, lists, grad_ref, r0, r1, r2, r3, r4, out_ref, total, sems):
    total[...] = grad_ref[...] + returned(lists, own_ref[0], (r0, r1, r2, r3, r4))
    wait(Copies(sems).start((total, out_ref.at[0])))


def finish_kernel(device_ref, x0_ref, total1, gains1, g_e_in, g_e_out, g_n_in, g_n_out, g_e_gain, g_n_gain, total0):
    total0[...] = sum_blocks(x0_ref)
    for layer, total in ((0, total0), (1, total1)):
        g_e_in[:, layer, :] = total[0:12, :]
        g_e_out[layer] = total[12:16, :]
        g_n_in[layer] = total[16:24, :]
        g_n_out[layer] = total[24:28, :]
        gains = gains1[...] if layer else pick_gains(total[24:32, :], device_ref[0])
        g_e_gain[layer : layer + 1, :] = gains[4:5, 0:4]
        g_n_gain[layer : layer + 1, :] = gains[5:6, 0:4]


def body(
    node_latent,
    edge_latent,
    node_cotangent,
    edge_w_in,
    edge_w_out,
    node_w_in,
    node_w_out,
    edge_gain,
    node_gain,
    edge_slot,
    edge_receiver,
    send_list,
    edge_count,
):
    width = node_latent.shape[2]
    nodes = node_latent.shape[1]
    edges = edge_slot.shape[0]
    graph = lax.axis_size("graph")
    own = lax.axis_index("graph").astype(jnp.int32)
    own_arr = own.reshape(1)
    device = (own * lax.axis_size("batch") + lax.axis_index("batch").astype(jnp.int32)).reshape(1)
    slot = edge_slot.reshape(1, edges)
    receiver = edge_receiver.reshape(1, edges)
    sds = jax.ShapeDtypeStruct
    vmem = pl.BlockSpec(memory_space=pltpu.VMEM)
    smem = pl.BlockSpec(memory_space=pltpu.SMEM)
    free = pl.BlockSpec(memory_space=pl.ANY)
    hbm = pl.BlockSpec(memory_space=pltpu.HBM)
    kept = pl.BlockSpec(memory_space=pltpu.VMEM)

    def exchange(blocks, back):
        sources = [(readers if back else neighbours)(i) for i in range(graph)]
        outs = {}
        for n in ORDER:
            outs[n] = lax.ppermute(blocks[n], "graph", [(sources[i][n], i) for i in range(graph)])
        return [outs[n] for n in range(5)]

    def call(kernel, mib, outs, scratch, specs, args):
        at = {id(hbm): pltpu.HBM, id(kept): pltpu.VMEM}
        real = {id(hbm): free, id(kept): vmem}
        shapes = [at[id(p)](o.shape, o.dtype) if id(p) in at else o for o, p in outs]
        args = [pltpu.with_memory_space_constraint(a, at[id(p)]) if id(p) in at else a for a, p in zip(args, specs)]
        return pl.pallas_call(
            kernel,
            out_shape=shapes,
            in_specs=[real.get(id(p), p) for p in specs],
            out_specs=[real.get(id(p), p) for _, p in outs],
            scratch_shapes=scratch,
            compiler_params=pltpu.CompilerParams(vmem_limit_bytes=mib * 1024 * 1024),
        )(*args)

    def vb16(*shape):
        return pltpu.VMEM(shape, BF16)

    def vf32(*shape):
        return pltpu.VMEM(shape, F32)

    def sems(n):
        return pltpu.SemaphoreType.DMA((n,))

    def ob16(*shape):
        return (sds(shape, BF16), kept)

    def of32(*shape):
        return (sds(shape, F32), kept)

    def swap(send):
        return lax.ppermute(send, "graph", [(i, i ^ 1) for i in range(graph)])

    def spread(packed):
        groups = [[(2 * c + k) * 4 + b for c in range(16) for b in range(4)] for k in range(2)]
        return lax.all_to_all(packed, ("graph", "batch"), 0, 0, tiled=True, axis_index_groups=groups)

    index_s = [pltpu.VMEM((1, edges), jnp.int32)] * 2
    weights = (edge_w_in, edge_w_out, node_w_in, node_w_out)
    weights_s = [vb16(*w.shape[1:]) for w in weights] + [vf32(*edge_gain.shape), vf32(*node_gain.shape)]
    weights_out = [ob16(*w.shape[1:]) for w in weights]
    edge_b, edge_f = vb16(edges, width), vf32(edges, width)
    grads_s = [vb16(r, width) for r in (1536, 512, 1024, 512)]
    blocks_out = [(sds((32, width), BF16), vmem)] * 5
    half = (sds((17, 112, width), BF16), vmem)

    lists, vb0, *first = call(
        gather_kernel, 2, [(sds(send_list.shape, jnp.int32), kept), ob16(nodes, width)] + blocks_out, [sems(2)],
        [smem, hbm, hbm], (own_arr, send_list, node_latent),
    )
    senders0 = exchange(first, False)
    onehot, eb0, we_in0, we_out0, wn_in0, wn_out0, e_gain, n_gain, part0, near0 = call(
        first_kernel,
        4,
        [ob16(512, edges), ob16(edges, width)] + weights_out + [of32(*edge_gain.shape), of32(*node_gain.shape), of32(edges, width), ob16(256, width)],
        index_s + [sems(12)],
        [smem, hbm, hbm, hbm, kept] + [hbm] * 6,
        (own_arr, slot, receiver, edge_latent, vb0, *weights, edge_gain, node_gain),
    )
    weights0 = (we_in0, we_out0, wn_in0, wn_out0, e_gain, n_gain)
    state, sides, eb1, saved, inv, *second = call(
        forward_kernel,
        10,
        [of32(4, nodes, width), ob16(416, width), ob16(edges, width), (sds((2, edges, width), BF16), hbm), (sds((edges, 128), F32), hbm)] + blocks_out,
        [vb16(512, width), edge_b, vb16(2, edges, width), vf32(edges, 128), sems(16)],
        [smem, smem] + [kept] * 12 + [vmem] * 5,
        (own_arr, edge_count, lists, vb0, onehot, eb0, *weights0, part0, near0, *senders0),
    )
    senders1 = exchange(second, False)
    cot, we_in1, we_out1, wn_in1, wn_out1, part1, near1 = call(
        second_kernel,
        4,
        [ob16(nodes, width)] + weights_out + [of32(edges, width), ob16(256, width)],
        [sems(8)],
        [kept, kept] + [hbm] * 5,
        (state, eb1, node_cotangent, *weights),
    )
    node_out, edge_grad, grad1, keep1, send1, *back1 = call(
        middle_kernel,
        20,
        [(sds((1, nodes, width), F32), hbm), (sds((edges, width), BF16), hbm), of32(nodes, width), half, half] + blocks_out,
        [vf32(nodes, width), edge_b, vb16(288, width), vb16(512, width), edge_b, edge_f, edge_f, vf32(edges, 128), edge_b, edge_b, edge_b] + grads_s + [sems(8)],
        [smem, smem] + [kept] * 12 + [vmem] * 5,
        (own_arr, edge_count, state, onehot, eb1, cot, we_in1, we_out1, wn_in1, wn_out1, e_gain, n_gain, part1, near1, *senders1),
    )
    packed_out = (sds((64, 32, width), BF16), hbm)
    pack_s = [vf32(4, 32, width), vb16(64, 32, width), sems(16)]
    returned1 = exchange(back1, True)
    (packed1,) = call(pack_kernel, 5, [packed_out], pack_s, [vmem, vmem], (keep1, swap(send1)))
    x1 = spread(packed1)
    grad0, keep0, send0, *back0 = call(
        backward_kernel,
        22,
        [(sds((nodes, width), F32), vmem), half, half] + blocks_out,
        [edge_b, vf32(3, nodes, width), vb16(416, width), edge_b, vb16(2, edges, width), vf32(edges, 128)] + weights_s + [edge_b, edge_b, edge_b] + grads_s + [sems(12)],
        [smem, smem, kept, kept] + [vmem] * 6 + [hbm, free, free] + [hbm] * 9,
        (own_arr, edge_count, lists, onehot, grad1, *returned1, edge_latent, state, sides, edge_grad, saved, inv, *weights, edge_gain, node_gain),
    )
    returned0 = exchange(back0, True)
    (packed0,) = call(pack_kernel, 5, [packed_out], pack_s, [vmem, vmem], (keep0, swap(send0)))
    x0 = spread(packed0)
    total1, gains1 = call(
        sum_kernel, 4, [of32(32, width), of32(8, 128)], [vb16(64, 32, width), sems(1)], [smem, free], (device, x1)
    )
    (node_grad,) = call(
        node_grad_kernel, 2, [(sds((1, nodes, width), F32), hbm)], [vf32(nodes, width), sems(1)],
        [smem, kept, vmem] + [vmem] * 5, (own_arr, lists, grad0, *returned0),
    )
    g_e_in, *grads = call(
        finish_kernel,
        2,
        [(sds((12, 2, width), F32), vmem)] + [(sds((2, r, width), F32), vmem) for r in (4, 8, 4)] + [(sds((2, 4), F32), vmem)] * 2,
        [vf32(32, width)],
        [smem, vmem, kept, kept],
        (device, x0, total1, gains1),
    )
    return (node_out, node_grad, jnp.swapaxes(g_e_in, 0, 1), *grads)


def solution(mesh):
    in_specs = (
        P("batch", "graph", None),
        P("batch", "graph", None),
        P("batch", "graph", None),
        P(),
        P(),
        P(),
        P(),
        P(),
        P(),
        P("graph"),
        P("graph"),
        P("graph", None),
        P("graph"),
    )
    out_specs = (
        P("batch", "graph", None),
        P("batch", "graph", None),
        P(None, ("graph", "batch"), None),
        P(None, ("graph", "batch"), None),
        P(None, ("graph", "batch"), None),
        P(None, ("graph", "batch"), None),
        P(None, ("graph", "batch")),
        P(None, ("graph", "batch")),
    )
    return jax.shard_map(body, mesh=mesh, in_specs=in_specs, out_specs=out_specs, check_vma=False)
```

time: 146 us -> 143 us (0.979)
  Pallas kernels: 39.5 us -> 37.5 us
    all_to_all x2, waiting for transfers between devices: 14.6 us -> 0.01 us  [spread(): lax.all_to_all(packed, ('graph', 'batch'), 0, 0, tiled=True, axis_index_g...]
    ppermute x20, waiting for transfers between devices: 37.2 us -> 46.8 us  [exchange(): lax.ppermute(blocks[n], 'graph', [(sources[i][n], i) for i in range(graph)])]
    ppermute x2, waiting for transfers between devices: 3.58 us -> 7.87 us  [swap(): return lax.ppermute(send, 'graph', [(i, i ^ 1) for i in range(graph)])]
    ppermute x20, starting transfers between devices: 31.3 us -> 35.2 us  [exchange(): lax.ppermute(blocks[n], 'graph', [(sources[i][n], i) for i in range(graph)])]
    pallas_call x8 -> x11, Pallas kernels: 39.5 us -> 37.5 us  [call(): pl.pallas_call(kernel, out_shape=shapes, in_specs=[real.get(id(p), p) for...]
    ppermute x2, starting transfers between devices: 1.8 us -> 0.17 us  [swap(): return lax.ppermute(send, 'graph', [(i, i ^ 1) for i in range(graph)])]
    all_to_all x2, starting transfers between devices: 15 us -> 13.4 us  [spread(): lax.all_to_all(packed, ('graph', 'batch'), 0, 0, tiled=True, axis_index_g...]
  transfers between devices with their start and end apart: 24 -> 24, of which waited for: 11 -> 8; matrix products, arithmetic and copies ran while one was open for 0% -> 0% of each run, Pallas kernels for 8% -> 13%
where the time goes in v2:
time: 143 us; the launch traced here: 142 us
  waiting for transfers between devices  54.6 us (38%)
  starting transfers between devices  48.8 us (34%)
  Pallas kernels  37.5 us (26%)
  between operations  1.53 us (1%)
    ppermute x20, waiting for transfers between devices, exchange(): lax.ppermute(blocks[n], 'graph', [(sources[i][n], i) for i in range(graph)])  46.8 us
    pallas_call x11, Pallas kernels, call(): pl.pallas_call(kernel, out_shape=shapes, in_specs=[real.get(id(p), p) for...  37.5 us
    ppermute x20, starting transfers between devices, exchange(): lax.ppermute(blocks[n], 'graph', [(sources[i][n], i) for i in range(graph)])  35.2 us
    all_to_all x2, starting transfers between devices, spread(): lax.all_to_all(packed, ('graph', 'batch'), 0, 0, tiled=True, axis_index_g...  13.4 us
    ppermute x2, waiting for transfers between devices, swap(): return lax.ppermute(send, 'graph', [(i, i ^ 1) for i in range(graph)])  7.87 us
  transfers between devices with their start and end apart: 24, of which 8 were waited for; matrix products, arithmetic and copies ran while one was open for 0% of the time, Pallas kernels for 13%

profile of v2, /device:TPU:0, one launch (start us, length us, event | category | flops | bytes accessed | tf_op | source)
XLA Modules:
  0.0 142.5 jit_solution(777458660387511568)
XLA Ops:
  0.6 1.2 shard_map.188
  1.9 6.4 %collective-permute-start.1 = (bf16[32,512]{1,0:T(8,128)(2,1)S(1)}, bf16[32,512]{1,0:T(8,128)(2,1)S(1)}, u32[]{:S(2)}, u32[]{:S(2)}) collective-permute-start(bf16[32,512]{1,0:T(8,128)(2,1)S(1)} %get-tuple-element.81), channel_id=1, source_target_pairs={{124,0},{8,4},{4,8},{16,12},{12,16},{24,20},{20,24},{32,28},{28,32... | collective-permute-start | bytes 98312 | tf_op jit(solution)/shard_map/ppermute | solution.py:451
  8.4 5.3 %collective-permute-start.3 = (bf16[32,512]{1,0:T(8,128)(2,1)S(1)}, bf16[32,512]{1,0:T(8,128)(2,1)S(1)}, u32[]{:S(2)}, u32[]{:S(2)}) collective-permute-start(bf16[32,512]{1,0:T(8,128)(2,1)S(1)} %get-tuple-element.83), channel_id=1, source_target_pairs={{8,0},{12,4},{16,8},{20,12},{24,16},{28,20},{32,24},{36,28},{40,32... | collective-permute-start | bytes 98312 | tf_op jit(solution)/shard_map/ppermute | solution.py:451
  14.4 3.2 %shard_map.189 = (bf16[512,1024]{1,0:T(8,128)(2,1)S(1)}, bf16[1024,512]{1,0:T(8,128)(2,1)S(1)}, bf16[1536,512]{1,0:T(8,128)(2,1)S(1)}, bf16[512,512]{1,0:T(8,128...) custom-call(s32[1]{0:T(128)} %bitcast.own_ref, ...), custom_call_target="tpu_custom_call" | custom-call | tf_op jit(solution)/shard_map/pallas_call | solution.py:459
  17.6 1.5 %collective-permute-done.4.b4 = bf16[32,512]{1,0:T(8,128)(2,1)S(1)} collective-permute-done((bf16[32,512]{1,0:T(8,128)(2,1)S(1)}, bf16[32,512]{1,0:T(8,128)(2,1)S(1)}, u32[]{:S(2)}, u32[]{:S(2)}) %collective-permute-start.4) | collective-permute-done | bytes 32800 | tf_op jit(solution)/shard_map/ppermute | solution.py:451
  19.2 4.1 %shard_map.190 = (f32[4,128,512]{2,1,0:T(8,128)S(1)}, bf16[416,512]{1,0:T(8,128)(2,1)S(1)}, bf16[1024,512]{1,0:T(8,128)(2,1)S(1)}, bf16[2,1024,512]{2,1,0:T(8,12...) custom-call(s32[1]{0:T(128)} %bitcast.own_ref, ...), custom_call_target="tpu_custom_call" | custom-call | tf_op jit(solution)/shard_map/pallas_call | solution.py:459
  23.4 1.9 %collective-permute-start.6 = (bf16[32,512]{1,0:T(8,128)(2,1)S(1)}, bf16[32,512]{1,0:T(8,128)(2,1)S(1)}, u32[]{:S(2)}, u32[]{:S(2)}) collective-permute-start(bf16[32,512]{1,0:T(8,128)(2,1)S(1)} %get-tuple-element.95), channel_id=1, source_target_pairs={{124,0},{8,4},{4,8},{16,12},{12,16},{24,20},{20,24},{32,28},{28,32... | collective-permute-start | bytes 98312 | tf_op jit(solution)/shard_map/ppermute | solution.py:451
  25.5 5.1 %collective-permute-start.8 = (bf16[32,512]{1,0:T(8,128)(2,1)S(1)}, bf16[32,512]{1,0:T(8,128)(2,1)S(1)}, u32[]{:S(2)}, u32[]{:S(2)}) collective-permute-start(bf16[32,512]{1,0:T(8,128)(2,1)S(1)} %get-tuple-element.97), channel_id=1, source_target_pairs={{8,0},{12,4},{16,8},{20,12},{24,16},{28,20},{32,24},{36,28},{40,32... | collective-permute-start | bytes 98312 | tf_op jit(solution)/shard_map/ppermute | solution.py:451
  30.7 2.3 %shard_map.191 = (bf16[128,512]{1,0:T(8,128)(2,1)S(1)}, bf16[1536,512]{1,0:T(8,128)(2,1)S(1)}, bf16[512,512]{1,0:T(8,128)(2,1)S(1)}, bf16[1024,512]{1,0:T(8,128)...) custom-call(f32[4,128,512]{2,1,0:T(8,128)S(1)} %get-tuple-element.85.state.state_ref,, ...), custom_call_target="tpu_custom_call" | custom-call | tf_op jit(solution)/shard_map/pallas_call | solution.py:459
  33.0 3.0 %collective-permute-done.9.b4 = bf16[32,512]{1,0:T(8,128)(2,1)S(1)} collective-permute-done((bf16[32,512]{1,0:T(8,128)(2,1)S(1)}, bf16[32,512]{1,0:T(8,128)(2,1)S(1)}, u32[]{:S(2)}, u32[]{:S(2)}) %collective-permute-start.9) | collective-permute-done | bytes 32800 | tf_op jit(solution)/shard_map/ppermute | solution.py:451
  36.1 10.4 %shard_map.192 = (f32[1,128,512]{2,1,0:T(8,128)}, bf16[1024,512]{1,0:T(8,128)(2,1)}, f32[128,512]{1,0:T(8,128)S(1)}, bf16[17,112,512]{2,1,0:T(8,128)(2,1)S(1)}, ...) custom-call(s32[1]{0:T(128)} %bitcast.own_ref, ...), custom_call_target="tpu_custom_call" | custom-call | tf_op jit(solution)/shard_map/pallas_call | solution.py:459
  46.6 3.9 %collective-permute-done.21.recv_ref = bf16[17,112,512]{2,1,0:T(8,128)(2,1)S(1)} collective-permute-done((bf16[17,112,512]{2,1,0:T(8,128)(2,1)S(1)}, bf16[17,112,512]{2,1,0:T(8,128)(2,1)S(1)}, u32[]{:S(2)}, u32[]{:S(2)}) %collective-permute-start.21) | collective-permute-done | bytes 1949728 | tf_op jit(solution)/shard_map/ppermute | solution.py:484
  50.5 1.6 %shard_map.196 = bf16[64,32,512]{2,1,0:T(8,128)(2,1)} custom-call(bf16[17,112,512]{2,1,0:T(8,128)(2,1)S(1)} %get-tuple-element.118.keep_ref, bf16[17,112,512]{2,1,0:T(8,128)(2,1)S(1)} %collective-permute-done.21.recv_ref), custom_call_target="tpu_custom_call" | custom-call | tf_op jit(solution)/shard_map/pallas_call | solution.py:459
  52.2 7.0 %all-to-all-start.1 = ((bf16[64,32,512]{2,1,0:T(8,128)(2,1)}), bf16[64,32,512]{2,1,0:T(8,128)(2,1)}, u32[]{:S(2)}, u32[]{:S(2)}) async-start(bf16[64,32,512]{2,1,0:T(8,128)(2,1)} %shard_map.196), calls=%async_computation.1 | async-start | bytes 4194304 | tf_op jit(solution)/shard_map/all_to_all | solution.py:488
  59.3 5.2 %collective-permute-start.11 = (bf16[32,512]{1,0:T(8,128)(2,1)S(1)}, bf16[32,512]{1,0:T(8,128)(2,1)S(1)}, u32[]{:S(2)}, u32[]{:S(2)}) collective-permute-start(bf16[32,512]{1,0:T(8,128)(2,1)S(1)} %get-tuple-element.102), channel_id=1, source_target_pairs={{124,0},{8,4},{4,8},{16,12},{12,16},{24,20},{20,24},{32,28},{28,32... | collective-permute-start | bytes 98312 | tf_op jit(solution)/shard_map/ppermute | solution.py:451
  64.5 0.8 collective-permute-start.12
  65.3 1.2 collective-permute-start.13
  66.5 0.6 collective-permute-start.14
  67.2 17.9 %collective-permute-done.11.r1 = bf16[32,512]{1,0:T(8,128)(2,1)S(1)} collective-permute-done((bf16[32,512]{1,0:T(8,128)(2,1)S(1)}, bf16[32,512]{1,0:T(8,128)(2,1)S(1)}, u32[]{:S(2)}, u32[]{:S(2)}) %collective-permute-start.11) | collective-permute-done | bytes 32800 | tf_op jit(solution)/shard_map/ppermute | solution.py:451
  85.1 3.1 %collective-permute-done.13.r3 = bf16[32,512]{1,0:T(8,128)(2,1)S(1)} collective-permute-done((bf16[32,512]{1,0:T(8,128)(2,1)S(1)}, bf16[32,512]{1,0:T(8,128)(2,1)S(1)}, u32[]{:S(2)}, u32[]{:S(2)}) %collective-permute-start.13) | collective-permute-done | bytes 32800 | tf_op jit(solution)/shard_map/ppermute | solution.py:451
  88.2 8.7 %shard_map.193 = (f32[128,512]{1,0:T(8,128)S(1)}, bf16[17,112,512]{2,1,0:T(8,128)(2,1)S(1)}, bf16[17,112,512]{2,1,0:T(8,128)(2,1)S(1)}, bf16[32,512]{1,0:T(8,128...) custom-call(s32[1]{0:T(128)} %bitcast.own_ref, ...), custom_call_target="tpu_custom_call" | custom-call | tf_op jit(solution)/shard_map/pallas_call | solution.py:459
  97.0 3.9 %collective-permute-done.20.recv_ref = bf16[17,112,512]{2,1,0:T(8,128)(2,1)S(1)} collective-permute-done((bf16[17,112,512]{2,1,0:T(8,128)(2,1)S(1)}, bf16[17,112,512]{2,1,0:T(8,128)(2,1)S(1)}, u32[]{:S(2)}, u32[]{:S(2)}) %collective-permute-start.20) | collective-permute-done | bytes 1949728 | tf_op jit(solution)/shard_map/ppermute | solution.py:484
  100.9 1.6 %shard_map.195 = bf16[64,32,512]{2,1,0:T(8,128)(2,1)} custom-call(bf16[17,112,512]{2,1,0:T(8,128)(2,1)S(1)} %get-tuple-element.116.keep_ref, bf16[17,112,512]{2,1,0:T(8,128)(2,1)S(1)} %collective-permute-done.20.recv_ref), custom_call_target="tpu_custom_call" | custom-call | tf_op jit(solution)/shard_map/pallas_call | solution.py:459
  102.6 6.3 %all-to-all-start = ((bf16[64,32,512]{2,1,0:T(8,128)(2,1)}), bf16[64,32,512]{2,1,0:T(8,128)(2,1)S(1)}, u32[]{:S(2)}, u32[]{:S(2)}) async-start(bf16[64,32,512]{2,1,0:T(8,128)(2,1)} %shard_map.195), calls=%async_computation | async-start | bytes 4194304 | tf_op jit(solution)/shard_map/all_to_all | solution.py:488
  109.0 5.3 %collective-permute-start.16 = (bf16[32,512]{1,0:T(8,128)(2,1)S(1)}, bf16[32,512]{1,0:T(8,128)(2,1)S(1)}, u32[]{:S(2)}, u32[]{:S(2)}) collective-permute-start(bf16[32,512]{1,0:T(8,128)(2,1)S(1)} %get-tuple-element.112), channel_id=1, source_target_pairs={{124,0},{8,4},{4,8},{16,12},{12,16},{24,20},{20,24},{32,28},{28,32... | collective-permute-start | bytes 98312 | tf_op jit(solution)/shard_map/ppermute | solution.py:451
  114.3 0.8 collective-permute-start.17
  115.1 1.2 collective-permute-start.18
  117.0 18.1 %collective-permute-done.16.r1 = bf16[32,512]{1,0:T(8,128)(2,1)S(1)} collective-permute-done((bf16[32,512]{1,0:T(8,128)(2,1)S(1)}, bf16[32,512]{1,0:T(8,128)(2,1)S(1)}, u32[]{:S(2)}, u32[]{:S(2)}) %collective-permute-start.16) | collective-permute-done | bytes 32800 | tf_op jit(solution)/shard_map/ppermute | solution.py:451
  135.1 3.1 %collective-permute-done.18.r3 = bf16[32,512]{1,0:T(8,128)(2,1)S(1)} collective-permute-done((bf16[32,512]{1,0:T(8,128)(2,1)S(1)}, bf16[32,512]{1,0:T(8,128)(2,1)S(1)}, u32[]{:S(2)}, u32[]{:S(2)}) %collective-permute-start.18) | collective-permute-done | bytes 32800 | tf_op jit(solution)/shard_map/ppermute | solution.py:451
  138.2 1.0 shard_map.194
  139.2 2.1 %shard_map.197 = (f32[32,512]{1,0:T(8,128)S(1)}, f32[8,128]{1,0:T(8,128)S(1)}) custom-call(s32[1]{0:T(128)} %bitcast.3.device_ref, bf16[64,32,512]{2,1,0:T(8,128)(2,1)} %all-to-all-done.1.x_ref), custom_call_target="tpu_custom_call" | custom-call | tf_op jit(solution)/shard_map/pallas_call | solution.py:459
  141.3 1.1 shard_map.198
  (27 shorter events, 1.4 us)
Async XLA Ops:
  1.8 15.7 %collective-permute-start = (bf16[32,512]{1,0:T(8,128)(2,1)S(1)}, bf16[32,512]{1,0:T(8,128)(2,1)S(1)}, u32[]{:S(2)}, u32[]{:S(2)}) collective-permute-start(bf16[32,512]{1,0:T(8,128)(2,1)S(1)} %get-tuple-element.80), channel_id=1, source_target_pairs={{4,0},{0,4},{12,8},{8,12},{20,16},{16,20},{28,24},{24,28},{36,32},... | collective-permute-start | bytes 98312 | tf_op jit(solution)/shard_map/ppermute | solution.py:451
  1.9 15.7 %collective-permute-start.1 = (bf16[32,512]{1,0:T(8,128)(2,1)S(1)}, bf16[32,512]{1,0:T(8,128)(2,1)S(1)}, u32[]{:S(2)}, u32[]{:S(2)}) collective-permute-start(bf16[32,512]{1,0:T(8,128)(2,1)S(1)} %get-tuple-element.81), channel_id=1, source_target_pairs={{124,0},{8,4},{4,8},{16,12},{12,16},{24,20},{20,24},{32,28},{28,32... | collective-permute-start | bytes 98312 | tf_op jit(solution)/shard_map/ppermute | solution.py:451
  8.4 9.2 %collective-permute-start.2 = (bf16[32,512]{1,0:T(8,128)(2,1)S(1)}, bf16[32,512]{1,0:T(8,128)(2,1)S(1)}, u32[]{:S(2)}, u32[]{:S(2)}) collective-permute-start(bf16[32,512]{1,0:T(8,128)(2,1)S(1)} %get-tuple-element.82), channel_id=1, source_target_pairs={{120,0},{124,4},{0,8},{4,12},{8,16},{12,20},{16,24},{20,28},{24,32... | collective-permute-start | bytes 98312 | tf_op jit(solution)/shard_map/ppermute | solution.py:451
  8.4 9.2 %collective-permute-start.3 = (bf16[32,512]{1,0:T(8,128)(2,1)S(1)}, bf16[32,512]{1,0:T(8,128)(2,1)S(1)}, u32[]{:S(2)}, u32[]{:S(2)}) collective-permute-start(bf16[32,512]{1,0:T(8,128)(2,1)S(1)} %get-tuple-element.83), channel_id=1, source_target_pairs={{8,0},{12,4},{16,8},{20,12},{24,16},{28,20},{32,24},{36,28},{40,32... | collective-permute-start | bytes 98312 | tf_op jit(solution)/shard_map/ppermute | solution.py:451
  13.7 5.4 %collective-permute-start.4 = (bf16[32,512]{1,0:T(8,128)(2,1)S(1)}, bf16[32,512]{1,0:T(8,128)(2,1)S(1)}, u32[]{:S(2)}, u32[]{:S(2)}) collective-permute-start(bf16[32,512]{1,0:T(8,128)(2,1)S(1)} %get-tuple-element.84), channel_id=1, source_target_pairs={{64,0},{68,4},{72,8},{76,12},{80,16},{84,20},{88,24},{92,28},{96,3... | collective-permute-start | bytes 98312 | tf_op jit(solution)/shard_map/ppermute | solution.py:451
  23.3 9.7 %collective-permute-start.5 = (bf16[32,512]{1,0:T(8,128)(2,1)S(1)}, bf16[32,512]{1,0:T(8,128)(2,1)S(1)}, u32[]{:S(2)}, u32[]{:S(2)}) collective-permute-start(bf16[32,512]{1,0:T(8,128)(2,1)S(1)} %get-tuple-element.94), channel_id=1, source_target_pairs={{4,0},{0,4},{12,8},{8,12},{20,16},{16,20},{28,24},{24,28},{36,32},... | collective-permute-start | bytes 98312 | tf_op jit(solution)/shard_map/ppermute | solution.py:451
  23.4 9.6 %collective-permute-start.6 = (bf16[32,512]{1,0:T(8,128)(2,1)S(1)}, bf16[32,512]{1,0:T(8,128)(2,1)S(1)}, u32[]{:S(2)}, u32[]{:S(2)}) collective-permute-start(bf16[32,512]{1,0:T(8,128)(2,1)S(1)} %get-tuple-element.95), channel_id=1, source_target_pairs={{124,0},{8,4},{4,8},{16,12},{12,16},{24,20},{20,24},{32,28},{28,32... | collective-permute-start | bytes 98312 | tf_op jit(solution)/shard_map/ppermute | solution.py:451
  25.3 7.7 %collective-permute-start.7 = (bf16[32,512]{1,0:T(8,128)(2,1)S(1)}, bf16[32,512]{1,0:T(8,128)(2,1)S(1)}, u32[]{:S(2)}, u32[]{:S(2)}) collective-permute-start(bf16[32,512]{1,0:T(8,128)(2,1)S(1)} %get-tuple-element.96), channel_id=1, source_target_pairs={{120,0},{124,4},{0,8},{4,12},{8,16},{12,20},{16,24},{20,28},{24,32... | collective-permute-start | bytes 98312 | tf_op jit(solution)/shard_map/ppermute | solution.py:451
  25.5 7.5 %collective-permute-start.8 = (bf16[32,512]{1,0:T(8,128)(2,1)S(1)}, bf16[32,512]{1,0:T(8,128)(2,1)S(1)}, u32[]{:S(2)}, u32[]{:S(2)}) collective-permute-start(bf16[32,512]{1,0:T(8,128)(2,1)S(1)} %get-tuple-element.97), channel_id=1, source_target_pairs={{8,0},{12,4},{16,8},{20,12},{24,16},{28,20},{32,24},{36,28},{40,32... | collective-permute-start | bytes 98312 | tf_op jit(solution)/shard_map/ppermute | solution.py:451
  30.6 5.4 %collective-permute-start.9 = (bf16[32,512]{1,0:T(8,128)(2,1)S(1)}, bf16[32,512]{1,0:T(8,128)(2,1)S(1)}, u32[]{:S(2)}, u32[]{:S(2)}) collective-permute-start(bf16[32,512]{1,0:T(8,128)(2,1)S(1)} %get-tuple-element.98), channel_id=1, source_target_pairs={{64,0},{68,4},{72,8},{76,12},{80,16},{84,20},{88,24},{92,28},{96,3... | collective-permute-start | bytes 98312 | tf_op jit(solution)/shard_map/ppermute | solution.py:451
  46.5 4.0 %collective-permute-start.21 = (bf16[17,112,512]{2,1,0:T(8,128)(2,1)S(1)}, bf16[17,112,512]{2,1,0:T(8,128)(2,1)S(1)}, u32[]{:S(2)}, u32[]{:S(2)}) collective-permute-start(bf16[17,112,512]{2,1,0:T(8,128)(2,1)S(1)} %get-tuple-element.119), channel_id=1, source_target_pairs={{0,4},{4,0},{8,12},{12,8},{16,20},{20,16},{24,28},{28,24},{32,36},... | collective-permute-start | bytes 5849096 | tf_op jit(solution)/shard_map/ppermute | solution.py:484
  52.2 50.4 %all-to-all-start.1 = ((bf16[64,32,512]{2,1,0:T(8,128)(2,1)}), bf16[64,32,512]{2,1,0:T(8,128)(2,1)}, u32[]{:S(2)}, u32[]{:S(2)}) async-start(bf16[64,32,512]{2,1,0:T(8,128)(2,1)} %shard_map.196), calls=%async_computation.1 | async-start | bytes 4194304 | tf_op jit(solution)/shard_map/all_to_all | solution.py:488
  59.2 8.0 %collective-permute-start.10 = (bf16[32,512]{1,0:T(8,128)(2,1)S(1)}, bf16[32,512]{1,0:T(8,128)(2,1)S(1)}, u32[]{:S(2)}, u32[]{:S(2)}) collective-permute-start(bf16[32,512]{1,0:T(8,128)(2,1)S(1)} %get-tuple-element.101), channel_id=1, source_target_pairs={{4,0},{0,4},{12,8},{8,12},{20,16},{16,20},{28,24},{24,28},{36,32},... | collective-permute-start | bytes 98312 | tf_op jit(solution)/shard_map/ppermute | solution.py:451
  59.3 25.8 %collective-permute-start.11 = (bf16[32,512]{1,0:T(8,128)(2,1)S(1)}, bf16[32,512]{1,0:T(8,128)(2,1)S(1)}, u32[]{:S(2)}, u32[]{:S(2)}) collective-permute-start(bf16[32,512]{1,0:T(8,128)(2,1)S(1)} %get-tuple-element.102), channel_id=1, source_target_pairs={{124,0},{8,4},{4,8},{16,12},{12,16},{24,20},{20,24},{32,28},{28,32... | collective-permute-start | bytes 98312 | tf_op jit(solution)/shard_map/ppermute | solution.py:451
  64.5 20.6 %collective-permute-start.12 = (bf16[32,512]{1,0:T(8,128)(2,1)S(1)}, bf16[32,512]{1,0:T(8,128)(2,1)S(1)}, u32[]{:S(2)}, u32[]{:S(2)}) collective-permute-start(bf16[32,512]{1,0:T(8,128)(2,1)S(1)} %get-tuple-element.103), channel_id=1, source_target_pairs={{8,0},{12,4},{16,8},{20,12},{24,16},{28,20},{32,24},{36,28},{40,32... | collective-permute-start | bytes 98312 | tf_op jit(solution)/shard_map/ppermute | solution.py:451
  65.3 22.8 %collective-permute-start.13 = (bf16[32,512]{1,0:T(8,128)(2,1)S(1)}, bf16[32,512]{1,0:T(8,128)(2,1)S(1)}, u32[]{:S(2)}, u32[]{:S(2)}) collective-permute-start(bf16[32,512]{1,0:T(8,128)(2,1)S(1)} %get-tuple-element.104), channel_id=1, source_target_pairs={{120,0},{124,4},{0,8},{4,12},{8,16},{12,20},{16,24},{20,28},{24,32... | collective-permute-start | bytes 98312 | tf_op jit(solution)/shard_map/ppermute | solution.py:451
  66.5 21.6 %collective-permute-start.14 = (bf16[32,512]{1,0:T(8,128)(2,1)S(1)}, bf16[32,512]{1,0:T(8,128)(2,1)S(1)}, u32[]{:S(2)}, u32[]{:S(2)}) collective-permute-start(bf16[32,512]{1,0:T(8,128)(2,1)S(1)} %get-tuple-element.105), channel_id=1, source_target_pairs={{64,0},{68,4},{72,8},{76,12},{80,16},{84,20},{88,24},{92,28},{96,3... | collective-permute-start | bytes 98312 | tf_op jit(solution)/shard_map/ppermute | solution.py:451
  96.9 4.0 %collective-permute-start.20 = (bf16[17,112,512]{2,1,0:T(8,128)(2,1)S(1)}, bf16[17,112,512]{2,1,0:T(8,128)(2,1)S(1)}, u32[]{:S(2)}, u32[]{:S(2)}) collective-permute-start(bf16[17,112,512]{2,1,0:T(8,128)(2,1)S(1)} %get-tuple-element.117), channel_id=1, source_target_pairs={{0,4},{4,0},{8,12},{12,8},{16,20},{20,16},{24,28},{28,24},{32,36},... | collective-permute-start | bytes 5849096 | tf_op jit(solution)/shard_map/ppermute | solution.py:484
  102.6 38.8 %all-to-all-start = ((bf16[64,32,512]{2,1,0:T(8,128)(2,1)}), bf16[64,32,512]{2,1,0:T(8,128)(2,1)S(1)}, u32[]{:S(2)}, u32[]{:S(2)}) async-start(bf16[64,32,512]{2,1,0:T(8,128)(2,1)} %shard_map.195), calls=%async_computation | async-start | bytes 4194304 | tf_op jit(solution)/shard_map/all_to_all | solution.py:488
  108.9 8.0 %collective-permute-start.15 = (bf16[32,512]{1,0:T(8,128)(2,1)S(1)}, bf16[32,512]{1,0:T(8,128)(2,1)S(1)}, u32[]{:S(2)}, u32[]{:S(2)}) collective-permute-start(bf16[32,512]{1,0:T(8,128)(2,1)S(1)} %get-tuple-element.111), channel_id=1, source_target_pairs={{4,0},{0,4},{12,8},{8,12},{20,16},{16,20},{28,24},{24,28},{36,32},... | collective-permute-start | bytes 98312 | tf_op jit(solution)/shard_map/ppermute | solution.py:451
  109.0 26.1 %collective-permute-start.16 = (bf16[32,512]{1,0:T(8,128)(2,1)S(1)}, bf16[32,512]{1,0:T(8,128)(2,1)S(1)}, u32[]{:S(2)}, u32[]{:S(2)}) collective-permute-start(bf16[32,512]{1,0:T(8,128)(2,1)S(1)} %get-tuple-element.112), channel_id=1, source_target_pairs={{124,0},{8,4},{4,8},{16,12},{12,16},{24,20},{20,24},{32,28},{28,32... | collective-permute-start | bytes 98312 | tf_op jit(solution)/shard_map/ppermute | solution.py:451
  114.3 20.8 %collective-permute-start.17 = (bf16[32,512]{1,0:T(8,128)(2,1)S(1)}, bf16[32,512]{1,0:T(8,128)(2,1)S(1)}, u32[]{:S(2)}, u32[]{:S(2)}) collective-permute-start(bf16[32,512]{1,0:T(8,128)(2,1)S(1)} %get-tuple-element.113), channel_id=1, source_target_pairs={{8,0},{12,4},{16,8},{20,12},{24,16},{28,20},{32,24},{36,28},{40,32... | collective-permute-start | bytes 98312 | tf_op jit(solution)/shard_map/ppermute | solution.py:451
  115.1 23.0 %collective-permute-start.18 = (bf16[32,512]{1,0:T(8,128)(2,1)S(1)}, bf16[32,512]{1,0:T(8,128)(2,1)S(1)}, u32[]{:S(2)}, u32[]{:S(2)}) collective-permute-start(bf16[32,512]{1,0:T(8,128)(2,1)S(1)} %get-tuple-element.114), channel_id=1, source_target_pairs={{120,0},{124,4},{0,8},{4,12},{8,16},{12,20},{16,24},{20,28},{24,32... | collective-permute-start | bytes 98312 | tf_op jit(solution)/shard_map/ppermute | solution.py:451
  116.3 21.8 %collective-permute-start.19 = (bf16[32,512]{1,0:T(8,128)(2,1)S(1)}, bf16[32,512]{1,0:T(8,128)(2,1)S(1)}, u32[]{:S(2)}, u32[]{:S(2)}) collective-permute-start(bf16[32,512]{1,0:T(8,128)(2,1)S(1)} %get-tuple-element.115), channel_id=1, source_target_pairs={{64,0},{68,4},{72,8},{76,12},{80,16},{84,20},{88,24},{92,28},{96,3... | collective-permute-start | bytes 98312 | tf_op jit(solution)/shard_map/ppermute | solution.py:451

commit v3 on v2

--- a/solution.py
+++ b/solution.py
@@ -7,7 +7,7 @@
 
 
 EPSILON = 1e-05
-CHUNK = 256
+CHUNK = 512
 ORDER = (4, 2, 3, 1, 0)
 F32 = jnp.float32
 BF16 = jnp.bfloat16
@@ -356,44 +356,46 @@
     write_grads(own & 1, g_in, g_out, gn_in, gn_out, grad_e_gain, grad_n_gain, keep, send)
 
 
-def pack_blocks(keep_ref, recv_ref, out_ref, stage, packed, sems):
-    gains = (keep_ref[16, 0:16, :].astype(F32) + recv_ref[16, 0:16, :].astype(F32))[0:8, :]
+def pack_kernel(keep_ref, recv_ref, out_ref, stage, packed, sems):
+    gains = keep_ref[16, 0:16, :].astype(F32) + recv_ref[16, 0:16, :].astype(F32)
+    for b in range(4):
+        for q in range(4):
+            stage[b, 112 + q : 113 + q, :] = gains[0:1, 128 * q : 128 * q + 128]
+            stage[b, 116 + q : 117 + q, :] = gains[1:2, 128 * q : 128 * q + 128]
     copies = Copies(sems)
     saves = []
     for c in range(16):
         rows = keep_ref[c].astype(F32) + recv_ref[c].astype(F32)
         for b in range(4):
-            stage[b, 0:12, :] = rows[12 * b : 12 * b + 12, :]
-            stage[b, 12:16, :] = rows[48 + 4 * b : 52 + 4 * b, :]
-            stage[b, 16:24, :] = rows[64 + 8 * b : 72 + 8 * b, :]
-            stage[b, 24:28, :] = rows[96 + 4 * b : 100 + 4 * b, :]
-            stage[b, 28:32, :] = gains[0:4, :]
+            for q in range(4):
+                lanes = slice(128 * q, 128 * q + 128)
+                at = 28 * q
+                stage[b, at : at + 12, :] = rows[12 * b : 12 * b + 12, lanes]
+                stage[b, at + 12 : at + 16, :] = rows[48 + 4 * b : 52 + 4 * b, lanes]
+                stage[b, at + 16 : at + 24, :] = rows[64 + 8 * b : 72 + 8 * b, lanes]
+                stage[b, at + 24 : at + 28, :] = rows[96 + 4 * b : 100 + 4 * b, lanes]
             packed[4 * c + b] = stage[b].astype(BF16)
         saves += copies.start((packed.at[pl.ds(4 * c, 4)], out_ref.at[pl.ds(4 * c, 4)]))
-    return saves
-
-
-def pack_kernel(keep_ref, recv_ref, out_ref, stage, packed, sems):
-    wait(pack_blocks(keep_ref, recv_ref, out_ref, stage, packed, sems))
+    wait(saves)
 
 
 def sum_blocks(x):
     def step(n, total):
         return total + x[n].astype(F32)
 
-    return lax.fori_loop(0, 64, step, jnp.zeros((32, 512), F32), unroll=8)
+    return lax.fori_loop(0, 64, step, jnp.zeros((120, 128), F32), unroll=8)
 
 
 def pick_gains(rows, device):
-    picks = lax.broadcasted_iota(jnp.int32, (512, 128), 0) - 4 * device
-    select = jnp.where(picks == lax.broadcasted_iota(jnp.int32, (512, 128), 1), 1.0, 0.0).astype(F32)
+    picks = lax.broadcasted_iota(jnp.int32, (128, 128), 0) - 4 * (device & 31)
+    select = jnp.where(picks == lax.broadcasted_iota(jnp.int32, (128, 128), 1), 1.0, 0.0).astype(F32)
     return lax.dot_general(rows, select, (((1,), (0,)), ((), ())), precision=lax.Precision.HIGHEST, preferred_element_type=F32)
 
 
 def sum_kernel(device_ref, x_ref, out_ref, gains_ref, x, sems):
     wait(Copies(sems).start((x_ref, x)))
     out_ref[...] = sum_blocks(x)
-    gains_ref[...] = pick_gains(out_ref[24:32, :], device_ref[0])
+    gains_ref[...] = pick_gains(out_ref[112:120, :], device_ref[0])
 
 
 def node_grad_kernel(own_ref, lists, grad_ref, r0, r1, r2, r3, r4, out_ref, total, sems):
@@ -403,14 +405,19 @@
 
 def finish_kernel(device_ref, x0_ref, total1, gains1, g_e_in, g_e_out, g_n_in, g_n_out, g_e_gain, g_n_gain, total0):
     total0[...] = sum_blocks(x0_ref)
+    device = device_ref[0]
+    row = lax.broadcasted_iota(jnp.int32, (8, 128), 0) - device // 32
     for layer, total in ((0, total0), (1, total1)):
-        g_e_in[:, layer, :] = total[0:12, :]
-        g_e_out[layer] = total[12:16, :]
-        g_n_in[layer] = total[16:24, :]
-        g_n_out[layer] = total[24:28, :]
-        gains = gains1[...] if layer else pick_gains(total[24:32, :], device_ref[0])
-        g_e_gain[layer : layer + 1, :] = gains[4:5, 0:4]
-        g_n_gain[layer : layer + 1, :] = gains[5:6, 0:4]
+        for q in range(4):
+            lanes = slice(128 * q, 128 * q + 128)
+            at = 28 * q
+            g_e_in[:, layer, lanes] = total[at : at + 12, :]
+            g_e_out[layer, :, lanes] = total[at + 12 : at + 16, :]
+            g_n_in[layer, :, lanes] = total[at + 16 : at + 24, :]
+            g_n_out[layer, :, lanes] = total[at + 24 : at + 28, :]
+        gains = gains1[...] if layer else pick_gains(total[112:120, :], device)
+        g_e_gain[layer : layer + 1, :] = jnp.sum(jnp.where(row == 0, gains, 0.0), axis=0, keepdims=True)[:, 0:4]
+        g_n_gain[layer : layer + 1, :] = jnp.sum(jnp.where(row == 4, gains, 0.0), axis=0, keepdims=True)[:, 0:4]
 
 
 def body(
@@ -535,8 +542,8 @@
         [smem, smem] + [kept] * 12 + [vmem] * 5,
         (own_arr, edge_count, state, onehot, eb1, cot, we_in1, we_out1, wn_in1, wn_out1, e_gain, n_gain, part1, near1, *senders1),
     )
-    packed_out = (sds((64, 32, width), BF16), hbm)
-    pack_s = [vf32(4, 32, width), vb16(64, 32, width), sems(16)]
+    packed_out = (sds((64, 120, 128), BF16), hbm)
+    pack_s = [vf32(4, 120, 128), vb16(64, 120, 128), sems(16)]
     returned1 = exchange(back1, True)
     (packed1,) = call(pack_kernel, 5, [packed_out], pack_s, [vmem, vmem], (keep1, swap(send1)))
     x1 = spread(packed1)
@@ -552,7 +559,7 @@
     (packed0,) = call(pack_kernel, 5, [packed_out], pack_s, [vmem, vmem], (keep0, swap(send0)))
     x0 = spread(packed0)
     total1, gains1 = call(
-        sum_kernel, 4, [of32(32, width), of32(8, 128)], [vb16(64, 32, width), sems(1)], [smem, free], (device, x1)
+        sum_kernel, 4, [of32(120, 128), of32(8, 128)], [vb16(64, 120, 128), sems(1)], [smem, free], (device, x1)
     )
     (node_grad,) = call(
         node_grad_kernel, 2, [(sds((1, nodes, width), F32), hbm)], [vf32(nodes, width), sems(1)],
@@ -560,10 +567,10 @@
     )
     g_e_in, *grads = call(
         finish_kernel,
-        2,
+        4,
         [(sds((12, 2, width), F32), vmem)] + [(sds((2, r, width), F32), vmem) for r in (4, 8, 4)] + [(sds((2, 4), F32), vmem)] * 2,
-        [vf32(32, width)],
-        [smem, vmem, kept, kept],
+        [vf32(120, 128)],
+        [smem, kept, kept, kept],
         (device, x0, total1, gains1),
     )
     return (node_out, node_grad, jnp.swapaxes(g_e_in, 0, 1), *grads)

time: 143 us -> 143 us (level)
  waiting for transfers between devices: 54.6 us -> 51.2 us
  local copies, waits for them, and re-layouts: 0 us -> 2.81 us
    all_to_all x2, waiting for transfers between devices: 0.01 us -> 24.1 us  [spread(): lax.all_to_all(packed, ('graph', 'batch'), 0, 0, tiled=True, axis_index_g...]
    ppermute x20, waiting for transfers between devices: 46.8 us -> 27.1 us  [exchange(): lax.ppermute(blocks[n], 'graph', [(sources[i][n], i) for i in range(graph)])]
    ppermute x2, waiting for transfers between devices: 7.87 us -> 0.01 us  [swap(): return lax.ppermute(send, 'graph', [(i, i ^ 1) for i in range(graph)])]
    ppermute x20, starting transfers between devices: 35.2 us -> 31.7 us  [exchange(): lax.ppermute(blocks[n], 'graph', [(sources[i][n], i) for i in range(graph)])]
    unnamed x0 -> x4, local copies, waits for them, and re-layouts: none -> 2.81 us
    ppermute x2, starting transfers between devices: 0.17 us -> 2.05 us  [swap(): return lax.ppermute(send, 'graph', [(i, i ^ 1) for i in range(graph)])]
  transfers between devices with their start and end apart: 24 -> 24, of which waited for: 8 -> 8; matrix products, arithmetic and copies ran while one was open for 0% -> 0% of each run, Pallas kernels for 13% -> 15%
where the time goes in v3:
time: 143 us; the launch traced here: 142 us
  waiting for transfers between devices  51.2 us (36%)
  starting transfers between devices  48.2 us (34%)
  Pallas kernels  38.5 us (27%)
  local copies, waits for them, and re-layouts  2.81 us (2%)
  between operations  1.52 us (1%)
    pallas_call x11, Pallas kernels, call(): pl.pallas_call(kernel, out_shape=shapes, in_specs=[real.get(id(p), p) for...  38.5 us
    ppermute x20, starting transfers between devices, exchange(): lax.ppermute(blocks[n], 'graph', [(sources[i][n], i) for i in range(graph)])  31.7 us
    ppermute x20, waiting for transfers between devices, exchange(): lax.ppermute(blocks[n], 'graph', [(sources[i][n], i) for i in range(graph)])  27.1 us
    all_to_all x2, waiting for transfers between devices, spread(): lax.all_to_all(packed, ('graph', 'batch'), 0, 0, tiled=True, axis_index_g...  24.1 us
    all_to_all x2, starting transfers between devices, spread(): lax.all_to_all(packed, ('graph', 'batch'), 0, 0, tiled=True, axis_index_g...  14.4 us
  transfers between devices with their start and end apart: 24, of which 8 were waited for; matrix products, arithmetic and copies ran while one was open for 0% of the time, Pallas kernels for 15%

profile of v3, /device:TPU:0, one launch (start us, length us, event | category | flops | bytes accessed | tf_op | source)
XLA Modules:
  0.0 142.3 jit_solution(1444957677972704971)
XLA Ops:
  0.6 1.2 shard_map.188
  1.9 6.4 %collective-permute-start.1 = (bf16[32,512]{1,0:T(8,128)(2,1)S(1)}, bf16[32,512]{1,0:T(8,128)(2,1)S(1)}, u32[]{:S(2)}, u32[]{:S(2)}) collective-permute-start(bf16[32,512]{1,0:T(8,128)(2,1)S(1)} %get-tuple-element.81), channel_id=1, source_target_pairs={{124,0},{8,4},{4,8},{16,12},{12,16},{24,20},{20,24},{32,28},{28,32... | collective-permute-start | bytes 98312 | tf_op jit(solution)/shard_map/ppermute | solution.py:458
  8.4 5.3 %collective-permute-start.3 = (bf16[32,512]{1,0:T(8,128)(2,1)S(1)}, bf16[32,512]{1,0:T(8,128)(2,1)S(1)}, u32[]{:S(2)}, u32[]{:S(2)}) collective-permute-start(bf16[32,512]{1,0:T(8,128)(2,1)S(1)} %get-tuple-element.83), channel_id=1, source_target_pairs={{8,0},{12,4},{16,8},{20,12},{24,16},{28,20},{32,24},{36,28},{40,32... | collective-permute-start | bytes 98312 | tf_op jit(solution)/shard_map/ppermute | solution.py:458
  14.4 3.2 %shard_map.189 = (bf16[512,1024]{1,0:T(8,128)(2,1)S(1)}, bf16[1024,512]{1,0:T(8,128)(2,1)S(1)}, bf16[1536,512]{1,0:T(8,128)(2,1)S(1)}, bf16[512,512]{1,0:T(8,128...) custom-call(s32[1]{0:T(128)} %bitcast.own_ref, ...), custom_call_target="tpu_custom_call" | custom-call | tf_op jit(solution)/shard_map/pallas_call | solution.py:466
  17.6 1.5 %collective-permute-done.4.b4 = bf16[32,512]{1,0:T(8,128)(2,1)S(1)} collective-permute-done((bf16[32,512]{1,0:T(8,128)(2,1)S(1)}, bf16[32,512]{1,0:T(8,128)(2,1)S(1)}, u32[]{:S(2)}, u32[]{:S(2)}) %collective-permute-start.4) | collective-permute-done | bytes 32800 | tf_op jit(solution)/shard_map/ppermute | solution.py:458
  19.2 3.8 %shard_map.190 = (f32[4,128,512]{2,1,0:T(8,128)S(1)}, bf16[416,512]{1,0:T(8,128)(2,1)S(1)}, bf16[1024,512]{1,0:T(8,128)(2,1)S(1)}, bf16[2,1024,512]{2,1,0:T(8,12...) custom-call(s32[1]{0:T(128)} %bitcast.own_ref, ...), custom_call_target="tpu_custom_call" | custom-call | tf_op jit(solution)/shard_map/pallas_call | solution.py:466
  23.0 1.9 %collective-permute-start.6 = (bf16[32,512]{1,0:T(8,128)(2,1)S(1)}, bf16[32,512]{1,0:T(8,128)(2,1)S(1)}, u32[]{:S(2)}, u32[]{:S(2)}) collective-permute-start(bf16[32,512]{1,0:T(8,128)(2,1)S(1)} %get-tuple-element.95), channel_id=1, source_target_pairs={{124,0},{8,4},{4,8},{16,12},{12,16},{24,20},{20,24},{32,28},{28,32... | collective-permute-start | bytes 98312 | tf_op jit(solution)/shard_map/ppermute | solution.py:458
  25.2 5.1 %collective-permute-start.8 = (bf16[32,512]{1,0:T(8,128)(2,1)S(1)}, bf16[32,512]{1,0:T(8,128)(2,1)S(1)}, u32[]{:S(2)}, u32[]{:S(2)}) collective-permute-start(bf16[32,512]{1,0:T(8,128)(2,1)S(1)} %get-tuple-element.97), channel_id=1, source_target_pairs={{8,0},{12,4},{16,8},{20,12},{24,16},{28,20},{32,24},{36,28},{40,32... | collective-permute-start | bytes 98312 | tf_op jit(solution)/shard_map/ppermute | solution.py:458
  30.3 2.3 %shard_map.191 = (bf16[128,512]{1,0:T(8,128)(2,1)S(1)}, bf16[1536,512]{1,0:T(8,128)(2,1)S(1)}, bf16[512,512]{1,0:T(8,128)(2,1)S(1)}, bf16[1024,512]{1,0:T(8,128)...) custom-call(f32[4,128,512]{2,1,0:T(8,128)S(1)} %get-tuple-element.85.state.state_ref,, ...), custom_call_target="tpu_custom_call" | custom-call | tf_op jit(solution)/shard_map/pallas_call | solution.py:466
  32.7 3.0 %collective-permute-done.9.b4 = bf16[32,512]{1,0:T(8,128)(2,1)S(1)} collective-permute-done((bf16[32,512]{1,0:T(8,128)(2,1)S(1)}, bf16[32,512]{1,0:T(8,128)(2,1)S(1)}, u32[]{:S(2)}, u32[]{:S(2)}) %collective-permute-start.9) | collective-permute-done | bytes 32800 | tf_op jit(solution)/shard_map/ppermute | solution.py:458
  35.7 9.5 %shard_map.192 = (f32[1,128,512]{2,1,0:T(8,128)}, bf16[1024,512]{1,0:T(8,128)(2,1)}, f32[128,512]{1,0:T(8,128)S(1)}, bf16[17,112,512]{2,1,0:T(8,128)(2,1)S(1)}, ...) custom-call(s32[1]{0:T(128)} %bitcast.own_ref, ...), custom_call_target="tpu_custom_call" | custom-call | tf_op jit(solution)/shard_map/pallas_call | solution.py:466
  45.8 1.5 %collective-permute-start.11 = (bf16[32,512]{1,0:T(8,128)(2,1)S(1)}, bf16[32,512]{1,0:T(8,128)(2,1)S(1)}, u32[]{:S(2)}, u32[]{:S(2)}) collective-permute-start(bf16[32,512]{1,0:T(8,128)(2,1)S(1)} %get-tuple-element.102), channel_id=1, source_target_pairs={{124,0},{8,4},{4,8},{16,12},{12,16},{24,20},{20,24},{32,28},{28,32... | collective-permute-start | bytes 98312 | tf_op jit(solution)/shard_map/ppermute | solution.py:458
  47.6 1.7 %collective-permute-start.13 = (bf16[32,512]{1,0:T(8,128)(2,1)S(1)}, bf16[32,512]{1,0:T(8,128)(2,1)S(1)}, u32[]{:S(2)}, u32[]{:S(2)}) collective-permute-start(bf16[32,512]{1,0:T(8,128)(2,1)S(1)} %get-tuple-element.104), channel_id=1, source_target_pairs={{120,0},{124,4},{0,8},{4,12},{8,16},{12,20},{16,24},{20,28},{24,32... | collective-permute-start | bytes 98312 | tf_op jit(solution)/shard_map/ppermute | solution.py:458
  49.8 2.7 %collective-permute-done.11.r1 = bf16[32,512]{1,0:T(8,128)(2,1)S(1)} collective-permute-done((bf16[32,512]{1,0:T(8,128)(2,1)S(1)}, bf16[32,512]{1,0:T(8,128)(2,1)S(1)}, u32[]{:S(2)}, u32[]{:S(2)}) %collective-permute-start.11) | collective-permute-done | bytes 32800 | tf_op jit(solution)/shard_map/ppermute | solution.py:458
  52.5 2.7 %collective-permute-done.13.r3 = bf16[32,512]{1,0:T(8,128)(2,1)S(1)} collective-permute-done((bf16[32,512]{1,0:T(8,128)(2,1)S(1)}, bf16[32,512]{1,0:T(8,128)(2,1)S(1)}, u32[]{:S(2)}, u32[]{:S(2)}) %collective-permute-start.13) | collective-permute-done | bytes 32800 | tf_op jit(solution)/shard_map/ppermute | solution.py:458
  55.1 9.7 %shard_map.193 = (f32[128,512]{1,0:T(8,128)S(1)}, bf16[17,112,512]{2,1,0:T(8,128)(2,1)S(1)}, bf16[17,112,512]{2,1,0:T(8,128)(2,1)}, bf16[32,512]{1,0:T(8,128)(2,...) custom-call(s32[1]{0:T(128)} %bitcast.own_ref, ...), custom_call_target="tpu_custom_call" | custom-call | tf_op jit(solution)/shard_map/pallas_call | solution.py:466
  64.8 1.3 copy-done
  66.1 2.0 %collective-permute-start.20 = (bf16[17,112,512]{2,1,0:T(8,128)(2,1)}, bf16[17,112,512]{2,1,0:T(8,128)(2,1)}, u32[]{:S(2)}, u32[]{:S(2)}) collective-permute-start(bf16[17,112,512]{2,1,0:T(8,128)(2,1)} %get-tuple-element.117), channel_id=1, source_target_pairs={{0,4},{4,0},{8,12},{12,8},{16,20},{20,16},{24,28},{28,24},{32,36},... | collective-permute-start | bytes 5849096 | tf_op jit(solution)/shard_map/ppermute | solution.py:491
  68.1 1.5 %shard_map.196 = bf16[64,120,128]{2,1,0:T(8,128)(2,1)} custom-call(bf16[17,112,512]{2,1,0:T(8,128)(2,1)S(1)} %get-tuple-element.118.keep_ref, bf16[17,112,512]{2,1,0:T(8,128)(2,1)S(1)} %collective-permute-done.21.recv_ref), custom_call_target="tpu_custom_call" | custom-call | tf_op jit(solution)/shard_map/pallas_call | solution.py:466
  69.6 8.2 %all-to-all-start.1 = ((bf16[64,120,128]{2,1,0:T(8,128)(2,1)}), bf16[64,120,128]{2,1,0:T(8,128)(2,1)S(1)}, u32[]{:S(2)}, u32[]{:S(2)}) async-start(bf16[64,120,128]{2,1,0:T(8,128)(2,1)} %shard_map.196), calls=%async_computation.1 | async-start | bytes 3932160 | tf_op jit(solution)/shard_map/all_to_all | solution.py:495
  77.8 1.5 %copy-done.1 = bf16[17,112,512]{2,1,0:T(8,128)(2,1)S(1)} copy-done((bf16[17,112,512]{2,1,0:T(8,128)(2,1)S(1)}, bf16[17,112,512]{2,1,0:T(8,128)(2,1)}, u32[]{:S(2)}) %copy-start.1) | copy-done | bytes 1949720
  79.3 3.0 %shard_map.195 = bf16[64,120,128]{2,1,0:T(8,128)(2,1)} custom-call(bf16[17,112,512]{2,1,0:T(8,128)(2,1)S(1)} %copy-done.1, bf16[17,112,512]{2,1,0:T(8,128)(2,1)} %collective-permute-done.20.recv_ref), custom_call_target="tpu_custom_call" | custom-call | tf_op jit(solution)/shard_map/pallas_call | solution.py:466
  82.3 23.8 %all-to-all-done.1.x_ref = bf16[64,120,128]{2,1,0:T(8,128)(2,1)S(1)} async-done(((bf16[64,120,128]{2,1,0:T(8,128)(2,1)}), bf16[64,120,128]{2,1,0:T(8,128)(2,1)S(1)}, u32[]{:S(2)}, u32[]{:S(2)}) %all-to-all-start.1) | async-done | bytes 1966112 | tf_op jit(solution)/shard_map/all_to_all | solution.py:495
  106.1 6.3 %all-to-all-start = ((bf16[64,120,128]{2,1,0:T(8,128)(2,1)}), bf16[64,120,128]{2,1,0:T(8,128)(2,1)}, u32[]{:S(2)}, u32[]{:S(2)}) async-start(bf16[64,120,128]{2,1,0:T(8,128)(2,1)} %shard_map.195), calls=%async_computation | async-start | bytes 3932160 | tf_op jit(solution)/shard_map/all_to_all | solution.py:495
  112.5 5.2 %collective-permute-start.16 = (bf16[32,512]{1,0:T(8,128)(2,1)S(1)}, bf16[32,512]{1,0:T(8,128)(2,1)S(1)}, u32[]{:S(2)}, u32[]{:S(2)}) collective-permute-start(bf16[32,512]{1,0:T(8,128)(2,1)S(1)} %get-tuple-element.112), channel_id=1, source_target_pairs={{124,0},{8,4},{4,8},{16,12},{12,16},{24,20},{20,24},{32,28},{28,32... | collective-permute-start | bytes 98312 | tf_op jit(solution)/shard_map/ppermute | solution.py:458
  117.7 0.8 collective-permute-start.17
  118.6 1.2 collective-permute-start.18
  120.4 15.1 %collective-permute-done.16.r1 = bf16[32,512]{1,0:T(8,128)(2,1)S(1)} collective-permute-done((bf16[32,512]{1,0:T(8,128)(2,1)S(1)}, bf16[32,512]{1,0:T(8,128)(2,1)S(1)}, u32[]{:S(2)}, u32[]{:S(2)}) %collective-permute-start.16) | collective-permute-done | bytes 32800 | tf_op jit(solution)/shard_map/ppermute | solution.py:458
  135.5 2.1 %collective-permute-done.18.r3 = bf16[32,512]{1,0:T(8,128)(2,1)S(1)} collective-permute-done((bf16[32,512]{1,0:T(8,128)(2,1)S(1)}, bf16[32,512]{1,0:T(8,128)(2,1)S(1)}, u32[]{:S(2)}, u32[]{:S(2)}) %collective-permute-start.18) | collective-permute-done | bytes 32800 | tf_op jit(solution)/shard_map/ppermute | solution.py:458
  137.6 1.0 shard_map.194
  138.6 0.8 shard_map.197
  139.7 2.6 %shard_map.198 = (f32[12,2,512]{2,1,0:T(2,128)}, f32[2,4,512]{2,1,0:T(4,128)}, f32[2,8,512]{2,1,0:T(8,128)}, f32[2,4,512]{2,1,0:T(4,128)}, f32[2,4]{1,0:T(2,128)}, /*index=5*/f32[2,4]{1,0:T(2,128)}) custom-call(s32[1]{0:T(128)} %bitcast.3.device_ref, bf16[64,120,128]{2,1,0:T(8,128)(2,1)} %all-to-all-done.x0_ref, f32[120,128]{1,0:T(8,128)S(1)} %get-tuple-element.120.total1, ...), custom_call_target="tpu_custom_call" | custom-call | tf_op jit(solution)/shard_map/pallas_call | solution.py:466
  (31 shorter events, 2.8 us)
Async XLA Ops:
  1.8 15.7 %collective-permute-start = (bf16[32,512]{1,0:T(8,128)(2,1)S(1)}, bf16[32,512]{1,0:T(8,128)(2,1)S(1)}, u32[]{:S(2)}, u32[]{:S(2)}) collective-permute-start(bf16[32,512]{1,0:T(8,128)(2,1)S(1)} %get-tuple-element.80), channel_id=1, source_target_pairs={{4,0},{0,4},{12,8},{8,12},{20,16},{16,20},{28,24},{24,28},{36,32},... | collective-permute-start | bytes 98312 | tf_op jit(solution)/shard_map/ppermute | solution.py:458
  1.9 15.7 %collective-permute-start.1 = (bf16[32,512]{1,0:T(8,128)(2,1)S(1)}, bf16[32,512]{1,0:T(8,128)(2,1)S(1)}, u32[]{:S(2)}, u32[]{:S(2)}) collective-permute-start(bf16[32,512]{1,0:T(8,128)(2,1)S(1)} %get-tuple-element.81), channel_id=1, source_target_pairs={{124,0},{8,4},{4,8},{16,12},{12,16},{24,20},{20,24},{32,28},{28,32... | collective-permute-start | bytes 98312 | tf_op jit(solution)/shard_map/ppermute | solution.py:458
  8.4 9.2 %collective-permute-start.2 = (bf16[32,512]{1,0:T(8,128)(2,1)S(1)}, bf16[32,512]{1,0:T(8,128)(2,1)S(1)}, u32[]{:S(2)}, u32[]{:S(2)}) collective-permute-start(bf16[32,512]{1,0:T(8,128)(2,1)S(1)} %get-tuple-element.82), channel_id=1, source_target_pairs={{120,0},{124,4},{0,8},{4,12},{8,16},{12,20},{16,24},{20,28},{24,32... | collective-permute-start | bytes 98312 | tf_op jit(solution)/shard_map/ppermute | solution.py:458
  8.4 9.2 %collective-permute-start.3 = (bf16[32,512]{1,0:T(8,128)(2,1)S(1)}, bf16[32,512]{1,0:T(8,128)(2,1)S(1)}, u32[]{:S(2)}, u32[]{:S(2)}) collective-permute-start(bf16[32,512]{1,0:T(8,128)(2,1)S(1)} %get-tuple-element.83), channel_id=1, source_target_pairs={{8,0},{12,4},{16,8},{20,12},{24,16},{28,20},{32,24},{36,28},{40,32... | collective-permute-start | bytes 98312 | tf_op jit(solution)/shard_map/ppermute | solution.py:458
  13.7 5.4 %collective-permute-start.4 = (bf16[32,512]{1,0:T(8,128)(2,1)S(1)}, bf16[32,512]{1,0:T(8,128)(2,1)S(1)}, u32[]{:S(2)}, u32[]{:S(2)}) collective-permute-start(bf16[32,512]{1,0:T(8,128)(2,1)S(1)} %get-tuple-element.84), channel_id=1, source_target_pairs={{64,0},{68,4},{72,8},{76,12},{80,16},{84,20},{88,24},{92,28},{96,3... | collective-permute-start | bytes 98312 | tf_op jit(solution)/shard_map/ppermute | solution.py:458
  22.9 9.7 %collective-permute-start.5 = (bf16[32,512]{1,0:T(8,128)(2,1)S(1)}, bf16[32,512]{1,0:T(8,128)(2,1)S(1)}, u32[]{:S(2)}, u32[]{:S(2)}) collective-permute-start(bf16[32,512]{1,0:T(8,128)(2,1)S(1)} %get-tuple-element.94), channel_id=1, source_target_pairs={{4,0},{0,4},{12,8},{8,12},{20,16},{16,20},{28,24},{24,28},{36,32},... | collective-permute-start | bytes 98312 | tf_op jit(solution)/shard_map/ppermute | solution.py:458
  23.0 9.6 %collective-permute-start.6 = (bf16[32,512]{1,0:T(8,128)(2,1)S(1)}, bf16[32,512]{1,0:T(8,128)(2,1)S(1)}, u32[]{:S(2)}, u32[]{:S(2)}) collective-permute-start(bf16[32,512]{1,0:T(8,128)(2,1)S(1)} %get-tuple-element.95), channel_id=1, source_target_pairs={{124,0},{8,4},{4,8},{16,12},{12,16},{24,20},{20,24},{32,28},{28,32... | collective-permute-start | bytes 98312 | tf_op jit(solution)/shard_map/ppermute | solution.py:458
  25.0 7.7 %collective-permute-start.7 = (bf16[32,512]{1,0:T(8,128)(2,1)S(1)}, bf16[32,512]{1,0:T(8,128)(2,1)S(1)}, u32[]{:S(2)}, u32[]{:S(2)}) collective-permute-start(bf16[32,512]{1,0:T(8,128)(2,1)S(1)} %get-tuple-element.96), channel_id=1, source_target_pairs={{120,0},{124,4},{0,8},{4,12},{8,16},{12,20},{16,24},{20,28},{24,32... | collective-permute-start | bytes 98312 | tf_op jit(solution)/shard_map/ppermute | solution.py:458
  25.2 7.5 %collective-permute-start.8 = (bf16[32,512]{1,0:T(8,128)(2,1)S(1)}, bf16[32,512]{1,0:T(8,128)(2,1)S(1)}, u32[]{:S(2)}, u32[]{:S(2)}) collective-permute-start(bf16[32,512]{1,0:T(8,128)(2,1)S(1)} %get-tuple-element.97), channel_id=1, source_target_pairs={{8,0},{12,4},{16,8},{20,12},{24,16},{28,20},{32,24},{36,28},{40,32... | collective-permute-start | bytes 98312 | tf_op jit(solution)/shard_map/ppermute | solution.py:458
  30.3 5.4 %collective-permute-start.9 = (bf16[32,512]{1,0:T(8,128)(2,1)S(1)}, bf16[32,512]{1,0:T(8,128)(2,1)S(1)}, u32[]{:S(2)}, u32[]{:S(2)}) collective-permute-start(bf16[32,512]{1,0:T(8,128)(2,1)S(1)} %get-tuple-element.98), channel_id=1, source_target_pairs={{64,0},{68,4},{72,8},{76,12},{80,16},{84,20},{88,24},{92,28},{96,3... | collective-permute-start | bytes 98312 | tf_op jit(solution)/shard_map/ppermute | solution.py:458
  45.2 22.9 %collective-permute-start.21 = (bf16[17,112,512]{2,1,0:T(8,128)(2,1)S(1)}, bf16[17,112,512]{2,1,0:T(8,128)(2,1)S(1)}, u32[]{:S(2)}, u32[]{:S(2)}) collective-permute-start(bf16[17,112,512]{2,1,0:T(8,128)(2,1)S(1)} %get-tuple-element.119), channel_id=1, source_target_pairs={{0,4},{4,0},{8,12},{12,8},{16,20},{20,16},{24,28},{28,24},{32,36},... | collective-permute-start | bytes 5849096 | tf_op jit(solution)/shard_map/ppermute | solution.py:491
  45.3 4.0 %collective-permute-start.10 = (bf16[32,512]{1,0:T(8,128)(2,1)S(1)}, bf16[32,512]{1,0:T(8,128)(2,1)S(1)}, u32[]{:S(2)}, u32[]{:S(2)}) collective-permute-start(bf16[32,512]{1,0:T(8,128)(2,1)S(1)} %get-tuple-element.101), channel_id=1, source_target_pairs={{4,0},{0,4},{12,8},{8,12},{20,16},{16,20},{28,24},{24,28},{36,32},... | collective-permute-start | bytes 98312 | tf_op jit(solution)/shard_map/ppermute | solution.py:458
  45.8 6.7 %collective-permute-start.11 = (bf16[32,512]{1,0:T(8,128)(2,1)S(1)}, bf16[32,512]{1,0:T(8,128)(2,1)S(1)}, u32[]{:S(2)}, u32[]{:S(2)}) collective-permute-start(bf16[32,512]{1,0:T(8,128)(2,1)S(1)} %get-tuple-element.102), channel_id=1, source_target_pairs={{124,0},{8,4},{4,8},{16,12},{12,16},{24,20},{20,24},{32,28},{28,32... | collective-permute-start | bytes 98312 | tf_op jit(solution)/shard_map/ppermute | solution.py:458
  47.3 5.1 %collective-permute-start.12 = (bf16[32,512]{1,0:T(8,128)(2,1)S(1)}, bf16[32,512]{1,0:T(8,128)(2,1)S(1)}, u32[]{:S(2)}, u32[]{:S(2)}) collective-permute-start(bf16[32,512]{1,0:T(8,128)(2,1)S(1)} %get-tuple-element.103), channel_id=1, source_target_pairs={{8,0},{12,4},{16,8},{20,12},{24,16},{28,20},{32,24},{36,28},{40,32... | collective-permute-start | bytes 98312 | tf_op jit(solution)/shard_map/ppermute | solution.py:458
  47.6 7.5 %collective-permute-start.13 = (bf16[32,512]{1,0:T(8,128)(2,1)S(1)}, bf16[32,512]{1,0:T(8,128)(2,1)S(1)}, u32[]{:S(2)}, u32[]{:S(2)}) collective-permute-start(bf16[32,512]{1,0:T(8,128)(2,1)S(1)} %get-tuple-element.104), channel_id=1, source_target_pairs={{120,0},{124,4},{0,8},{4,12},{8,16},{12,20},{16,24},{20,28},{24,32... | collective-permute-start | bytes 98312 | tf_op jit(solution)/shard_map/ppermute | solution.py:458
  49.3 5.8 %collective-permute-start.14 = (bf16[32,512]{1,0:T(8,128)(2,1)S(1)}, bf16[32,512]{1,0:T(8,128)(2,1)S(1)}, u32[]{:S(2)}, u32[]{:S(2)}) collective-permute-start(bf16[32,512]{1,0:T(8,128)(2,1)S(1)} %get-tuple-element.105), channel_id=1, source_target_pairs={{64,0},{68,4},{72,8},{76,12},{80,16},{84,20},{88,24},{92,28},{96,3... | collective-permute-start | bytes 98312 | tf_op jit(solution)/shard_map/ppermute | solution.py:458
  64.8 1.3 copy-start
  66.1 11.6 %collective-permute-start.20 = (bf16[17,112,512]{2,1,0:T(8,128)(2,1)}, bf16[17,112,512]{2,1,0:T(8,128)(2,1)}, u32[]{:S(2)}, u32[]{:S(2)}) collective-permute-start(bf16[17,112,512]{2,1,0:T(8,128)(2,1)} %get-tuple-element.117), channel_id=1, source_target_pairs={{0,4},{4,0},{8,12},{12,8},{16,20},{20,16},{24,28},{28,24},{32,36},... | collective-permute-start | bytes 5849096 | tf_op jit(solution)/shard_map/ppermute | solution.py:491
  69.6 36.6 %all-to-all-start.1 = ((bf16[64,120,128]{2,1,0:T(8,128)(2,1)}), bf16[64,120,128]{2,1,0:T(8,128)(2,1)S(1)}, u32[]{:S(2)}, u32[]{:S(2)}) async-start(bf16[64,120,128]{2,1,0:T(8,128)(2,1)} %shard_map.196), calls=%async_computation.1 | async-start | bytes 3932160 | tf_op jit(solution)/shard_map/all_to_all | solution.py:495
  77.7 1.5 %copy-start.1 = (bf16[17,112,512]{2,1,0:T(8,128)(2,1)S(1)}, bf16[17,112,512]{2,1,0:T(8,128)(2,1)}, u32[]{:S(2)}) copy-start(bf16[17,112,512]{2,1,0:T(8,128)(2,1)} %copy-done) | copy-start | bytes 5849092
  106.1 33.5 %all-to-all-start = ((bf16[64,120,128]{2,1,0:T(8,128)(2,1)}), bf16[64,120,128]{2,1,0:T(8,128)(2,1)}, u32[]{:S(2)}, u32[]{:S(2)}) async-start(bf16[64,120,128]{2,1,0:T(8,128)(2,1)} %shard_map.195), calls=%async_computation | async-start | bytes 3932160 | tf_op jit(solution)/shard_map/all_to_all | solution.py:495
  112.4 8.0 %collective-permute-start.15 = (bf16[32,512]{1,0:T(8,128)(2,1)S(1)}, bf16[32,512]{1,0:T(8,128)(2,1)S(1)}, u32[]{:S(2)}, u32[]{:S(2)}) collective-permute-start(bf16[32,512]{1,0:T(8,128)(2,1)S(1)} %get-tuple-element.111), channel_id=1, source_target_pairs={{4,0},{0,4},{12,8},{8,12},{20,16},{16,20},{28,24},{24,28},{36,32},... | collective-permute-start | bytes 98312 | tf_op jit(solution)/shard_map/ppermute | solution.py:458
  112.5 23.0 %collective-permute-start.16 = (bf16[32,512]{1,0:T(8,128)(2,1)S(1)}, bf16[32,512]{1,0:T(8,128)(2,1)S(1)}, u32[]{:S(2)}, u32[]{:S(2)}) collective-permute-start(bf16[32,512]{1,0:T(8,128)(2,1)S(1)} %get-tuple-element.112), channel_id=1, source_target_pairs={{124,0},{8,4},{4,8},{16,12},{12,16},{24,20},{20,24},{32,28},{28,32... | collective-permute-start | bytes 98312 | tf_op jit(solution)/shard_map/ppermute | solution.py:458
  117.7 17.8 %collective-permute-start.17 = (bf16[32,512]{1,0:T(8,128)(2,1)S(1)}, bf16[32,512]{1,0:T(8,128)(2,1)S(1)}, u32[]{:S(2)}, u32[]{:S(2)}) collective-permute-start(bf16[32,512]{1,0:T(8,128)(2,1)S(1)} %get-tuple-element.113), channel_id=1, source_target_pairs={{8,0},{12,4},{16,8},{20,12},{24,16},{28,20},{32,24},{36,28},{40,32... | collective-permute-start | bytes 98312 | tf_op jit(solution)/shard_map/ppermute | solution.py:458
  118.6 19.0 %collective-permute-start.18 = (bf16[32,512]{1,0:T(8,128)(2,1)S(1)}, bf16[32,512]{1,0:T(8,128)(2,1)S(1)}, u32[]{:S(2)}, u32[]{:S(2)}) collective-permute-start(bf16[32,512]{1,0:T(8,128)(2,1)S(1)} %get-tuple-element.114), channel_id=1, source_target_pairs={{120,0},{124,4},{0,8},{4,12},{8,16},{12,20},{16,24},{20,28},{24,32... | collective-permute-start | bytes 98312 | tf_op jit(solution)/shard_map/ppermute | solution.py:458
  119.8 17.8 %collective-permute-start.19 = (bf16[32,512]{1,0:T(8,128)(2,1)S(1)}, bf16[32,512]{1,0:T(8,128)(2,1)S(1)}, u32[]{:S(2)}, u32[]{:S(2)}) collective-permute-start(bf16[32,512]{1,0:T(8,128)(2,1)S(1)} %get-tuple-element.115), channel_id=1, source_target_pairs={{64,0},{68,4},{72,8},{76,12},{80,16},{84,20},{88,24},{92,28},{96,3... | collective-permute-start | bytes 98312 | tf_op jit(solution)/shard_map/ppermute | solution.py:458

commit v4 on v3

--- a/solution.py
+++ b/solution.py
@@ -47,13 +47,16 @@
     return s * (1.0 + pre * (1.0 - s))
 
 
+def near(own):
+    return ((((own - 1) & 31) ^ 1) + 1) & 31
+
+
 def neighbours(own):
-    return own ^ 1, ((((own - 1) & 31) ^ 1) + 1) & 31, (own - 2) & 31, (own + 2) & 31, own ^ 16
+    return own ^ 1, near(own), near(own) ^ 1, near(own ^ 1), own ^ 16
 
 
 def readers(own):
-    swap, near, below, above, far = neighbours(own)
-    return swap, near, above, below, far
+    return own ^ 1, near(own), near(own ^ 1), near(own) ^ 1, own ^ 16
 
 
 def list_onehot(lists_ref, reader, nodes):
@@ -63,9 +66,10 @@
 
 
 def send_blocks(lists_ref, own, vb, outs):
-    for reader, out in zip(readers(own), outs):
+    swap, pair, side, far = outs
+    for reader, (out, at) in zip(readers(own), ((swap, 0), (pair, 0), (side, 0), (pair, 32), (far, 0))):
         onehot = list_onehot(lists_ref, reader, vb.shape[0])
-        out[...] = tn(onehot, vb).astype(BF16)
+        out[at : at + 32, :] = tn(onehot, vb).astype(BF16)
 
 
 def returned(lists_ref, own, blocks):
@@ -146,9 +150,9 @@
     return grad_gain, nt(da, w_in_ref[0:512, :]), nt(da, w_in_ref[512:1024, :])
 
 
-def gather_kernel(own_ref, lists_ref, vb_ref, lists, vb, o0, o1, o2, o3, o4, sems):
+def gather_kernel(own_ref, lists_ref, vb_ref, lists, vb, o0, o1, o2, o3, sems):
     wait(Copies(sems).start((lists_ref, lists), (vb_ref.at[0], vb)))
-    send_blocks(lists, own_ref[0], vb[...], (o0, o1, o2, o3, o4))
+    send_blocks(lists, own_ref[0], vb[...], (o0, o1, o2, o3))
 
 
 def start_weights(copies, layer, sources, targets):
@@ -196,8 +200,8 @@
 
 def fill_remote(proj, near, senders, vb, blocks, w_in_ref):
     senders[0:128, :] = vb
-    for n, block in enumerate(blocks):
-        senders[128 + 32 * n : 160 + 32 * n, :] = block[...]
+    for n, (block, at) in enumerate(zip(blocks, (0, 0, 0, 32, 0))):
+        senders[128 + 32 * n : 160 + 32 * n, :] = block[at : at + 32, :]
     proj[0:256, :] = near[...]
     proj[256:416, :] = nn(senders[128:288, :], w_in_ref[512:1024, :]).astype(BF16)
     proj[416:512, :] = jnp.zeros((96, 512), BF16)
@@ -205,7 +209,7 @@
 
 def forward_kernel(
     own_ref, count_ref, lists, vb_ref, onehot, eb, we_in, we_out, wn_in, wn_out, e_gain, n_gain, part, near, b0, b1, b2, b3, b4,
-    state, sides, eb_next, saved_out, inv_out, o0, o1, o2, o3, o4,
+    state, sides, eb_next, saved_out, inv_out, o0, o1, o2, o3,
     proj, message, saved, inv_s, sems,
 ):
     own, count = own_ref[0], count_ref[0]
@@ -236,7 +240,7 @@
     state[2] = normed
     state[3] = jnp.broadcast_to(inv, (128, 512))
     sides[288:416, :] = agg
-    send_blocks(lists, own, v.astype(BF16), (o0, o1, o2, o3, o4))
+    send_blocks(lists, own, v.astype(BF16), (o0, o1, o2, o3))
     wait(saves)
 
 
@@ -451,11 +455,19 @@
     hbm = pl.BlockSpec(memory_space=pltpu.HBM)
     kept = pl.BlockSpec(memory_space=pltpu.VMEM)
 
-    def exchange(blocks, back):
-        sources = [(readers if back else neighbours)(i) for i in range(graph)]
+    def move(block, source):
+        return lax.ppermute(block, "graph", [(source(i), i) for i in range(graph)])
+
+    def fetch(blocks):
+        swap, pair, side, far = blocks
+        pair = move(pair, near)
+        side, far, swap = move(side, lambda i: near(i) ^ 1), move(far, lambda i: i ^ 16), move(swap, lambda i: i ^ 1)
+        return swap, pair, side, move(pair, lambda i: i ^ 1), far
+
+    def give_back(blocks):
         outs = {}
         for n in ORDER:
-            outs[n] = lax.ppermute(blocks[n], "graph", [(sources[i][n], i) for i in range(graph)])
+            outs[n] = move(blocks[n], lambda i, n=n: readers(i)[n])
         return [outs[n] for n in range(5)]
 
     def call(kernel, mib, outs, scratch, specs, args):
@@ -501,13 +513,14 @@
     edge_b, edge_f = vb16(edges, width), vf32(edges, width)
     grads_s = [vb16(r, width) for r in (1536, 512, 1024, 512)]
     blocks_out = [(sds((32, width), BF16), vmem)] * 5
+    fetch_out = [(sds((r, width), BF16), vmem) for r in (32, 64, 32, 32)]
     half = (sds((17, 112, width), BF16), vmem)
 
     lists, vb0, *first = call(
-        gather_kernel, 2, [(sds(send_list.shape, jnp.int32), kept), ob16(nodes, width)] + blocks_out, [sems(2)],
+        gather_kernel, 2, [(sds(send_list.shape, jnp.int32), kept), ob16(nodes, width)] + fetch_out, [sems(2)],
         [smem, hbm, hbm], (own_arr, send_list, node_latent),
     )
-    senders0 = exchange(first, False)
+    senders0 = fetch(first)
     onehot, eb0, we_in0, we_out0, wn_in0, wn_out0, e_gain, n_gain, part0, near0 = call(
         first_kernel,
         4,
@@ -520,12 +533,12 @@
     state, sides, eb1, saved, inv, *second = call(
         forward_kernel,
         10,
-        [of32(4, nodes, width), ob16(416, width), ob16(edges, width), (sds((2, edges, width), BF16), hbm), (sds((edges, 128), F32), hbm)] + blocks_out,
+        [of32(4, nodes, width), ob16(416, width), ob16(edges, width), (sds((2, edges, width), BF16), hbm), (sds((edges, 128), F32), hbm)] + fetch_out,
         [vb16(512, width), edge_b, vb16(2, edges, width), vf32(edges, 128), sems(16)],
         [smem, smem] + [kept] * 12 + [vmem] * 5,
         (own_arr, edge_count, lists, vb0, onehot, eb0, *weights0, part0, near0, *senders0),
     )
-    senders1 = exchange(second, False)
+    senders1 = fetch(second)
     cot, we_in1, we_out1, wn_in1, wn_out1, part1, near1 = call(
         second_kernel,
         4,
@@ -544,7 +557,7 @@
     )
     packed_out = (sds((64, 120, 128), BF16), hbm)
     pack_s = [vf32(4, 120, 128), vb16(64, 120, 128), sems(16)]
-    returned1 = exchange(back1, True)
+    returned1 = give_back(back1)
     (packed1,) = call(pack_kernel, 5, [packed_out], pack_s, [vmem, vmem], (keep1, swap(send1)))
     x1 = spread(packed1)
     grad0, keep0, send0, *back0 = call(
@@ -555,7 +568,7 @@
         [smem, smem, kept, kept] + [vmem] * 6 + [hbm, free, free] + [hbm] * 9,
         (own_arr, edge_count, lists, onehot, grad1, *returned1, edge_latent, state, sides, edge_grad, saved, inv, *weights, edge_gain, node_gain),
     )
-    returned0 = exchange(back0, True)
+    returned0 = give_back(back0)
     (packed0,) = call(pack_kernel, 5, [packed_out], pack_s, [vmem, vmem], (keep0, swap(send0)))
     x0 = spread(packed0)
     total1, gains1 = call(

time: 143 us -> 144 us (level)
  waiting for transfers between devices: 51.2 us -> 57.8 us
  starting transfers between devices: 48.2 us -> 43.2 us
    ppermute x20, waiting for transfers between devices: 27.1 us -> 33.5 us  [move(): return lax.ppermute(block, 'graph', [(source(i), i) for i in range(graph)])]
    ppermute x20, starting transfers between devices: 31.7 us -> 27.5 us  [move(): return lax.ppermute(block, 'graph', [(source(i), i) for i in range(graph)])]
  transfers between devices with their start and end apart: 24 -> 24, of which waited for: 8 -> 9; matrix products, arithmetic and copies ran while one was open for 0% -> 0% of each run, Pallas kernels for 15% -> 15%
where the time goes in v4:
time: 144 us
  waiting for transfers between devices  57.8 us (40%)
  starting transfers between devices  43.2 us (30%)
  Pallas kernels  38.7 us (27%)
  local copies, waits for them, and re-layouts  2.81 us (2%)
  between operations  1.46 us (1%)
    pallas_call x11, Pallas kernels, call(): pl.pallas_call(kernel, out_shape=shapes, in_specs=[real.get(id(p), p) for...  38.7 us
    ppermute x20, waiting for transfers between devices, move(): return lax.ppermute(block, 'graph', [(source(i), i) for i in range(graph)])  33.5 us
    ppermute x20, starting transfers between devices, move(): return lax.ppermute(block, 'graph', [(source(i), i) for i in range(graph)])  27.5 us
    all_to_all x2, waiting for transfers between devices, spread(): lax.all_to_all(packed, ('graph', 'batch'), 0, 0, tiled=True, axis_index_g...  24.4 us
    all_to_all x2, starting transfers between devices, spread(): lax.all_to_all(packed, ('graph', 'batch'), 0, 0, tiled=True, axis_index_g...  14.5 us
  transfers between devices with their start and end apart: 24, of which 9 were waited for; matrix products, arithmetic and copies ran while one was open for 0% of the time, Pallas kernels for 15%

profile of v4, /device:TPU:0, one launch (start us, length us, event | category | flops | bytes accessed | tf_op | source)
XLA Modules:
  0.0 144.0 jit_solution(11142098155844485006)
XLA Ops:
  0.6 1.2 shard_map.188
  1.8 5.9 %collective-permute-start.1 = (bf16[64,512]{1,0:T(8,128)(2,1)S(1)}, bf16[64,512]{1,0:T(8,128)(2,1)S(1)}, u32[]{:S(2)}, u32[]{:S(2)}) collective-permute-start(bf16[64,512]{1,0:T(8,128)(2,1)S(1)} %get-tuple-element.79), channel_id=1, source_target_pairs={{124,0},{8,4},{4,8},{16,12},{12,16},{24,20},{20,24},{32,28},{28,32... | collective-permute-start | bytes 196616 | tf_op jit(solution)/shard_map/ppermute | solution.py:459
  7.7 2.0 %collective-permute-done.1.b1 = bf16[64,512]{1,0:T(8,128)(2,1)S(1)} collective-permute-done((bf16[64,512]{1,0:T(8,128)(2,1)S(1)}, bf16[64,512]{1,0:T(8,128)(2,1)S(1)}, u32[]{:S(2)}, u32[]{:S(2)}) %collective-permute-start.1) | collective-permute-done | bytes 65568 | tf_op jit(solution)/shard_map/ppermute | solution.py:459
  10.2 2.1 %collective-permute-start.4 = (bf16[32,512]{1,0:T(8,128)(2,1)S(1)}, bf16[32,512]{1,0:T(8,128)(2,1)S(1)}, u32[]{:S(2)}, u32[]{:S(2)}) collective-permute-start(bf16[32,512]{1,0:T(8,128)(2,1)S(1)} %get-tuple-element.81), channel_id=1, source_target_pairs={{64,0},{68,4},{72,8},{76,12},{80,16},{84,20},{88,24},{92,28},{96,3... | collective-permute-start | bytes 98312 | tf_op jit(solution)/shard_map/ppermute | solution.py:459
  12.9 3.2 %shard_map.189 = (bf16[512,1024]{1,0:T(8,128)(2,1)S(1)}, bf16[1024,512]{1,0:T(8,128)(2,1)S(1)}, bf16[1536,512]{1,0:T(8,128)(2,1)S(1)}, bf16[512,512]{1,0:T(8,128...) custom-call(s32[1]{0:T(128)} %bitcast.own_ref, ...), custom_call_target="tpu_custom_call" | custom-call | tf_op jit(solution)/shard_map/pallas_call | solution.py:478
  16.1 1.3 collective-permute-done.2.b2
  17.4 3.9 %shard_map.190 = (f32[4,128,512]{2,1,0:T(8,128)S(1)}, bf16[416,512]{1,0:T(8,128)(2,1)S(1)}, bf16[1024,512]{1,0:T(8,128)(2,1)S(1)}, bf16[2,1024,512]{2,1,0:T(8,12...) custom-call(s32[1]{0:T(128)} %bitcast.own_ref, ...), custom_call_target="tpu_custom_call" | custom-call | tf_op jit(solution)/shard_map/pallas_call | solution.py:478
  21.4 4.0 %collective-permute-start.6 = (bf16[64,512]{1,0:T(8,128)(2,1)S(1)}, bf16[64,512]{1,0:T(8,128)(2,1)S(1)}, u32[]{:S(2)}, u32[]{:S(2)}) collective-permute-start(bf16[64,512]{1,0:T(8,128)(2,1)S(1)} %get-tuple-element.92), channel_id=1, source_target_pairs={{124,0},{8,4},{4,8},{16,12},{12,16},{24,20},{20,24},{32,28},{28,32... | collective-permute-start | bytes 196616 | tf_op jit(solution)/shard_map/ppermute | solution.py:459
  25.4 3.1 %collective-permute-done.6.b1 = bf16[64,512]{1,0:T(8,128)(2,1)S(1)} collective-permute-done((bf16[64,512]{1,0:T(8,128)(2,1)S(1)}, bf16[64,512]{1,0:T(8,128)(2,1)S(1)}, u32[]{:S(2)}, u32[]{:S(2)}) %collective-permute-start.6) | collective-permute-done | bytes 65568 | tf_op jit(solution)/shard_map/ppermute | solution.py:459
  29.0 1.7 %collective-permute-start.9 = (bf16[32,512]{1,0:T(8,128)(2,1)S(1)}, bf16[32,512]{1,0:T(8,128)(2,1)S(1)}, u32[]{:S(2)}, u32[]{:S(2)}) collective-permute-start(bf16[32,512]{1,0:T(8,128)(2,1)S(1)} %get-tuple-element.94), channel_id=1, source_target_pairs={{64,0},{68,4},{72,8},{76,12},{80,16},{84,20},{88,24},{92,28},{96,3... | collective-permute-start | bytes 98312 | tf_op jit(solution)/shard_map/ppermute | solution.py:459
  30.6 2.3 %shard_map.191 = (bf16[128,512]{1,0:T(8,128)(2,1)S(1)}, bf16[1536,512]{1,0:T(8,128)(2,1)S(1)}, bf16[512,512]{1,0:T(8,128)(2,1)S(1)}, bf16[1024,512]{1,0:T(8,128)...) custom-call(f32[4,128,512]{2,1,0:T(8,128)S(1)} %get-tuple-element.82.state.state_ref,, ...), custom_call_target="tpu_custom_call" | custom-call | tf_op jit(solution)/shard_map/pallas_call | solution.py:478
  33.0 3.2 %collective-permute-done.7.b2 = bf16[32,512]{1,0:T(8,128)(2,1)S(1)} collective-permute-done((bf16[32,512]{1,0:T(8,128)(2,1)S(1)}, bf16[32,512]{1,0:T(8,128)(2,1)S(1)}, u32[]{:S(2)}, u32[]{:S(2)}) %collective-permute-start.7) | collective-permute-done | bytes 32800 | tf_op jit(solution)/shard_map/ppermute | solution.py:459
  36.2 9.5 %shard_map.192 = (f32[1,128,512]{2,1,0:T(8,128)}, bf16[1024,512]{1,0:T(8,128)(2,1)}, f32[128,512]{1,0:T(8,128)S(1)}, bf16[17,112,512]{2,1,0:T(8,128)(2,1)S(1)}, ...) custom-call(s32[1]{0:T(128)} %bitcast.own_ref, ...), custom_call_target="tpu_custom_call" | custom-call | tf_op jit(solution)/shard_map/pallas_call | solution.py:478
  45.7 1.2 collective-permute-start.21
  47.0 2.7 %collective-permute-start.11 = (bf16[32,512]{1,0:T(8,128)(2,1)S(1)}, bf16[32,512]{1,0:T(8,128)(2,1)S(1)}, u32[]{:S(2)}, u32[]{:S(2)}) collective-permute-start(bf16[32,512]{1,0:T(8,128)(2,1)S(1)} %get-tuple-element.98), channel_id=1, source_target_pairs={{124,0},{8,4},{4,8},{16,12},{12,16},{24,20},{20,24},{32,28},{28,32... | collective-permute-start | bytes 98312 | tf_op jit(solution)/shard_map/ppermute | solution.py:459
  50.0 1.7 %collective-permute-start.13 = (bf16[32,512]{1,0:T(8,128)(2,1)S(1)}, bf16[32,512]{1,0:T(8,128)(2,1)S(1)}, u32[]{:S(2)}, u32[]{:S(2)}) collective-permute-start(bf16[32,512]{1,0:T(8,128)(2,1)S(1)} %get-tuple-element.100), channel_id=1, source_target_pairs={{120,0},{12,4},{0,8},{20,12},{8,16},{28,20},{16,24},{36,28},{24,32... | collective-permute-start | bytes 98312 | tf_op jit(solution)/shard_map/ppermute | solution.py:459
  51.9 1.8 %collective-permute-done.11.r1 = bf16[32,512]{1,0:T(8,128)(2,1)S(1)} collective-permute-done((bf16[32,512]{1,0:T(8,128)(2,1)S(1)}, bf16[32,512]{1,0:T(8,128)(2,1)S(1)}, u32[]{:S(2)}, u32[]{:S(2)}) %collective-permute-start.11) | collective-permute-done | bytes 32800 | tf_op jit(solution)/shard_map/ppermute | solution.py:459
  53.6 3.8 %collective-permute-done.13.r3 = bf16[32,512]{1,0:T(8,128)(2,1)S(1)} collective-permute-done((bf16[32,512]{1,0:T(8,128)(2,1)S(1)}, bf16[32,512]{1,0:T(8,128)(2,1)S(1)}, u32[]{:S(2)}, u32[]{:S(2)}) %collective-permute-start.13) | collective-permute-done | bytes 32800 | tf_op jit(solution)/shard_map/ppermute | solution.py:459
  57.5 9.7 %shard_map.193 = (f32[128,512]{1,0:T(8,128)S(1)}, bf16[17,112,512]{2,1,0:T(8,128)(2,1)S(1)}, bf16[17,112,512]{2,1,0:T(8,128)(2,1)}, bf16[32,512]{1,0:T(8,128)(2,...) custom-call(s32[1]{0:T(128)} %bitcast.own_ref, ...), custom_call_target="tpu_custom_call" | custom-call | tf_op jit(solution)/shard_map/pallas_call | solution.py:478
  67.2 1.3 copy-done
  68.5 1.5 %shard_map.196 = bf16[64,120,128]{2,1,0:T(8,128)(2,1)} custom-call(bf16[17,112,512]{2,1,0:T(8,128)(2,1)S(1)} %get-tuple-element.114.keep_ref, bf16[17,112,512]{2,1,0:T(8,128)(2,1)S(1)} %collective-permute-done.21.recv_ref), custom_call_target="tpu_custom_call" | custom-call | tf_op jit(solution)/shard_map/pallas_call | solution.py:478
  70.0 8.2 %all-to-all-start.1 = ((bf16[64,120,128]{2,1,0:T(8,128)(2,1)}), bf16[64,120,128]{2,1,0:T(8,128)(2,1)S(1)}, u32[]{:S(2)}, u32[]{:S(2)}) async-start(bf16[64,120,128]{2,1,0:T(8,128)(2,1)} %shard_map.196), calls=%async_computation.1 | async-start | bytes 3932160 | tf_op jit(solution)/shard_map/all_to_all | solution.py:507
  78.2 1.5 %copy-done.1 = bf16[17,112,512]{2,1,0:T(8,128)(2,1)S(1)} copy-done((bf16[17,112,512]{2,1,0:T(8,128)(2,1)S(1)}, bf16[17,112,512]{2,1,0:T(8,128)(2,1)}, u32[]{:S(2)}) %copy-start.1) | copy-done | bytes 1949720
  79.7 3.0 %shard_map.195 = bf16[64,120,128]{2,1,0:T(8,128)(2,1)} custom-call(bf16[17,112,512]{2,1,0:T(8,128)(2,1)S(1)} %copy-done.1, bf16[17,112,512]{2,1,0:T(8,128)(2,1)} %collective-permute-done.20.recv_ref), custom_call_target="tpu_custom_call" | custom-call | tf_op jit(solution)/shard_map/pallas_call | solution.py:478
  82.8 24.3 %all-to-all-done.1.x_ref = bf16[64,120,128]{2,1,0:T(8,128)(2,1)S(1)} async-done(((bf16[64,120,128]{2,1,0:T(8,128)(2,1)}), bf16[64,120,128]{2,1,0:T(8,128)(2,1)S(1)}, u32[]{:S(2)}, u32[]{:S(2)}) %all-to-all-start.1) | async-done | bytes 1966112 | tf_op jit(solution)/shard_map/all_to_all | solution.py:507
  107.1 6.3 %all-to-all-start = ((bf16[64,120,128]{2,1,0:T(8,128)(2,1)}), bf16[64,120,128]{2,1,0:T(8,128)(2,1)}, u32[]{:S(2)}, u32[]{:S(2)}) async-start(bf16[64,120,128]{2,1,0:T(8,128)(2,1)} %shard_map.195), calls=%async_computation | async-start | bytes 3932160 | tf_op jit(solution)/shard_map/all_to_all | solution.py:507
  113.5 5.2 %collective-permute-start.16 = (bf16[32,512]{1,0:T(8,128)(2,1)S(1)}, bf16[32,512]{1,0:T(8,128)(2,1)S(1)}, u32[]{:S(2)}, u32[]{:S(2)}) collective-permute-start(bf16[32,512]{1,0:T(8,128)(2,1)S(1)} %get-tuple-element.108), channel_id=1, source_target_pairs={{124,0},{8,4},{4,8},{16,12},{12,16},{24,20},{20,24},{32,28},{28,32... | collective-permute-start | bytes 98312 | tf_op jit(solution)/shard_map/ppermute | solution.py:459
  119.5 1.2 collective-permute-start.18
  121.3 15.7 %collective-permute-done.16.r1 = bf16[32,512]{1,0:T(8,128)(2,1)S(1)} collective-permute-done((bf16[32,512]{1,0:T(8,128)(2,1)S(1)}, bf16[32,512]{1,0:T(8,128)(2,1)S(1)}, u32[]{:S(2)}, u32[]{:S(2)}) %collective-permute-start.16) | collective-permute-done | bytes 32800 | tf_op jit(solution)/shard_map/ppermute | solution.py:459
  137.1 2.5 %collective-permute-done.18.r3 = bf16[32,512]{1,0:T(8,128)(2,1)S(1)} collective-permute-done((bf16[32,512]{1,0:T(8,128)(2,1)S(1)}, bf16[32,512]{1,0:T(8,128)(2,1)S(1)}, u32[]{:S(2)}, u32[]{:S(2)}) %collective-permute-start.18) | collective-permute-done | bytes 32800 | tf_op jit(solution)/shard_map/ppermute | solution.py:459
  139.6 1.0 shard_map.194
  141.4 2.6 %shard_map.198 = (f32[12,2,512]{2,1,0:T(2,128)}, f32[2,4,512]{2,1,0:T(4,128)}, f32[2,8,512]{2,1,0:T(8,128)}, f32[2,4,512]{2,1,0:T(4,128)}, f32[2,4]{1,0:T(2,128)}, /*index=5*/f32[2,4]{1,0:T(2,128)}) custom-call(s32[1]{0:T(128)} %bitcast.3.device_ref, bf16[64,120,128]{2,1,0:T(8,128)(2,1)} %all-to-all-done.x0_ref, f32[120,128]{1,0:T(8,128)S(1)} %get-tuple-element.116.total1, ...), custom_call_target="tpu_custom_call" | custom-call | tf_op jit(solution)/shard_map/pallas_call | solution.py:478
  (31 shorter events, 4.0 us)
Async XLA Ops:
  1.8 7.8 %collective-permute-start.1 = (bf16[64,512]{1,0:T(8,128)(2,1)S(1)}, bf16[64,512]{1,0:T(8,128)(2,1)S(1)}, u32[]{:S(2)}, u32[]{:S(2)}) collective-permute-start(bf16[64,512]{1,0:T(8,128)(2,1)S(1)} %get-tuple-element.79), channel_id=1, source_target_pairs={{124,0},{8,4},{4,8},{16,12},{12,16},{24,20},{20,24},{32,28},{28,32... | collective-permute-start | bytes 196616 | tf_op jit(solution)/shard_map/ppermute | solution.py:459
  9.7 7.8 %collective-permute-start.3 = (bf16[64,512]{1,0:T(8,128)(2,1)S(1)}, bf16[64,512]{1,0:T(8,128)(2,1)S(1)}, u32[]{:S(2)}, u32[]{:S(2)}) collective-permute-start(bf16[64,512]{1,0:T(8,128)(2,1)S(1)} %collective-permute-done.1.b1), channel_id=1, source_target_pairs={{4,0},{0,4},{12,8},{8,12},{20,16},{16,20},{28,24},{24,28},{36,32},... | collective-permute-start | bytes 196616 | tf_op jit(solution)/shard_map/ppermute | solution.py:459
  9.7 6.4 %collective-permute-start = (bf16[32,512]{1,0:T(8,128)(2,1)S(1)}, bf16[32,512]{1,0:T(8,128)(2,1)S(1)}, u32[]{:S(2)}, u32[]{:S(2)}) collective-permute-start(bf16[32,512]{1,0:T(8,128)(2,1)S(1)} %get-tuple-element.78), channel_id=1, source_target_pairs={{4,0},{0,4},{12,8},{8,12},{20,16},{16,20},{28,24},{24,28},{36,32},... | collective-permute-start | bytes 98312 | tf_op jit(solution)/shard_map/ppermute | solution.py:459
  10.2 7.2 %collective-permute-start.2 = (bf16[32,512]{1,0:T(8,128)(2,1)S(1)}, bf16[32,512]{1,0:T(8,128)(2,1)S(1)}, u32[]{:S(2)}, u32[]{:S(2)}) collective-permute-start(bf16[32,512]{1,0:T(8,128)(2,1)S(1)} %get-tuple-element.80), channel_id=1, source_target_pairs={{120,0},{12,4},{0,8},{20,12},{8,16},{28,20},{16,24},{36,28},{24,32... | collective-permute-start | bytes 98312 | tf_op jit(solution)/shard_map/ppermute | solution.py:459
  10.2 7.2 %collective-permute-start.4 = (bf16[32,512]{1,0:T(8,128)(2,1)S(1)}, bf16[32,512]{1,0:T(8,128)(2,1)S(1)}, u32[]{:S(2)}, u32[]{:S(2)}) collective-permute-start(bf16[32,512]{1,0:T(8,128)(2,1)S(1)} %get-tuple-element.81), channel_id=1, source_target_pairs={{64,0},{68,4},{72,8},{76,12},{80,16},{84,20},{88,24},{92,28},{96,3... | collective-permute-start | bytes 98312 | tf_op jit(solution)/shard_map/ppermute | solution.py:459
  21.4 7.1 %collective-permute-start.6 = (bf16[64,512]{1,0:T(8,128)(2,1)S(1)}, bf16[64,512]{1,0:T(8,128)(2,1)S(1)}, u32[]{:S(2)}, u32[]{:S(2)}) collective-permute-start(bf16[64,512]{1,0:T(8,128)(2,1)S(1)} %get-tuple-element.92), channel_id=1, source_target_pairs={{124,0},{8,4},{4,8},{16,12},{12,16},{24,20},{20,24},{32,28},{28,32... | collective-permute-start | bytes 196616 | tf_op jit(solution)/shard_map/ppermute | solution.py:459
  28.5 7.8 %collective-permute-start.8 = (bf16[64,512]{1,0:T(8,128)(2,1)S(1)}, bf16[64,512]{1,0:T(8,128)(2,1)S(1)}, u32[]{:S(2)}, u32[]{:S(2)}) collective-permute-start(bf16[64,512]{1,0:T(8,128)(2,1)S(1)} %collective-permute-done.6.b1), channel_id=1, source_target_pairs={{4,0},{0,4},{12,8},{8,12},{20,16},{16,20},{28,24},{24,28},{36,32},... | collective-permute-start | bytes 196616 | tf_op jit(solution)/shard_map/ppermute | solution.py:459
  28.5 4.5 %collective-permute-start.5 = (bf16[32,512]{1,0:T(8,128)(2,1)S(1)}, bf16[32,512]{1,0:T(8,128)(2,1)S(1)}, u32[]{:S(2)}, u32[]{:S(2)}) collective-permute-start(bf16[32,512]{1,0:T(8,128)(2,1)S(1)} %get-tuple-element.91), channel_id=1, source_target_pairs={{4,0},{0,4},{12,8},{8,12},{20,16},{16,20},{28,24},{24,28},{36,32},... | collective-permute-start | bytes 98312 | tf_op jit(solution)/shard_map/ppermute | solution.py:459
  29.0 7.2 %collective-permute-start.7 = (bf16[32,512]{1,0:T(8,128)(2,1)S(1)}, bf16[32,512]{1,0:T(8,128)(2,1)S(1)}, u32[]{:S(2)}, u32[]{:S(2)}) collective-permute-start(bf16[32,512]{1,0:T(8,128)(2,1)S(1)} %get-tuple-element.93), channel_id=1, source_target_pairs={{120,0},{12,4},{0,8},{20,12},{8,16},{28,20},{16,24},{36,28},{24,32... | collective-permute-start | bytes 98312 | tf_op jit(solution)/shard_map/ppermute | solution.py:459
  29.0 7.2 %collective-permute-start.9 = (bf16[32,512]{1,0:T(8,128)(2,1)S(1)}, bf16[32,512]{1,0:T(8,128)(2,1)S(1)}, u32[]{:S(2)}, u32[]{:S(2)}) collective-permute-start(bf16[32,512]{1,0:T(8,128)(2,1)S(1)} %get-tuple-element.94), channel_id=1, source_target_pairs={{64,0},{68,4},{72,8},{76,12},{80,16},{84,20},{88,24},{92,28},{96,3... | collective-permute-start | bytes 98312 | tf_op jit(solution)/shard_map/ppermute | solution.py:459
  45.7 22.8 %collective-permute-start.21 = (bf16[17,112,512]{2,1,0:T(8,128)(2,1)S(1)}, bf16[17,112,512]{2,1,0:T(8,128)(2,1)S(1)}, u32[]{:S(2)}, u32[]{:S(2)}) collective-permute-start(bf16[17,112,512]{2,1,0:T(8,128)(2,1)S(1)} %get-tuple-element.115), channel_id=1, source_target_pairs={{0,4},{4,0},{8,12},{12,8},{16,20},{20,16},{24,28},{28,24},{32,36},... | collective-permute-start | bytes 5849096 | tf_op jit(solution)/shard_map/ppermute | solution.py:503
  46.9 4.8 %collective-permute-start.10 = (bf16[32,512]{1,0:T(8,128)(2,1)S(1)}, bf16[32,512]{1,0:T(8,128)(2,1)S(1)}, u32[]{:S(2)}, u32[]{:S(2)}) collective-permute-start(bf16[32,512]{1,0:T(8,128)(2,1)S(1)} %get-tuple-element.97), channel_id=1, source_target_pairs={{4,0},{0,4},{12,8},{8,12},{20,16},{16,20},{28,24},{24,28},{36,32},... | collective-permute-start | bytes 98312 | tf_op jit(solution)/shard_map/ppermute | solution.py:459
  47.0 6.7 %collective-permute-start.11 = (bf16[32,512]{1,0:T(8,128)(2,1)S(1)}, bf16[32,512]{1,0:T(8,128)(2,1)S(1)}, u32[]{:S(2)}, u32[]{:S(2)}) collective-permute-start(bf16[32,512]{1,0:T(8,128)(2,1)S(1)} %get-tuple-element.98), channel_id=1, source_target_pairs={{124,0},{8,4},{4,8},{16,12},{12,16},{24,20},{20,24},{32,28},{28,32... | collective-permute-start | bytes 98312 | tf_op jit(solution)/shard_map/ppermute | solution.py:459
  49.7 4.0 %collective-permute-start.12 = (bf16[32,512]{1,0:T(8,128)(2,1)S(1)}, bf16[32,512]{1,0:T(8,128)(2,1)S(1)}, u32[]{:S(2)}, u32[]{:S(2)}) collective-permute-start(bf16[32,512]{1,0:T(8,128)(2,1)S(1)} %get-tuple-element.99), channel_id=1, source_target_pairs={{8,0},{124,4},{16,8},{4,12},{24,16},{12,20},{32,24},{20,28},{40,32... | collective-permute-start | bytes 98312 | tf_op jit(solution)/shard_map/ppermute | solution.py:459
  50.0 7.5 %collective-permute-start.13 = (bf16[32,512]{1,0:T(8,128)(2,1)S(1)}, bf16[32,512]{1,0:T(8,128)(2,1)S(1)}, u32[]{:S(2)}, u32[]{:S(2)}) collective-permute-start(bf16[32,512]{1,0:T(8,128)(2,1)S(1)} %get-tuple-element.100), channel_id=1, source_target_pairs={{120,0},{12,4},{0,8},{20,12},{8,16},{28,20},{16,24},{36,28},{24,32... | collective-permute-start | bytes 98312 | tf_op jit(solution)/shard_map/ppermute | solution.py:459
  51.7 5.8 %collective-permute-start.14 = (bf16[32,512]{1,0:T(8,128)(2,1)S(1)}, bf16[32,512]{1,0:T(8,128)(2,1)S(1)}, u32[]{:S(2)}, u32[]{:S(2)}) collective-permute-start(bf16[32,512]{1,0:T(8,128)(2,1)S(1)} %get-tuple-element.101), channel_id=1, source_target_pairs={{64,0},{68,4},{72,8},{76,12},{80,16},{84,20},{88,24},{92,28},{96,3... | collective-permute-start | bytes 98312 | tf_op jit(solution)/shard_map/ppermute | solution.py:459
  67.2 1.3 copy-start
  68.5 9.7 %collective-permute-start.20 = (bf16[17,112,512]{2,1,0:T(8,128)(2,1)}, bf16[17,112,512]{2,1,0:T(8,128)(2,1)}, u32[]{:S(2)}, u32[]{:S(2)}) collective-permute-start(bf16[17,112,512]{2,1,0:T(8,128)(2,1)} %get-tuple-element.113), channel_id=1, source_target_pairs={{0,4},{4,0},{8,12},{12,8},{16,20},{20,16},{24,28},{28,24},{32,36},... | collective-permute-start | bytes 5849096 | tf_op jit(solution)/shard_map/ppermute | solution.py:503
  70.0 37.1 %all-to-all-start.1 = ((bf16[64,120,128]{2,1,0:T(8,128)(2,1)}), bf16[64,120,128]{2,1,0:T(8,128)(2,1)S(1)}, u32[]{:S(2)}, u32[]{:S(2)}) async-start(bf16[64,120,128]{2,1,0:T(8,128)(2,1)} %shard_map.196), calls=%async_computation.1 | async-start | bytes 3932160 | tf_op jit(solution)/shard_map/all_to_all | solution.py:507
  78.2 1.5 %copy-start.1 = (bf16[17,112,512]{2,1,0:T(8,128)(2,1)S(1)}, bf16[17,112,512]{2,1,0:T(8,128)(2,1)}, u32[]{:S(2)}) copy-start(bf16[17,112,512]{2,1,0:T(8,128)(2,1)} %copy-done) | copy-start | bytes 5849092
  107.1 34.3 %all-to-all-start = ((bf16[64,120,128]{2,1,0:T(8,128)(2,1)}), bf16[64,120,128]{2,1,0:T(8,128)(2,1)}, u32[]{:S(2)}, u32[]{:S(2)}) async-start(bf16[64,120,128]{2,1,0:T(8,128)(2,1)} %shard_map.195), calls=%async_computation | async-start | bytes 3932160 | tf_op jit(solution)/shard_map/all_to_all | solution.py:507
  113.4 8.0 %collective-permute-start.15 = (bf16[32,512]{1,0:T(8,128)(2,1)S(1)}, bf16[32,512]{1,0:T(8,128)(2,1)S(1)}, u32[]{:S(2)}, u32[]{:S(2)}) collective-permute-start(bf16[32,512]{1,0:T(8,128)(2,1)S(1)} %get-tuple-element.107), channel_id=1, source_target_pairs={{4,0},{0,4},{12,8},{8,12},{20,16},{16,20},{28,24},{24,28},{36,32},... | collective-permute-start | bytes 98312 | tf_op jit(solution)/shard_map/ppermute | solution.py:459
  113.5 23.6 %collective-permute-start.16 = (bf16[32,512]{1,0:T(8,128)(2,1)S(1)}, bf16[32,512]{1,0:T(8,128)(2,1)S(1)}, u32[]{:S(2)}, u32[]{:S(2)}) collective-permute-start(bf16[32,512]{1,0:T(8,128)(2,1)S(1)} %get-tuple-element.108), channel_id=1, source_target_pairs={{124,0},{8,4},{4,8},{16,12},{12,16},{24,20},{20,24},{32,28},{28,32... | collective-permute-start | bytes 98312 | tf_op jit(solution)/shard_map/ppermute | solution.py:459
  118.7 18.4 %collective-permute-start.17 = (bf16[32,512]{1,0:T(8,128)(2,1)S(1)}, bf16[32,512]{1,0:T(8,128)(2,1)S(1)}, u32[]{:S(2)}, u32[]{:S(2)}) collective-permute-start(bf16[32,512]{1,0:T(8,128)(2,1)S(1)} %get-tuple-element.109), channel_id=1, source_target_pairs={{8,0},{124,4},{16,8},{4,12},{24,16},{12,20},{32,24},{20,28},{40,32... | collective-permute-start | bytes 98312 | tf_op jit(solution)/shard_map/ppermute | solution.py:459
  119.5 20.1 %collective-permute-start.18 = (bf16[32,512]{1,0:T(8,128)(2,1)S(1)}, bf16[32,512]{1,0:T(8,128)(2,1)S(1)}, u32[]{:S(2)}, u32[]{:S(2)}) collective-permute-start(bf16[32,512]{1,0:T(8,128)(2,1)S(1)} %get-tuple-element.110), channel_id=1, source_target_pairs={{120,0},{12,4},{0,8},{20,12},{8,16},{28,20},{16,24},{36,28},{24,32... | collective-permute-start | bytes 98312 | tf_op jit(solution)/shard_map/ppermute | solution.py:459
  120.7 18.9 %collective-permute-start.19 = (bf16[32,512]{1,0:T(8,128)(2,1)S(1)}, bf16[32,512]{1,0:T(8,128)(2,1)S(1)}, u32[]{:S(2)}, u32[]{:S(2)}) collective-permute-start(bf16[32,512]{1,0:T(8,128)(2,1)S(1)} %get-tuple-element.111), channel_id=1, source_target_pairs={{64,0},{68,4},{72,8},{76,12},{80,16},{84,20},{88,24},{92,28},{96,3... | collective-permute-start | bytes 98312 | tf_op jit(solution)/shard_map/ppermute | solution.py:459

commit v5 on v4

--- a/solution.py
+++ b/solution.py
@@ -8,7 +8,6 @@
 
 EPSILON = 1e-05
 CHUNK = 512
-ORDER = (4, 2, 3, 1, 0)
 F32 = jnp.float32
 BF16 = jnp.bfloat16
 
@@ -73,9 +72,10 @@
 
 
 def returned(lists_ref, own, blocks):
+    swap, pair, side, far = blocks
     total = None
-    for reader, block in zip(readers(own), blocks):
-        term = nn(list_onehot(lists_ref, reader, 128), block[...])
+    for reader, (block, at) in zip(readers(own), ((swap, 0), (pair, 0), (side, 0), (pair, 32), (far, 0))):
+        term = nn(list_onehot(lists_ref, reader, 128), block[at : at + 32, :])
         total = term if total is None else total + term
     return total
 
@@ -253,8 +253,9 @@
     g_in[512:1024, :] = tn(senders[...], at_sender).astype(BF16)
     g_in[1024:1536, :] = tn(vb, at_receiver).astype(BF16)
     back = nt(at_sender, we_in[512:1024, :])
-    for n, out in enumerate(outs):
-        out[...] = back[128 + 32 * n : 160 + 32 * n, :].astype(BF16)
+    swap, pair, side, far = outs
+    for n, (out, at) in enumerate(((swap, 0), (pair, 0), (side, 0), (swap, 32), (far, 0))):
+        out[at : at + 32, :] = back[128 + 32 * n : 160 + 32 * n, :].astype(BF16)
     return nt(at_receiver, we_in[1024:1536, :]) + back[0:128, :]
 
 
@@ -268,7 +269,7 @@
 
 def middle_kernel(
     own_ref, count_ref, state, onehot, eb, cot, we_in, we_out, wn_in, wn_out, e_gain, n_gain, part, near, b0, b1, b2, b3, b4,
-    node_out, edge_grad_out, grad_out, keep, send, o0, o1, o2, o3, o4,
+    node_out, edge_grad_out, grad_out, keep, send, o0, o1, o2, o3,
     v, edge_grad, senders, proj, message, pre_s, normed_s, inv_s, hidden_s, dz_s, da_s, g_in, g_out, gn_in, gn_out, sems,
 ):
     own, count = own_ref[0], count_ref[0]
@@ -311,16 +312,16 @@
         edge_grad[rows, :] = nt(da, we_in[0:512, :]).astype(BF16)
         at = pl.ds(n * CHUNK, CHUNK)
         saves += copies.start((edge_grad.at[at], edge_grad_out.at[at]))
-    grad_ends = edge_tail(onehot, senders, vb, eb, hidden_s, dz_s, da_s, we_in, g_in, g_out, (o0, o1, o2, o3, o4))
+    grad_ends = edge_tail(onehot, senders, vb, eb, hidden_s, dz_s, da_s, we_in, g_in, g_out, (o0, o1, o2, o3))
     grad_out[...] = grad + grad_v + grad_ends
     write_grads(own & 1, g_in, g_out, gn_in, gn_out, grad_e_gain, grad_n_gain, keep, send)
     wait(saves)
 
 
 def backward_kernel(
-    own_ref, count_ref, lists, onehot, grad_ref, r0, r1, r2, r3, r4, eb_ref, state_ref, sides_ref, edge_grad_ref, saved_ref, inv_ref,
+    own_ref, count_ref, lists, onehot, grad_ref, r0, r1, r2, r3, eb_ref, state_ref, sides_ref, edge_grad_ref, saved_ref, inv_ref,
     we_in_ref, we_out_ref, wn_in_ref, wn_out_ref, e_gain_ref, n_gain_ref,
-    grad_out, keep, send, o0, o1, o2, o3, o4,
+    grad_out, keep, send, o0, o1, o2, o3,
     eb, state, sides, edge_grad, saved, inv_s, we_in, we_out, wn_in, wn_out, e_gain, n_gain,
     hidden_s, dz_s, da_s, g_in, g_out, gn_in, gn_out, sems,
 ):
@@ -332,7 +333,7 @@
     last = copies.start((eb_ref.at[0], eb), (we_in_ref.at[0], we_in))
     wait(node)
     vb = sides[0:128, :]
-    grad = grad_ref[...] + returned(lists, own, (r0, r1, r2, r3, r4))
+    grad = grad_ref[...] + returned(lists, own, (r0, r1, r2, r3))
     n_pre = state[0]
     n_hidden = (n_pre * sigmoid(n_pre)).astype(BF16)
     grad_n_gain, grad_v, grad_agg = node_backward(
@@ -355,7 +356,7 @@
         hidden_s[rows, :] = (pre * s).astype(BF16)
         da_s[rows, :] = (nt(dz, we_out[...]) * (s * (1.0 + pre * (1.0 - s)))).astype(BF16)
     wait(last)
-    grad_ends = edge_tail(onehot, sides.at[0:288], vb, eb, hidden_s, dz_s, da_s, we_in, g_in, g_out, (o0, o1, o2, o3, o4))
+    grad_ends = edge_tail(onehot, sides.at[0:288], vb, eb, hidden_s, dz_s, da_s, we_in, g_in, g_out, (o0, o1, o2, o3))
     grad_out[...] = grad + grad_v + grad_ends
     write_grads(own & 1, g_in, g_out, gn_in, gn_out, grad_e_gain, grad_n_gain, keep, send)
 
@@ -402,8 +403,8 @@
     gains_ref[...] = pick_gains(out_ref[112:120, :], device_ref[0])
 
 
-def node_grad_kernel(own_ref, lists, grad_ref, r0, r1, r2, r3, r4, out_ref, total, sems):
-    total[...] = grad_ref[...] + returned(lists, own_ref[0], (r0, r1, r2, r3, r4))
+def node_grad_kernel(own_ref, lists, grad_ref, r0, r1, r2, r3, out_ref, total, sems):
+    total[...] = grad_ref[...] + returned(lists, own_ref[0], (r0, r1, r2, r3))
     wait(Copies(sems).start((total, out_ref.at[0])))
 
 
@@ -465,10 +466,10 @@
         return swap, pair, side, move(pair, lambda i: i ^ 1), far
 
     def give_back(blocks):
-        outs = {}
-        for n in ORDER:
-            outs[n] = move(blocks[n], lambda i, n=n: readers(i)[n])
-        return [outs[n] for n in range(5)]
+        swap, pair, side, far = blocks
+        swap = move(swap, lambda i: i ^ 1)
+        side, far = move(side, lambda i: near(i ^ 1)), move(far, lambda i: i ^ 16)
+        return swap, move(jnp.concatenate([pair, swap[32:64]], axis=0), near), side, far
 
     def call(kernel, mib, outs, scratch, specs, args):
         at = {id(hbm): pltpu.HBM, id(kept): pltpu.VMEM}
@@ -512,7 +513,7 @@
     weights_out = [ob16(*w.shape[1:]) for w in weights]
     edge_b, edge_f = vb16(edges, width), vf32(edges, width)
     grads_s = [vb16(r, width) for r in (1536, 512, 1024, 512)]
-    blocks_out = [(sds((32, width), BF16), vmem)] * 5
+    back_out = [(sds((r, width), BF16), vmem) for r in (64, 32, 32, 32)]
     fetch_out = [(sds((r, width), BF16), vmem) for r in (32, 64, 32, 32)]
     half = (sds((17, 112, width), BF16), vmem)
 
@@ -550,7 +551,7 @@
     node_out, edge_grad, grad1, keep1, send1, *back1 = call(
         middle_kernel,
         20,
-        [(sds((1, nodes, width), F32), hbm), (sds((edges, width), BF16), hbm), of32(nodes, width), half, half] + blocks_out,
+        [(sds((1, nodes, width), F32), hbm), (sds((edges, width), BF16), hbm), of32(nodes, width), half, half] + back_out,
         [vf32(nodes, width), edge_b, vb16(288, width), vb16(512, width), edge_b, edge_f, edge_f, vf32(edges, 128), edge_b, edge_b, edge_b] + grads_s + [sems(8)],
         [smem, smem] + [kept] * 12 + [vmem] * 5,
         (own_arr, edge_count, state, onehot, eb1, cot, we_in1, we_out1, wn_in1, wn_out1, e_gain, n_gain, part1, near1, *senders1),
@@ -563,9 +564,9 @@
     grad0, keep0, send0, *back0 = call(
         backward_kernel,
         22,
-        [(sds((nodes, width), F32), vmem), half, half] + blocks_out,
+        [(sds((nodes, width), F32), vmem), half, half] + back_out,
         [edge_b, vf32(3, nodes, width), vb16(416, width), edge_b, vb16(2, edges, width), vf32(edges, 128)] + weights_s + [edge_b, edge_b, edge_b] + grads_s + [sems(12)],
-        [smem, smem, kept, kept] + [vmem] * 6 + [hbm, free, free] + [hbm] * 9,
+        [smem, smem, kept, kept] + [vmem] * 5 + [hbm, free, free] + [hbm] * 9,
         (own_arr, edge_count, lists, onehot, grad1, *returned1, edge_latent, state, sides, edge_grad, saved, inv, *weights, edge_gain, node_gain),
     )
     returned0 = give_back(back0)
@@ -576,7 +577,7 @@
     )
     (node_grad,) = call(
         node_grad_kernel, 2, [(sds((1, nodes, width), F32), hbm)], [vf32(nodes, width), sems(1)],
-        [smem, kept, vmem] + [vmem] * 5, (own_arr, lists, grad0, *returned0),
+        [smem, kept, vmem] + [vmem] * 4, (own_arr, lists, grad0, *returned0),
     )
     g_e_in, *grads = call(
         finish_kernel,

time: 144 us -> 146 us (1.014)
  waiting for transfers between devices: 57.8 us -> 63 us
  starting transfers between devices: 43.2 us -> 39.2 us
    ppermute x20 -> x18, waiting for transfers between devices: 33.5 us -> 37.2 us  [move(): return lax.ppermute(block, 'graph', [(source(i), i) for i in range(graph)])]
    ppermute x20 -> x18, starting transfers between devices: 27.5 us -> 24.3 us  [move(): return lax.ppermute(block, 'graph', [(source(i), i) for i in range(graph)])]
  transfers between devices with their start and end apart: 24 -> 22, of which waited for: 9 -> 12; matrix products, arithmetic and copies ran while one was open for 0% -> 0% of each run, Pallas kernels for 15% -> 15%
where the time goes in v5:
time: 146 us; the launch traced here: 145 us
  waiting for transfers between devices  63 us (43%)
  starting transfers between devices  39.2 us (27%)
  Pallas kernels  38.8 us (27%)
  local copies, waits for them, and re-layouts  2.83 us (2%)
  between operations  1.46 us (1%)
    pallas_call x11, Pallas kernels, call(): pl.pallas_call(kernel, out_shape=shapes, in_specs=[real.get(id(p), p) for...  38.8 us
    ppermute x18, waiting for transfers between devices, move(): return lax.ppermute(block, 'graph', [(source(i), i) for i in range(graph)])  37.2 us
    all_to_all x2, waiting for transfers between devices, spread(): lax.all_to_all(packed, ('graph', 'batch'), 0, 0, tiled=True, axis_index_g...  25.8 us
    ppermute x18, starting transfers between devices, move(): return lax.ppermute(block, 'graph', [(source(i), i) for i in range(graph)])  24.3 us
    all_to_all x2, starting transfers between devices, spread(): lax.all_to_all(packed, ('graph', 'batch'), 0, 0, tiled=True, axis_index_g...  13.8 us
  transfers between devices with their start and end apart: 22, of which 12 were waited for; matrix products, arithmetic and copies ran while one was open for 0% of the time, Pallas kernels for 15%

profile of v5, /device:TPU:0, one launch (start us, length us, event | category | flops | bytes accessed | tf_op | source)
XLA Modules:
  0.0 145.3 jit_solution(11053092430016788485)
XLA Ops:
  0.6 1.2 shard_map.188
  1.8 5.9 %collective-permute-start.1 = (bf16[64,512]{1,0:T(8,128)(2,1)S(1)}, bf16[64,512]{1,0:T(8,128)(2,1)S(1)}, u32[]{:S(2)}, u32[]{:S(2)}) collective-permute-start(bf16[64,512]{1,0:T(8,128)(2,1)S(1)} %get-tuple-element.77), channel_id=1, source_target_pairs={{124,0},{8,4},{4,8},{16,12},{12,16},{24,20},{20,24},{32,28},{28,32... | collective-permute-start | bytes 196616 | tf_op jit(solution)/shard_map/ppermute | solution.py:460
  7.7 2.0 %collective-permute-done.1.b1 = bf16[64,512]{1,0:T(8,128)(2,1)S(1)} collective-permute-done((bf16[64,512]{1,0:T(8,128)(2,1)S(1)}, bf16[64,512]{1,0:T(8,128)(2,1)S(1)}, u32[]{:S(2)}, u32[]{:S(2)}) %collective-permute-start.1) | collective-permute-done | bytes 65568 | tf_op jit(solution)/shard_map/ppermute | solution.py:460
  10.2 2.1 %collective-permute-start.4 = (bf16[32,512]{1,0:T(8,128)(2,1)S(1)}, bf16[32,512]{1,0:T(8,128)(2,1)S(1)}, u32[]{:S(2)}, u32[]{:S(2)}) collective-permute-start(bf16[32,512]{1,0:T(8,128)(2,1)S(1)} %get-tuple-element.79), channel_id=1, source_target_pairs={{64,0},{68,4},{72,8},{76,12},{80,16},{84,20},{88,24},{92,28},{96,3... | collective-permute-start | bytes 98312 | tf_op jit(solution)/shard_map/ppermute | solution.py:460
  12.9 3.2 %shard_map.189 = (bf16[512,1024]{1,0:T(8,128)(2,1)S(1)}, bf16[1024,512]{1,0:T(8,128)(2,1)S(1)}, bf16[1536,512]{1,0:T(8,128)(2,1)S(1)}, bf16[512,512]{1,0:T(8,128...) custom-call(s32[1]{0:T(128)} %bitcast.own_ref, ...), custom_call_target="tpu_custom_call" | custom-call | tf_op jit(solution)/shard_map/pallas_call | solution.py:479
  16.1 1.3 collective-permute-done.2.b2
  17.4 4.0 %shard_map.190 = (f32[4,128,512]{2,1,0:T(8,128)S(1)}, bf16[416,512]{1,0:T(8,128)(2,1)S(1)}, bf16[1024,512]{1,0:T(8,128)(2,1)S(1)}, bf16[2,1024,512]{2,1,0:T(8,12...) custom-call(s32[1]{0:T(128)} %bitcast.own_ref, ...), custom_call_target="tpu_custom_call" | custom-call | tf_op jit(solution)/shard_map/pallas_call | solution.py:479
  21.4 4.0 %collective-permute-start.6 = (bf16[64,512]{1,0:T(8,128)(2,1)S(1)}, bf16[64,512]{1,0:T(8,128)(2,1)S(1)}, u32[]{:S(2)}, u32[]{:S(2)}) collective-permute-start(bf16[64,512]{1,0:T(8,128)(2,1)S(1)} %get-tuple-element.90), channel_id=1, source_target_pairs={{124,0},{8,4},{4,8},{16,12},{12,16},{24,20},{20,24},{32,28},{28,32... | collective-permute-start | bytes 196616 | tf_op jit(solution)/shard_map/ppermute | solution.py:460
  25.4 3.1 %collective-permute-done.6.b1 = bf16[64,512]{1,0:T(8,128)(2,1)S(1)} collective-permute-done((bf16[64,512]{1,0:T(8,128)(2,1)S(1)}, bf16[64,512]{1,0:T(8,128)(2,1)S(1)}, u32[]{:S(2)}, u32[]{:S(2)}) %collective-permute-start.6) | collective-permute-done | bytes 65568 | tf_op jit(solution)/shard_map/ppermute | solution.py:460
  29.0 1.7 %collective-permute-start.9 = (bf16[32,512]{1,0:T(8,128)(2,1)S(1)}, bf16[32,512]{1,0:T(8,128)(2,1)S(1)}, u32[]{:S(2)}, u32[]{:S(2)}) collective-permute-start(bf16[32,512]{1,0:T(8,128)(2,1)S(1)} %get-tuple-element.92), channel_id=1, source_target_pairs={{64,0},{68,4},{72,8},{76,12},{80,16},{84,20},{88,24},{92,28},{96,3... | collective-permute-start | bytes 98312 | tf_op jit(solution)/shard_map/ppermute | solution.py:460
  30.7 2.3 %shard_map.191 = (bf16[128,512]{1,0:T(8,128)(2,1)S(1)}, bf16[1536,512]{1,0:T(8,128)(2,1)S(1)}, bf16[512,512]{1,0:T(8,128)(2,1)S(1)}, bf16[1024,512]{1,0:T(8,128)...) custom-call(f32[4,128,512]{2,1,0:T(8,128)S(1)} %get-tuple-element.80.state.state_ref,, ...), custom_call_target="tpu_custom_call" | custom-call | tf_op jit(solution)/shard_map/pallas_call | solution.py:479
  33.0 3.2 %collective-permute-done.7.b2 = bf16[32,512]{1,0:T(8,128)(2,1)S(1)} collective-permute-done((bf16[32,512]{1,0:T(8,128)(2,1)S(1)}, bf16[32,512]{1,0:T(8,128)(2,1)S(1)}, u32[]{:S(2)}, u32[]{:S(2)}) %collective-permute-start.7) | collective-permute-done | bytes 32800 | tf_op jit(solution)/shard_map/ppermute | solution.py:460
  36.2 9.5 %shard_map.192 = (f32[1,128,512]{2,1,0:T(8,128)}, bf16[1024,512]{1,0:T(8,128)(2,1)}, f32[128,512]{1,0:T(8,128)S(1)}, bf16[17,112,512]{2,1,0:T(8,128)(2,1)S(1)}, ...) custom-call(s32[1]{0:T(128)} %bitcast.own_ref, ...), custom_call_target="tpu_custom_call" | custom-call | tf_op jit(solution)/shard_map/pallas_call | solution.py:479
  45.7 1.2 collective-permute-start.19
  47.0 3.6 %collective-permute-done.10.r0 = bf16[64,512]{1,0:T(8,128)(2,1)S(1)} collective-permute-done((bf16[64,512]{1,0:T(8,128)(2,1)S(1)}, bf16[64,512]{1,0:T(8,128)(2,1)S(1)}, u32[]{:S(2)}, u32[]{:S(2)}) %collective-permute-start.10) | collective-permute-done | bytes 65568 | tf_op jit(solution)/shard_map/ppermute | solution.py:460
  50.6 2.8 %collective-permute-start.11 = (bf16[64,512]{1,0:T(8,128)(2,1)S(1)}, bf16[64,512]{1,0:T(8,128)(2,1)S(1)}, u32[]{:S(2)}, u32[]{:S(2)}) collective-permute-start(bf16[64,512]{1,0:T(8,128)(2,1)S(1)} %pad_maximum_fusion), channel_id=1, source_target_pairs={{124,0},{8,4},{4,8},{16,12},{12,16},{24,20},{20,24},{32,28},{28,32... | collective-permute-start | bytes 196616 | tf_op jit(solution)/shard_map/ppermute | solution.py:460
  53.7 3.6 %collective-permute-done.12.r2 = bf16[32,512]{1,0:T(8,128)(2,1)S(1)} collective-permute-done((bf16[32,512]{1,0:T(8,128)(2,1)S(1)}, bf16[32,512]{1,0:T(8,128)(2,1)S(1)}, u32[]{:S(2)}, u32[]{:S(2)}) %collective-permute-start.12) | collective-permute-done | bytes 32800 | tf_op jit(solution)/shard_map/ppermute | solution.py:460
  57.3 1.8 %collective-permute-done.13.r3 = bf16[32,512]{1,0:T(8,128)(2,1)S(1)} collective-permute-done((bf16[32,512]{1,0:T(8,128)(2,1)S(1)}, bf16[32,512]{1,0:T(8,128)(2,1)S(1)}, u32[]{:S(2)}, u32[]{:S(2)}) %collective-permute-start.13) | collective-permute-done | bytes 32800 | tf_op jit(solution)/shard_map/ppermute | solution.py:460
  59.1 9.8 %shard_map.193 = (f32[128,512]{1,0:T(8,128)S(1)}, bf16[17,112,512]{2,1,0:T(8,128)(2,1)S(1)}, bf16[17,112,512]{2,1,0:T(8,128)(2,1)}, bf16[64,512]{1,0:T(8,128)(2,...) custom-call(s32[1]{0:T(128)} %bitcast.own_ref, ...), custom_call_target="tpu_custom_call" | custom-call | tf_op jit(solution)/shard_map/pallas_call | solution.py:479
  68.9 1.3 copy-done
  70.2 1.5 %shard_map.196 = bf16[64,120,128]{2,1,0:T(8,128)(2,1)} custom-call(bf16[17,112,512]{2,1,0:T(8,128)(2,1)S(1)} %get-tuple-element.110.keep_ref, bf16[17,112,512]{2,1,0:T(8,128)(2,1)S(1)} %collective-permute-done.19.recv_ref), custom_call_target="tpu_custom_call" | custom-call | tf_op jit(solution)/shard_map/pallas_call | solution.py:479
  71.7 7.5 %all-to-all-start.1 = ((bf16[64,120,128]{2,1,0:T(8,128)(2,1)}), bf16[64,120,128]{2,1,0:T(8,128)(2,1)S(1)}, u32[]{:S(2)}, u32[]{:S(2)}) async-start(bf16[64,120,128]{2,1,0:T(8,128)(2,1)} %shard_map.196), calls=%async_computation.1 | async-start | bytes 3932160 | tf_op jit(solution)/shard_map/all_to_all | solution.py:508
  79.2 1.5 %copy-done.1 = bf16[17,112,512]{2,1,0:T(8,128)(2,1)S(1)} copy-done((bf16[17,112,512]{2,1,0:T(8,128)(2,1)S(1)}, bf16[17,112,512]{2,1,0:T(8,128)(2,1)}, u32[]{:S(2)}) %copy-start.1) | copy-done | bytes 1949720
  80.7 3.0 %shard_map.195 = bf16[64,120,128]{2,1,0:T(8,128)(2,1)} custom-call(bf16[17,112,512]{2,1,0:T(8,128)(2,1)S(1)} %copy-done.1, bf16[17,112,512]{2,1,0:T(8,128)(2,1)} %collective-permute-done.18.recv_ref), custom_call_target="tpu_custom_call" | custom-call | tf_op jit(solution)/shard_map/pallas_call | solution.py:479
  83.8 24.3 %all-to-all-done.1.x_ref = bf16[64,120,128]{2,1,0:T(8,128)(2,1)S(1)} async-done(((bf16[64,120,128]{2,1,0:T(8,128)(2,1)}), bf16[64,120,128]{2,1,0:T(8,128)(2,1)S(1)}, u32[]{:S(2)}, u32[]{:S(2)}) %all-to-all-start.1) | async-done | bytes 1966112 | tf_op jit(solution)/shard_map/all_to_all | solution.py:508
  108.1 6.3 %all-to-all-start = ((bf16[64,120,128]{2,1,0:T(8,128)(2,1)}), bf16[64,120,128]{2,1,0:T(8,128)(2,1)}, u32[]{:S(2)}, u32[]{:S(2)}) async-start(bf16[64,120,128]{2,1,0:T(8,128)(2,1)} %shard_map.195), calls=%async_computation | async-start | bytes 3932160 | tf_op jit(solution)/shard_map/all_to_all | solution.py:508
  114.4 1.2 collective-permute-done.14.r0
  115.7 5.0 %collective-permute-start.15 = (bf16[64,512]{1,0:T(8,128)(2,1)S(1)}, bf16[64,512]{1,0:T(8,128)(2,1)S(1)}, u32[]{:S(2)}, u32[]{:S(2)}) collective-permute-start(bf16[64,512]{1,0:T(8,128)(2,1)S(1)} %pad_maximum_fusion.1), channel_id=1, source_target_pairs={{124,0},{8,4},{4,8},{16,12},{12,16},{24,20},{20,24},{32,28},{28,32... | collective-permute-start | bytes 196616 | tf_op jit(solution)/shard_map/ppermute | solution.py:460
  122.1 14.8 %collective-permute-done.16.r2 = bf16[32,512]{1,0:T(8,128)(2,1)S(1)} collective-permute-done((bf16[32,512]{1,0:T(8,128)(2,1)S(1)}, bf16[32,512]{1,0:T(8,128)(2,1)S(1)}, u32[]{:S(2)}, u32[]{:S(2)}) %collective-permute-start.16) | collective-permute-done | bytes 32800 | tf_op jit(solution)/shard_map/ppermute | solution.py:460
  136.9 2.5 %collective-permute-done.17.r3 = bf16[32,512]{1,0:T(8,128)(2,1)S(1)} collective-permute-done((bf16[32,512]{1,0:T(8,128)(2,1)S(1)}, bf16[32,512]{1,0:T(8,128)(2,1)S(1)}, u32[]{:S(2)}, u32[]{:S(2)}) %collective-permute-start.17) | collective-permute-done | bytes 32800 | tf_op jit(solution)/shard_map/ppermute | solution.py:460
  141.3 1.5 %all-to-all-done.x0_ref = bf16[64,120,128]{2,1,0:T(8,128)(2,1)} async-done(((bf16[64,120,128]{2,1,0:T(8,128)(2,1)}), bf16[64,120,128]{2,1,0:T(8,128)(2,1)}, u32[]{:S(2)}, u32[]{:S(2)}) %all-to-all-start) | async-done | bytes 1966112 | tf_op jit(solution)/shard_map/all_to_all | solution.py:508
  142.7 2.6 %shard_map.198 = (f32[12,2,512]{2,1,0:T(2,128)}, f32[2,4,512]{2,1,0:T(4,128)}, f32[2,8,512]{2,1,0:T(8,128)}, f32[2,4,512]{2,1,0:T(4,128)}, f32[2,4]{1,0:T(2,128)}, /*index=5*/f32[2,4]{1,0:T(2,128)}) custom-call(s32[1]{0:T(128)} %bitcast.3.device_ref, bf16[64,120,128]{2,1,0:T(8,128)(2,1)} %all-to-all-done.x0_ref, f32[120,128]{1,0:T(8,128)S(1)} %get-tuple-element.112.total1, ...), custom_call_target="tpu_custom_call" | custom-call | tf_op jit(solution)/shard_map/pallas_call | solution.py:479
  (31 shorter events, 4.9 us)
Async XLA Ops:
  1.8 7.8 %collective-permute-start.1 = (bf16[64,512]{1,0:T(8,128)(2,1)S(1)}, bf16[64,512]{1,0:T(8,128)(2,1)S(1)}, u32[]{:S(2)}, u32[]{:S(2)}) collective-permute-start(bf16[64,512]{1,0:T(8,128)(2,1)S(1)} %get-tuple-element.77), channel_id=1, source_target_pairs={{124,0},{8,4},{4,8},{16,12},{12,16},{24,20},{20,24},{32,28},{28,32... | collective-permute-start | bytes 196616 | tf_op jit(solution)/shard_map/ppermute | solution.py:460
  9.7 7.8 %collective-permute-start.3 = (bf16[64,512]{1,0:T(8,128)(2,1)S(1)}, bf16[64,512]{1,0:T(8,128)(2,1)S(1)}, u32[]{:S(2)}, u32[]{:S(2)}) collective-permute-start(bf16[64,512]{1,0:T(8,128)(2,1)S(1)} %collective-permute-done.1.b1), channel_id=1, source_target_pairs={{4,0},{0,4},{12,8},{8,12},{20,16},{16,20},{28,24},{24,28},{36,32},... | collective-permute-start | bytes 196616 | tf_op jit(solution)/shard_map/ppermute | solution.py:460
  9.7 6.4 %collective-permute-start = (bf16[32,512]{1,0:T(8,128)(2,1)S(1)}, bf16[32,512]{1,0:T(8,128)(2,1)S(1)}, u32[]{:S(2)}, u32[]{:S(2)}) collective-permute-start(bf16[32,512]{1,0:T(8,128)(2,1)S(1)} %get-tuple-element.76), channel_id=1, source_target_pairs={{4,0},{0,4},{12,8},{8,12},{20,16},{16,20},{28,24},{24,28},{36,32},... | collective-permute-start | bytes 98312 | tf_op jit(solution)/shard_map/ppermute | solution.py:460
  10.2 7.2 %collective-permute-start.2 = (bf16[32,512]{1,0:T(8,128)(2,1)S(1)}, bf16[32,512]{1,0:T(8,128)(2,1)S(1)}, u32[]{:S(2)}, u32[]{:S(2)}) collective-permute-start(bf16[32,512]{1,0:T(8,128)(2,1)S(1)} %get-tuple-element.78), channel_id=1, source_target_pairs={{120,0},{12,4},{0,8},{20,12},{8,16},{28,20},{16,24},{36,28},{24,32... | collective-permute-start | bytes 98312 | tf_op jit(solution)/shard_map/ppermute | solution.py:460
  10.2 7.2 %collective-permute-start.4 = (bf16[32,512]{1,0:T(8,128)(2,1)S(1)}, bf16[32,512]{1,0:T(8,128)(2,1)S(1)}, u32[]{:S(2)}, u32[]{:S(2)}) collective-permute-start(bf16[32,512]{1,0:T(8,128)(2,1)S(1)} %get-tuple-element.79), channel_id=1, source_target_pairs={{64,0},{68,4},{72,8},{76,12},{80,16},{84,20},{88,24},{92,28},{96,3... | collective-permute-start | bytes 98312 | tf_op jit(solution)/shard_map/ppermute | solution.py:460
  21.4 7.1 %collective-permute-start.6 = (bf16[64,512]{1,0:T(8,128)(2,1)S(1)}, bf16[64,512]{1,0:T(8,128)(2,1)S(1)}, u32[]{:S(2)}, u32[]{:S(2)}) collective-permute-start(bf16[64,512]{1,0:T(8,128)(2,1)S(1)} %get-tuple-element.90), channel_id=1, source_target_pairs={{124,0},{8,4},{4,8},{16,12},{12,16},{24,20},{20,24},{32,28},{28,32... | collective-permute-start | bytes 196616 | tf_op jit(solution)/shard_map/ppermute | solution.py:460
  28.5 7.8 %collective-permute-start.8 = (bf16[64,512]{1,0:T(8,128)(2,1)S(1)}, bf16[64,512]{1,0:T(8,128)(2,1)S(1)}, u32[]{:S(2)}, u32[]{:S(2)}) collective-permute-start(bf16[64,512]{1,0:T(8,128)(2,1)S(1)} %collective-permute-done.6.b1), channel_id=1, source_target_pairs={{4,0},{0,4},{12,8},{8,12},{20,16},{16,20},{28,24},{24,28},{36,32},... | collective-permute-start | bytes 196616 | tf_op jit(solution)/shard_map/ppermute | solution.py:460
  28.5 4.5 %collective-permute-start.5 = (bf16[32,512]{1,0:T(8,128)(2,1)S(1)}, bf16[32,512]{1,0:T(8,128)(2,1)S(1)}, u32[]{:S(2)}, u32[]{:S(2)}) collective-permute-start(bf16[32,512]{1,0:T(8,128)(2,1)S(1)} %get-tuple-element.89), channel_id=1, source_target_pairs={{4,0},{0,4},{12,8},{8,12},{20,16},{16,20},{28,24},{24,28},{36,32},... | collective-permute-start | bytes 98312 | tf_op jit(solution)/shard_map/ppermute | solution.py:460
  29.0 7.2 %collective-permute-start.7 = (bf16[32,512]{1,0:T(8,128)(2,1)S(1)}, bf16[32,512]{1,0:T(8,128)(2,1)S(1)}, u32[]{:S(2)}, u32[]{:S(2)}) collective-permute-start(bf16[32,512]{1,0:T(8,128)(2,1)S(1)} %get-tuple-element.91), channel_id=1, source_target_pairs={{120,0},{12,4},{0,8},{20,12},{8,16},{28,20},{16,24},{36,28},{24,32... | collective-permute-start | bytes 98312 | tf_op jit(solution)/shard_map/ppermute | solution.py:460
  29.0 7.2 %collective-permute-start.9 = (bf16[32,512]{1,0:T(8,128)(2,1)S(1)}, bf16[32,512]{1,0:T(8,128)(2,1)S(1)}, u32[]{:S(2)}, u32[]{:S(2)}) collective-permute-start(bf16[32,512]{1,0:T(8,128)(2,1)S(1)} %get-tuple-element.92), channel_id=1, source_target_pairs={{64,0},{68,4},{72,8},{76,12},{80,16},{84,20},{88,24},{92,28},{96,3... | collective-permute-start | bytes 98312 | tf_op jit(solution)/shard_map/ppermute | solution.py:460
  45.7 24.5 %collective-permute-start.19 = (bf16[17,112,512]{2,1,0:T(8,128)(2,1)S(1)}, bf16[17,112,512]{2,1,0:T(8,128)(2,1)S(1)}, u32[]{:S(2)}, u32[]{:S(2)}) collective-permute-start(bf16[17,112,512]{2,1,0:T(8,128)(2,1)S(1)} %get-tuple-element.111), channel_id=1, source_target_pairs={{0,4},{4,0},{8,12},{12,8},{16,20},{20,16},{24,28},{28,24},{32,36},... | collective-permute-start | bytes 5849096 | tf_op jit(solution)/shard_map/ppermute | solution.py:504
  46.9 3.7 %collective-permute-start.10 = (bf16[64,512]{1,0:T(8,128)(2,1)S(1)}, bf16[64,512]{1,0:T(8,128)(2,1)S(1)}, u32[]{:S(2)}, u32[]{:S(2)}) collective-permute-start(bf16[64,512]{1,0:T(8,128)(2,1)S(1)} %get-tuple-element.95), channel_id=1, source_target_pairs={{4,0},{0,4},{12,8},{8,12},{20,16},{16,20},{28,24},{24,28},{36,32},... | collective-permute-start | bytes 196616 | tf_op jit(solution)/shard_map/ppermute | solution.py:460
  50.6 8.5 %collective-permute-start.11 = (bf16[64,512]{1,0:T(8,128)(2,1)S(1)}, bf16[64,512]{1,0:T(8,128)(2,1)S(1)}, u32[]{:S(2)}, u32[]{:S(2)}) collective-permute-start(bf16[64,512]{1,0:T(8,128)(2,1)S(1)} %pad_maximum_fusion), channel_id=1, source_target_pairs={{124,0},{8,4},{4,8},{16,12},{12,16},{24,20},{20,24},{32,28},{28,32... | collective-permute-start | bytes 196616 | tf_op jit(solution)/shard_map/ppermute | solution.py:460
  53.4 3.9 %collective-permute-start.12 = (bf16[32,512]{1,0:T(8,128)(2,1)S(1)}, bf16[32,512]{1,0:T(8,128)(2,1)S(1)}, u32[]{:S(2)}, u32[]{:S(2)}) collective-permute-start(bf16[32,512]{1,0:T(8,128)(2,1)S(1)} %get-tuple-element.97), channel_id=1, source_target_pairs={{8,0},{124,4},{16,8},{4,12},{24,16},{12,20},{32,24},{20,28},{40,32... | collective-permute-start | bytes 98312 | tf_op jit(solution)/shard_map/ppermute | solution.py:460
  53.7 5.4 %collective-permute-start.13 = (bf16[32,512]{1,0:T(8,128)(2,1)S(1)}, bf16[32,512]{1,0:T(8,128)(2,1)S(1)}, u32[]{:S(2)}, u32[]{:S(2)}) collective-permute-start(bf16[32,512]{1,0:T(8,128)(2,1)S(1)} %get-tuple-element.98), channel_id=1, source_target_pairs={{64,0},{68,4},{72,8},{76,12},{80,16},{84,20},{88,24},{92,28},{96,3... | collective-permute-start | bytes 98312 | tf_op jit(solution)/shard_map/ppermute | solution.py:460
  68.9 1.3 copy-start
  70.2 9.0 %collective-permute-start.18 = (bf16[17,112,512]{2,1,0:T(8,128)(2,1)}, bf16[17,112,512]{2,1,0:T(8,128)(2,1)}, u32[]{:S(2)}, u32[]{:S(2)}) collective-permute-start(bf16[17,112,512]{2,1,0:T(8,128)(2,1)} %get-tuple-element.109), channel_id=1, source_target_pairs={{0,4},{4,0},{8,12},{12,8},{16,20},{20,16},{24,28},{28,24},{32,36},... | collective-permute-start | bytes 5849096 | tf_op jit(solution)/shard_map/ppermute | solution.py:504
  71.7 36.4 %all-to-all-start.1 = ((bf16[64,120,128]{2,1,0:T(8,128)(2,1)}), bf16[64,120,128]{2,1,0:T(8,128)(2,1)S(1)}, u32[]{:S(2)}, u32[]{:S(2)}) async-start(bf16[64,120,128]{2,1,0:T(8,128)(2,1)} %shard_map.196), calls=%async_computation.1 | async-start | bytes 3932160 | tf_op jit(solution)/shard_map/all_to_all | solution.py:508
  79.2 1.5 %copy-start.1 = (bf16[17,112,512]{2,1,0:T(8,128)(2,1)S(1)}, bf16[17,112,512]{2,1,0:T(8,128)(2,1)}, u32[]{:S(2)}) copy-start(bf16[17,112,512]{2,1,0:T(8,128)(2,1)} %copy-done) | copy-start | bytes 5849092
  108.1 34.6 %all-to-all-start = ((bf16[64,120,128]{2,1,0:T(8,128)(2,1)}), bf16[64,120,128]{2,1,0:T(8,128)(2,1)}, u32[]{:S(2)}, u32[]{:S(2)}) async-start(bf16[64,120,128]{2,1,0:T(8,128)(2,1)} %shard_map.195), calls=%async_computation | async-start | bytes 3932160 | tf_op jit(solution)/shard_map/all_to_all | solution.py:508
  114.4 1.3 collective-permute-start.14
  115.7 23.8 %collective-permute-start.15 = (bf16[64,512]{1,0:T(8,128)(2,1)S(1)}, bf16[64,512]{1,0:T(8,128)(2,1)S(1)}, u32[]{:S(2)}, u32[]{:S(2)}) collective-permute-start(bf16[64,512]{1,0:T(8,128)(2,1)S(1)} %pad_maximum_fusion.1), channel_id=1, source_target_pairs={{124,0},{8,4},{4,8},{16,12},{12,16},{24,20},{20,24},{32,28},{28,32... | collective-permute-start | bytes 196616 | tf_op jit(solution)/shard_map/ppermute | solution.py:460
  120.7 16.3 %collective-permute-start.16 = (bf16[32,512]{1,0:T(8,128)(2,1)S(1)}, bf16[32,512]{1,0:T(8,128)(2,1)S(1)}, u32[]{:S(2)}, u32[]{:S(2)}) collective-permute-start(bf16[32,512]{1,0:T(8,128)(2,1)S(1)} %get-tuple-element.106), channel_id=1, source_target_pairs={{8,0},{124,4},{16,8},{4,12},{24,16},{12,20},{32,24},{20,28},{40,32... | collective-permute-start | bytes 98312 | tf_op jit(solution)/shard_map/ppermute | solution.py:460
  121.5 18.0 %collective-permute-start.17 = (bf16[32,512]{1,0:T(8,128)(2,1)S(1)}, bf16[32,512]{1,0:T(8,128)(2,1)S(1)}, u32[]{:S(2)}, u32[]{:S(2)}) collective-permute-start(bf16[32,512]{1,0:T(8,128)(2,1)S(1)} %get-tuple-element.107), channel_id=1, source_target_pairs={{64,0},{68,4},{72,8},{76,12},{80,16},{84,20},{88,24},{92,28},{96,3... | collective-permute-start | bytes 98312 | tf_op jit(solution)/shard_map/ppermute | solution.py:460
